TPU v7x, 256 devices: a whole 4x4x8 slice. The times are simulated.
256 devices in a mesh: gx: 8 (over x, core), gy: 4 (over y), gz: 8 (over z).
Axes of the slice: x: 4, y: 4, z: 8, core: 2. Of those that a mesh axis runs over, the one named last changes fastest.
Arguments:
- velocity: float32 [3, 128, 128, 1024], P(None, 'gx', 'gy', 'gz'), may hold values from -6 to 6
- forcing: float32 [3, 128, 128, 1024], P(None, 'gx', 'gy', 'gz'), may hold values from -12 to 12
- phase_block: int32 [32, 32, 256], P('gx', 'gy', 'gz'), may hold values from 0 to 7
- prefactor: float32 [8], replicated, may hold values from 0.5 to 4
- yield_stress: float32 [8], replicated, may hold values from 1 to 16
Outputs:
- smoothed: float32 [3, 128, 128, 1024], P(None, 'gx', 'gy', 'gz')
- viscosity_field: float32 [128, 128, 1024], P('gx', 'gy', 'gz')
- coarse_one: float32 [64, 64, 512], P('gx', 'gy', 'gz')
- coarse_two: float32 [32, 32, 256], P('gx', 'gy', 'gz')
- coarse_three: float32 [16, 16, 128], P('gx', 'gy', 'gz')
- residual_field: float32 [3, 128, 128, 1024], P(None, 'gx', 'gy', 'gz')
- residual_rms: float32 [], replicated
All inputs are finite; a program needn't handle non-finite values.
Results may differ from a plain program's by a relative error of at most 0.000053.
Values sent between devices are 32-bit elements; how exact they have to be, the bound alone decides.
No kernel may reach another device: no remote copies, remote signals or barrier semaphores. Data moves between devices by JAX's collectives and lax.ppermute only.
A program may use at most 64 MiB of HBM per device.

v0:
```python
import functools

import jax
import jax.numpy as jnp
from jax import lax
from jax.sharding import Mesh
from jax.sharding import PartitionSpec as P

BLOCK = 4
GX = ("gx_0", "gx_1")
GX_GY_GZ = ("gx_0", "gx_1", "gy", "gz")


RELAXATION = 0.8
NEIGHBOUR_OFFSETS = ((1, 0, 0), (-1, 0, 0), (0, 1, 0), (0, -1, 0), (0, 0, 1), (0, 0, -1))
UNIT_STEPS = ((1, 0, 0), (0, 1, 0), (0, 0, 1))


def padded_2(shard, sides, width):
    edges = {}
    for axis, dim in sides:
        peers, length = (lax.axis_size(axis), shard.shape[dim])
        up = [(i, (i + 1) % peers) for i in range(peers - 1)]
        last = lax.slice_in_dim(shard, length - width, length, axis=dim)
        initial = lax.slice_in_dim(shard, 0, width, axis=dim)
        edges[dim] = (
            lax.ppermute(last, axis, up),
            lax.ppermute(initial, axis, [(b, a) for a, b in up]),
        )
    done = []
    for _, dim in sides:
        low, high = edges[dim]
        around = [(width, width) if d in done else (0, 0) for d in range(shard.ndim)]
        shard = jnp.concatenate([jnp.pad(low, around), shard, jnp.pad(high, around)], axis=dim)
        done.append(dim)
    return shard


def by_axis(shard, axes):
    return functools.reduce(lax.psum, axes, shard)


def padded_3(block, sides, width):
    for axis, dim in sides:
        count = lax.axis_size(axis)
        forward = [(i, i + 1) for i in range(count - 1)]
        backward = [(target, source) for source, target in forward]
        low = lax.ppermute(
            lax.slice_in_dim(block, block.shape[dim] - width, None, axis=dim), axis, forward
        )
        high = lax.ppermute(lax.slice_in_dim(block, 0, width, axis=dim), axis, backward)
        block = jnp.concatenate([low, block, high], axis=dim)
    return block


def offset_view(field, shift_x, shift_y, shift_z):
    size_x = field.shape[-3] - 2
    size_y = field.shape[-2] - 2
    size_z = field.shape[-1] - 2
    return field[
        ...,
        1 + shift_x : 1 + shift_x + size_x,
        1 + shift_y : 1 + shift_y + size_y,
        1 + shift_z : 1 + shift_z + size_z,
    ]


def viscosity_of(padded_vel, prefactor_cells, yield_cells):
    gradient = []
    for comp_a in range(3):
        row_list = []
        for comp_b in range(3):
            step_up = UNIT_STEPS[comp_b]
            step_down = (-step_up[0], -step_up[1], -step_up[2])
            row_list.append(
                0.5
                * (
                    offset_view(padded_vel[comp_a], *step_up)
                    - offset_view(padded_vel[comp_a], *step_down)
                )
            )
        gradient.append(row_list)
    strain_sq = jnp.zeros(gradient[0][0].shape, jnp.float32)
    for comp_a in range(3):
        for comp_b in range(3):
            strain = 0.5 * (gradient[comp_a][comp_b] + gradient[comp_b][comp_a])
            strain_sq = strain_sq + strain * strain
    invariant = 0.5 * strain_sq + 1.0
    creeping = prefactor_cells * jnp.power(invariant, -1.0 / 3.0)
    plastic = yield_cells / (2.0 * jnp.sqrt(invariant))
    return jnp.minimum(creeping, plastic)


def restrict_dim(field, dim_index):
    coarse_len = (field.shape[dim_index] - 2) // 2

    def every_other(start):
        return lax.slice_in_dim(field, start, start + 2 * coarse_len - 1, 2, dim_index)

    return (every_other(0) + 3.0 * every_other(1) + 3.0 * every_other(2) + every_other(3)) * 0.125


def coarsen(padded):
    return restrict_dim(restrict_dim(restrict_dim(padded, 0), 1), 2)


def smooth_terms(padded_vel, padded_visc):
    centre = offset_view(padded_visc, 0, 0, 0)
    diagonal = jnp.zeros(centre.shape, jnp.float32)
    neighbours = jnp.zeros((3,) + centre.shape, jnp.float32)
    for offset in NEIGHBOUR_OFFSETS:
        face_visc = 0.5 * (centre + offset_view(padded_visc, *offset))
        diagonal = diagonal + face_visc
        neighbours = neighbours + face_visc[None] * offset_view(padded_vel, *offset)
    return (diagonal, neighbours)


def jacobi_sweep(padded_vel, padded_visc, forcing):
    diagonal, neighbours = smooth_terms(padded_vel, padded_visc)
    centre_vel = offset_view(padded_vel, 0, 0, 0)
    return (
        centre_vel
        + RELAXATION * (forcing - (diagonal[None] * centre_vel - neighbours)) / diagonal[None]
    )


def misfit(padded_vel, padded_visc, forcing):
    diagonal, neighbours = smooth_terms(padded_vel, padded_visc)
    centre_vel = offset_view(padded_vel, 0, 0, 0)
    return forcing - (diagonal[None] * centre_vel - neighbours)


def expand_table(phase_block, table):
    block_table = jnp.zeros(phase_block.shape, jnp.float32)
    for phase_id in range(table.shape[0]):
        block_table = block_table + jnp.where(phase_block == phase_id, table[phase_id], 0.0)
    blocks_x, blocks_y, blocks_z = phase_block.shape
    spread = jnp.broadcast_to(
        block_table[:, None, :, None, :, None], (blocks_x, BLOCK, blocks_y, BLOCK, blocks_z, BLOCK)
    )
    return spread.reshape(blocks_x * BLOCK, blocks_y * BLOCK, blocks_z * BLOCK)


def inside_box(box_shape, rim_width, block_cells):
    along_x = lax.iota(jnp.int32, box_shape[0]) + lax.axis_index(GX) * block_cells[0] - rim_width
    along_y = lax.iota(jnp.int32, box_shape[1]) + lax.axis_index("gy") * block_cells[1] - rim_width
    along_z = lax.iota(jnp.int32, box_shape[2]) + lax.axis_index("gz") * block_cells[2] - rim_width
    inside_x = (along_x >= 0) & (along_x < block_cells[0] * lax.axis_size(GX))
    inside_y = (along_y >= 0) & (along_y < block_cells[1] * lax.axis_size("gy"))
    inside_z = (along_z >= 0) & (along_z < block_cells[2] * lax.axis_size("gz"))
    return inside_x[:, None, None] & inside_y[None, :, None] & inside_z[None, None, :]


def sweep_halo(field):
    return padded_2(field, ((GX, 1), ("gy", 2), ("gz", 3)), 1)


def per_device(velocity, forcing, phase_block, prefactor, yield_stress):
    cells_x, cells_y, cells_z = (velocity.shape[1], velocity.shape[2], velocity.shape[3])
    block_cells = (cells_x, cells_y, cells_z)
    prefactor_cells = expand_table(phase_block, prefactor)
    yield_cells = expand_table(phase_block, yield_stress)
    padded_vel = sweep_halo(velocity)
    viscosity_field = viscosity_of(padded_vel, prefactor_cells, yield_cells)
    padded_visc = padded_2(viscosity_field, ((GX, 0), ("gy", 1), ("gz", 2)), 1)
    current = jacobi_sweep(padded_vel, padded_visc, forcing)
    current = jacobi_sweep(sweep_halo(current), padded_visc, forcing)
    padded_final = padded_2(current, ((GX, 1), ("gy", 2), ("gz", 3)), 1)
    misfit_field = misfit(padded_final, padded_visc, forcing)
    sum_squares = by_axis(jnp.sum(misfit_field * misfit_field), GX_GY_GZ)
    all_cells = float(
        3
        * cells_x
        * lax.axis_size(GX)
        * cells_y
        * lax.axis_size("gy")
        * cells_z
        * lax.axis_size("gz")
    )
    residual_rms = jnp.sqrt(sum_squares / all_cells)
    levels = []
    level_field = padded_3(viscosity_field, ((GX, 0), ("gy", 1), ("gz", 2)), 7)
    rim_width = 7
    level_cells = block_cells
    for level in range(3):
        level_field = coarsen(level_field)
        rim_width = (rim_width - 1) // 2
        level_cells = (level_cells[0] // 2, level_cells[1] // 2, level_cells[2] // 2)
        level_field = jnp.where(
            inside_box(level_field.shape, rim_width, level_cells), level_field, 0.0
        )
        levels.append(
            level_field[
                rim_width : level_field.shape[0] - rim_width,
                rim_width : level_field.shape[1] - rim_width,
                rim_width : level_field.shape[2] - rim_width,
            ]
        )
    return (current, viscosity_field, levels[0], levels[1], levels[2], misfit_field, residual_rms)


def solution(mesh):
    split = Mesh(
        mesh.devices.reshape(4, 2, mesh.shape["gy"], mesh.shape["gz"]), ("gx_0", "gx_1", "gy", "gz")
    )
    return jax.shard_map(
        per_device,
        mesh=split,
        in_specs=(P(None, GX, "gy", "gz"), P(None, GX, "gy", "gz"), P(GX, "gy", "gz"), P(), P()),
        out_specs=(
            P(None, GX, "gy", "gz"),
            P(GX, "gy", "gz"),
            P(GX, "gy", "gz"),
            P(GX, "gy", "gz"),
            P(GX, "gy", "gz"),
            P(None, GX, "gy", "gz"),
            P(),
        ),
        check_vma=False,
    )
```

profile of v0, /device:TPU:24, one launch (start us, length us, event | category | flops | bytes accessed | tf_op | source)
XLA Modules:
  0.0 231.4 jit_solution(3585826509020688203)
XLA Ops:
  0.6 1.5 fusion.106
  2.1 2.3 %collective-permute-start.2 = (f32[3,1,32,128]{3,2,1,0:T(8,128)}, f32[3,1,32,128]{3,2,1,0:T(8,128)}, u32[]{:S(2)}, u32[]{:S(2)}) collective-permute-start(f32[3,1,32,128]{3,2,1,0:T(8,128)} %get-tuple-element.45), channel_id=1, source_target_pairs={{0,32},{32,64},{64,96},{96,128},{128,160},{160,192},{192,224},{1,3... | collective-permute-start | bytes 147464 | tf_op jit(solution)/shard_map/ppermute | solution.py:27
  4.4 1.7 fusion.104
  6.5 3.8 %collective-permute-start = (f32[3,16,32,1]{2,1,3,0:T(8,128)S(1)}, f32[3,16,32,1]{2,1,3,0:T(8,128)S(1)}, u32[]{:S(2)}, u32[]{:S(2)}) collective-permute-start(f32[3,16,32,1]{2,1,3,0:T(8,128)S(1)} %copy.28), channel_id=1, source_target_pairs={{0,1},{1,2},{2,3},{3,4},{4,5},{5,6},{6,7},{8,9},{9,10},{10,11},{11... | collective-permute-start | bytes 18440 | tf_op jit(solution)/shard_map/ppermute | solution.py:27
  10.7 1.3 collective-permute-start.5
  12.0 1.3 collective-permute-start.1
  13.3 4.5 %collective-permute-start.4 = (f32[3,16,1,128]{3,2,1,0:T(1,128)S(1)}, f32[3,16,1,128]{3,2,1,0:T(1,128)S(1)}, u32[]{:S(2)}, u32[]{:S(2)}) collective-permute-start(f32[3,16,1,128]{3,2,1,0:T(1,128)S(1)} %get-tuple-element.43), channel_id=1, source_target_pairs={{8,0},{16,8},{24,16},{9,1},{17,9},{25,17},{10,2},{18,10},{26,18},{... | collective-permute-start | bytes 73736 | tf_op jit(solution)/shard_map/ppermute | solution.py:28
  21.2 5.0 %select_add_fusion.1 = (f32[4,8,32]{2,1,0:T(8,128)S(1)}, pred[4,8,32]{2,1,0:T(8,128)(4,1)S(1)}, pred[4,8,32]{2,1,0:T(8,128)(4,1)S(1)}, pred[4,8,32]{2,1,0:T(8,12...) fusion(f32[]{:T(128)} %bitcast.7, f32[]{:T(128)} %bitcast.6, ...), kind=kLoop, calls=%fused_computation.188 | loop fusion | flops 23552 | bytes 16416 | tf_op jit(solution)/shard_map/add | solution.py:136
  26.2 5.0 %select_add_fusion = f32[4,8,32]{2,1,0:T(8,128)S(1)} fusion(pred[4,8,32]{2,1,0:T(8,128)(4,1)S(1)} %get-tuple-element.24, pred[4,8,32]{2,1,0:T(8,128)(4,1)S(1)} %get-tuple-element.23, pred[4,8,32]{2,1,0:T(8,128)(4,1)S(1)} %get-tuple-element.22, pred[4,8,32]{2,1,0:T(8,128)(4,1)S(1)} %get-tuple-element.21, pred[4,8,32]{2,1,0:T(8,128)(4,1)S(1)} %get-tuple-element.20, ...), kind=kLoop, calls=%fused_computation.187 | loop fusion | flops 15360 | bytes 12320 | tf_op jit(solution)/shard_map/add | solution.py:136
  31.8 4.4 %broadcast_in_dim.142 = f32[4,4,8,4,32,4]{5,4,3,2,1,0:T(8,128)} broadcast(f32[4,8,32]{2,1,0:T(8,128)S(1)} %select_add_fusion), dimensions={0,2,4} | broadcast | bytes 266240 | tf_op jit(solution)/shard_map/broadcast_in_dim | solution.py:138
  36.2 8.2 %reshape.195 = f32[16,32,128]{2,1,0:T(8,128)S(1)} reshape(f32[4,4,8,4,32,4]{5,4,3,2,1,0:T(8,128)} %broadcast_in_dim.142) | data formatting | bytes 524288 | tf_op jit(solution)/shard_map/reshape | solution.py:141
  44.4 4.4 %broadcast_in_dim.133 = f32[4,4,8,4,32,4]{5,4,3,2,1,0:T(8,128)} broadcast(f32[4,8,32]{2,1,0:T(8,128)S(1)} %get-tuple-element.16), dimensions={0,2,4} | broadcast | bytes 266240 | tf_op jit(solution)/shard_map/broadcast_in_dim | solution.py:138
  48.8 8.2 %reshape.194 = f32[16,32,128]{2,1,0:T(8,128)S(1)} reshape(f32[4,4,8,4,32,4]{5,4,3,2,1,0:T(8,128)} %broadcast_in_dim.133) | data formatting | bytes 524288 | tf_op jit(solution)/shard_map/reshape | solution.py:141
  57.0 1.3 collective-permute-start.3
  59.3 0.9 constant_dynamic-update-slice_fusion.2
  60.3 1.2 pad_maximum_fusion
  61.8 1.2 divide_minimum_fusion
  63.2 2.7 %collective-permute-start.8 = (f32[16,1,128]{2,1,0:T(1,128)S(1)}, f32[16,1,128]{2,1,0:T(1,128)S(1)}, u32[]{:S(2)}, u32[]{:S(2)}) collective-permute-start(f32[16,1,128]{2,1,0:T(1,128)S(1)} %get-tuple-element.55), channel_id=1, source_target_pairs={{8,0},{16,8},{24,16},{9,1},{17,9},{25,17},{10,2},{18,10},{26,18},{... | collective-permute-start | bytes 24584 | tf_op jit(solution)/shard_map/ppermute | solution.py:28
  65.8 1.3 collective-permute-start.10
  67.1 5.2 %collective-permute-start.11 = (f32[16,32,1]{2,1,0:T(8,128)S(1)}, f32[16,32,1]{2,1,0:T(8,128)S(1)}, u32[]{:S(2)}, u32[]{:S(2)}) collective-permute-start(f32[16,32,1]{2,1,0:T(8,128)S(1)} %get-tuple-element.52), channel_id=1, source_target_pairs={{0,1},{1,2},{2,3},{3,4},{4,5},{5,6},{6,7},{8,9},{9,10},{10,11},{11... | collective-permute-start | bytes 6152 | tf_op jit(solution)/shard_map/ppermute | solution.py:27
  72.3 1.3 collective-permute-start.6
  73.6 4.5 %collective-permute-start.7 = (f32[1,32,128]{2,1,0:T(8,128)S(1)}, f32[1,32,128]{2,1,0:T(8,128)S(1)}, u32[]{:S(2)}, u32[]{:S(2)}) collective-permute-start(f32[1,32,128]{2,1,0:T(8,128)S(1)} %get-tuple-element.56), channel_id=1, source_target_pairs={{0,32},{32,64},{64,96},{96,128},{128,160},{160,192},{192,224},{1,3... | collective-permute-start | bytes 49160 | tf_op jit(solution)/shard_map/ppermute | solution.py:27
  78.1 1.5 collective-permute-start.9
  80.2 3.4 %collective-permute-done.9 = f32[16,1,128]{2,1,0:T(1,128)S(1)} collective-permute-done((f32[16,1,128]{2,1,0:T(1,128)S(1)}, f32[16,1,128]{2,1,0:T(1,128)S(1)}, u32[]{:S(2)}, u32[]{:S(2)}) %collective-permute-start.9) | collective-permute-done | bytes 8224 | tf_op jit(solution)/shard_map/ppermute | solution.py:27
  84.1 4.0 %fusion.39 = f32[3,16,32,128]{3,2,1,0:T(8,128)S(1)} fusion(f32[3,16,32,128]{3,2,1,0:T(8,128)S(1)} %copy-done.2, f32[3,16,32,128]{3,2,1,0:T(8,128)} %param.6, f32[3,18,34,1]{3,2,1,0:T(8,128)S(1)} %pad.52, f32[3,18,1,128]{3,2,1,0:T(1,128)S(1)} %pad.54, f32[3,18,32,128]{3,2,1,0:T(8,128)} %copy-done.14, f32[3,18,1,128]{3,2,1,0:T(1,128)S(1)} %pad.53, ...), kind=kLoop, calls=%fused_computation.80 | loop fusion | flops 5308416 | bytes 5247328 | tf_op jit(solution)/shard_map/add | solution.py:122
  89.5 1.4 collective-permute-start.16
  91.9 4.5 %collective-permute-start.17 = (f32[3,16,32,1]{2,1,3,0:T(8,128)S(1)}, f32[3,16,32,1]{2,1,3,0:T(8,128)S(1)}, u32[]{:S(2)}, u32[]{:S(2)}) collective-permute-start(f32[3,16,32,1]{2,1,3,0:T(8,128)S(1)} %copy.18), channel_id=1, source_target_pairs={{0,1},{1,2},{2,3},{3,4},{4,5},{5,6},{6,7},{8,9},{9,10},{10,11},{11... | collective-permute-start | bytes 18440 | tf_op jit(solution)/shard_map/ppermute | solution.py:27
  96.4 1.3 collective-permute-start.12
  97.7 3.7 %collective-permute-start.13 = (f32[3,1,32,128]{3,2,1,0:T(8,128)}, f32[3,1,32,128]{3,2,1,0:T(8,128)}, u32[]{:S(2)}, u32[]{:S(2)}) collective-permute-start(f32[3,1,32,128]{3,2,1,0:T(8,128)} %get-tuple-element.36), channel_id=1, source_target_pairs={{0,32},{32,64},{64,96},{96,128},{128,160},{160,192},{192,224},{1,3... | collective-permute-start | bytes 147464 | tf_op jit(solution)/shard_map/ppermute | solution.py:27
  101.4 2.3 %collective-permute-start.14 = (f32[3,16,1,128]{3,2,1,0:T(1,128)}, f32[3,16,1,128]{3,2,1,0:T(1,128)S(1)}, u32[]{:S(2)}, u32[]{:S(2)}) collective-permute-start(f32[3,16,1,128]{3,2,1,0:T(1,128)} %get-tuple-element.39), channel_id=1, source_target_pairs={{8,0},{16,8},{24,16},{9,1},{17,9},{25,17},{10,2},{18,10},{26,18},{... | collective-permute-start | bytes 73736 | tf_op jit(solution)/shard_map/ppermute | solution.py:28
  103.8 1.3 collective-permute-start.15
  105.1 1.2 copy.17
  106.3 1.2 copy.19
  107.6 2.1 collective-permute-done.15
  109.8 3.2 %fusion.22 = f32[3,16,32,128]{3,2,1,0:T(8,128)S(1)} fusion(f32[3,16,32,128]{3,2,1,0:T(8,128)S(1)} %fusion.39, f32[3,16,32,128]{3,2,1,0:T(8,128)S(1)} %copy-done.4, f32[3,16,32,1]{3,2,1,0:T(8,128)} %copy.19, f32[3,18,1,128]{3,2,1,0:T(1,128)S(1)} %pad.60, f32[3,18,1,128]{3,2,1,0:T(1,128)S(1)} %pad.61, f32[3,1,32,128]{3,2,1,0:T(8,128)S(1)} %collective-permute-done.12, ...), kind=kLoop, calls=%fused_computation.43 | loop fusion | flops 8060928 | bytes 4360192 | tf_op jit(solution)/shard_map/add | solution.py:122
  113.0 1.2 fusion.98
  114.8 1.0 copy.24
  115.8 1.3 collective-permute-start.28
  117.7 1.5 copy.26
  119.2 5.6 %collective-permute-start.29 = (f32[3,16,32,1]{2,1,3,0:T(8,128)S(1)}, f32[3,16,32,1]{2,1,3,0:T(8,128)S(1)}, u32[]{:S(2)}, u32[]{:S(2)}) collective-permute-start(f32[3,16,32,1]{2,1,3,0:T(8,128)S(1)} %copy.26), channel_id=1, source_target_pairs={{0,1},{1,2},{2,3},{3,4},{4,5},{5,6},{6,7},{8,9},{9,10},{10,11},{11... | collective-permute-start | bytes 18440 | tf_op jit(solution)/shard_map/ppermute | solution.py:27
  124.8 1.3 collective-permute-start.24
  126.1 3.6 %collective-permute-start.25 = (f32[3,1,32,128]{3,2,1,0:T(8,128)}, f32[3,1,32,128]{3,2,1,0:T(8,128)}, u32[]{:S(2)}, u32[]{:S(2)}) collective-permute-start(f32[3,1,32,128]{3,2,1,0:T(8,128)} %get-tuple-element.32), channel_id=1, source_target_pairs={{0,32},{32,64},{64,96},{96,128},{128,160},{160,192},{192,224},{1,3... | collective-permute-start | bytes 147464 | tf_op jit(solution)/shard_map/ppermute | solution.py:27
  129.7 3.1 %collective-permute-start.26 = (f32[3,16,1,128]{3,2,1,0:T(1,128)}, f32[3,16,1,128]{3,2,1,0:T(1,128)}, u32[]{:S(2)}, u32[]{:S(2)}) collective-permute-start(f32[3,16,1,128]{3,2,1,0:T(1,128)} %get-tuple-element.31), channel_id=1, source_target_pairs={{8,0},{16,8},{24,16},{9,1},{17,9},{25,17},{10,2},{18,10},{26,18},{... | collective-permute-start | bytes 73736 | tf_op jit(solution)/shard_map/ppermute | solution.py:28
  132.8 1.3 collective-permute-start.27
  134.8 1.3 copy.25
  136.1 3.0 %collective-permute-start.18 = (f32[7,32,128]{2,1,0:T(8,128)}, f32[7,32,128]{2,1,0:T(8,128)}, u32[]{:S(2)}, u32[]{:S(2)}) collective-permute-start(f32[7,32,128]{2,1,0:T(8,128)} %get-tuple-element.50), channel_id=1, source_target_pairs={{0,32},{32,64},{64,96},{96,128},{128,160},{160,192},{192,224},{1,3... | collective-permute-start | bytes 344072 | tf_op jit(solution)/shard_map/ppermute | solution.py:48
  139.1 1.2 copy.27
  140.3 1.3 collective-permute-start.19
  143.2 4.4 %multiply_reduce_fusion = (f32[]{:T(128)}, f32[3,16,32,128]{3,2,1,0:T(8,128)}) fusion(f32[3,16,32,128]{3,2,1,0:T(8,128)S(1)} %copy-done.4, f32[3,18,1,128]{3,2,1,0:T(1,128)S(1)} %pad.64, f32[3,1,32,128]{3,2,1,0:T(8,128)S(1)} %collective-permute-done.24, f32[3,16,32,128]{3,2,1,0:T(8,128)S(1)} %fusion.22, f32[3,1,32,128]{3,2,1,0:T(8,128)} %collective-permute-done.25, ...), kind=kLoop, calls=%fused_computation.99 | loop fusion | flops 7864319 | bytes 4360196 | tf_op jit(solution)/shard_map/reduce_sum | solution.py:170
  147.6 11.5 %psum.28 = f32[]{:T(128)} all-reduce(f32[]{:T(128)} %get-tuple-element.7), channel_id=1, replica_groups=mesh['gx_0'=4,'gx_1'=2,'gy'=4,'gz'=8] {'gx_0'}, use_global_device_ids=true, to_apply=%region_1.2 | all-reduce | flops 1 | bytes 8 | tf_op jit(solution)/shard_map/psum | solution.py:40
  159.1 0.8 pad_maximum_fusion.63
  159.9 1.3 collective-permute-start.20
  161.2 5.2 %collective-permute-start.21 = (f32[30,7,128]{2,1,0:T(8,128)S(1)}, f32[30,7,128]{2,1,0:T(8,128)S(1)}, u32[]{:S(2)}, u32[]{:S(2)}) collective-permute-start(f32[30,7,128]{2,1,0:T(8,128)S(1)} %get-tuple-element.49), channel_id=1, source_target_pairs={{8,0},{16,8},{24,16},{9,1},{17,9},{25,17},{10,2},{18,10},{26,18},{... | collective-permute-start | bytes 322568 | tf_op jit(solution)/shard_map/ppermute | solution.py:51
  166.4 3.1 %psum.29 = f32[]{:T(128)} all-reduce(f32[]{:T(128)} %psum.28), channel_id=1, replica_groups=mesh['gx_0'=4,'gx_1'=2,'gy'=4,'gz'=8] {'gx_1'}, use_global_device_ids=true, to_apply=%region_2.3 | all-reduce | flops 1 | bytes 8 | tf_op jit(solution)/shard_map/psum | solution.py:40
  169.5 9.1 %psum.30 = f32[]{:T(128)} all-reduce(f32[]{:T(128)} %psum.29), channel_id=1, replica_groups=mesh['gx_0'=4,'gx_1'=2,'gy'=4,'gz'=8] {'gy'}, use_global_device_ids=true, to_apply=%region_3.4 | all-reduce | flops 1 | bytes 8 | tf_op jit(solution)/shard_map/psum | solution.py:40
  178.7 1.0 pad_maximum_fusion.44
  180.3 4.9 %collective-permute-start.22 = (f32[30,46,7]{1,0,2:T(8,128)S(1)}, f32[30,46,7]{1,0,2:T(8,128)S(1)}, u32[]{:S(2)}, u32[]{:S(2)}) collective-permute-start(f32[30,46,7]{1,0,2:T(8,128)S(1)} %copy.20), channel_id=1, source_target_pairs={{0,1},{1,2},{2,3},{3,4},{4,5},{5,6},{6,7},{8,9},{9,10},{10,11},{11... | collective-permute-start | bytes 115928 | tf_op jit(solution)/shard_map/ppermute | solution.py:48
  185.5 1.3 collective-permute-start.23
  186.9 20.7 %psum.31 = f32[]{:T(128)} all-reduce(f32[]{:T(128)} %psum.30), channel_id=1, replica_groups=mesh['gx_0'=4,'gx_1'=2,'gy'=4,'gz'=8] {'gz'}, use_global_device_ids=true, to_apply=%region_4.5 | all-reduce | flops 1 | bytes 8 | tf_op jit(solution)/shard_map/psum | solution.py:40
  209.0 1.7 pad_maximum_fusion.1
  213.1 3.1 %slice.525 = f32[14,22,70]{2,1,0:T(8,128)S(1)} slice(f32[14,22,142]{2,1,0:T(8,128)S(1)} %add_multiply_fusion.1), slice={[0:14:1], [0:22:1], [0:139:2]} | slice | bytes 172480 | tf_op jit(solution)/shard_map/slice | solution.py:98
  216.2 3.2 %slice.526 = f32[14,22,70]{2,1,0:T(8,128)S(1)} slice(f32[14,22,142]{2,1,0:T(8,128)S(1)} %add_multiply_fusion.1), slice={[0:14:1], [0:22:1], [1:140:2]} | slice | bytes 172480 | tf_op jit(solution)/shard_map/slice | solution.py:98
  219.4 3.2 %slice.527 = f32[14,22,70]{2,1,0:T(8,128)S(1)} slice(f32[14,22,142]{2,1,0:T(8,128)S(1)} %add_multiply_fusion.1), slice={[0:14:1], [0:22:1], [2:141:2]} | slice | bytes 172480 | tf_op jit(solution)/shard_map/slice | solution.py:98
  222.6 3.2 %slice.528 = f32[14,22,70]{2,1,0:T(8,128)S(1)} slice(f32[14,22,142]{2,1,0:T(8,128)S(1)} %add_multiply_fusion.1), slice={[0:14:1], [0:22:1], [3:142:2]} | slice | bytes 172480 | tf_op jit(solution)/shard_map/slice | solution.py:98
  (156 shorter events, 21.3 us)
Async XLA Ops:
  2.1 57.2 %collective-permute-start.2 = (f32[3,1,32,128]{3,2,1,0:T(8,128)}, f32[3,1,32,128]{3,2,1,0:T(8,128)}, u32[]{:S(2)}, u32[]{:S(2)}) collective-permute-start(f32[3,1,32,128]{3,2,1,0:T(8,128)} %get-tuple-element.45), channel_id=1, source_target_pairs={{0,32},{32,64},{64,96},{96,128},{128,160},{160,192},{192,224},{1,3... | collective-permute-start | bytes 147464 | tf_op jit(solution)/shard_map/ppermute | solution.py:27
  6.1 5.9 %copy-start.2 = (f32[3,16,32,128]{3,2,1,0:T(8,128)S(1)}, f32[3,16,32,128]{3,2,1,0:T(8,128)}, u32[]{:S(2)}) copy-start(f32[3,16,32,128]{3,2,1,0:T(8,128)} %param.5) | copy-start | bytes 2359300
  6.1 11.8 %copy-start.16 = (f32[8]{0:T(128)S(1)}, f32[8]{0:T(128)}, u32[]{:S(2)}) copy-start(f32[8]{0:T(128)} %param.8) | copy-start | bytes 100
  6.1 12.5 %copy-start.17 = (f32[8]{0:T(128)S(1)}, f32[8]{0:T(128)}, u32[]{:S(2)}) copy-start(f32[8]{0:T(128)} %param.9) | copy-start | bytes 100
  6.1 15.0 %copy-start.18 = (s32[4,8,32]{2,1,0:T(8,128)S(1)}, s32[4,8,32]{2,1,0:T(8,128)}, u32[]{:S(2)}) copy-start(s32[4,8,32]{2,1,0:T(8,128)} %param.7) | copy-start | bytes 12292
  6.5 50.5 %collective-permute-start = (f32[3,16,32,1]{2,1,3,0:T(8,128)S(1)}, f32[3,16,32,1]{2,1,3,0:T(8,128)S(1)}, u32[]{:S(2)}, u32[]{:S(2)}) collective-permute-start(f32[3,16,32,1]{2,1,3,0:T(8,128)S(1)} %copy.28), channel_id=1, source_target_pairs={{0,1},{1,2},{2,3},{3,4},{4,5},{5,6},{6,7},{8,9},{9,10},{10,11},{11... | collective-permute-start | bytes 18440 | tf_op jit(solution)/shard_map/ppermute | solution.py:27
  10.7 48.1 %collective-permute-start.5 = (f32[3,16,32,1]{2,1,3,0:T(8,128)S(1)}, f32[3,16,32,1]{2,1,3,0:T(8,128)S(1)}, u32[]{:S(2)}, u32[]{:S(2)}) collective-permute-start(f32[3,16,32,1]{2,1,3,0:T(8,128)S(1)} %copy.29), channel_id=1, source_target_pairs={{1,0},{2,1},{3,2},{4,3},{5,4},{6,5},{7,6},{9,8},{10,9},{11,10},{12... | collective-permute-start | bytes 18440 | tf_op jit(solution)/shard_map/ppermute | solution.py:28
  12.0 47.2 %collective-permute-start.1 = (f32[3,16,1,128]{3,2,1,0:T(1,128)S(1)}, f32[3,16,1,128]{3,2,1,0:T(1,128)S(1)}, u32[]{:S(2)}, u32[]{:S(2)}) collective-permute-start(f32[3,16,1,128]{3,2,1,0:T(1,128)S(1)} %get-tuple-element.42), channel_id=1, source_target_pairs={{0,8},{8,16},{16,24},{1,9},{9,17},{17,25},{2,10},{10,18},{18,26},{... | collective-permute-start | bytes 73736 | tf_op jit(solution)/shard_map/ppermute | solution.py:27
  13.3 46.0 %collective-permute-start.4 = (f32[3,16,1,128]{3,2,1,0:T(1,128)S(1)}, f32[3,16,1,128]{3,2,1,0:T(1,128)S(1)}, u32[]{:S(2)}, u32[]{:S(2)}) collective-permute-start(f32[3,16,1,128]{3,2,1,0:T(1,128)S(1)} %get-tuple-element.43), channel_id=1, source_target_pairs={{8,0},{16,8},{24,16},{9,1},{17,9},{25,17},{10,2},{18,10},{26,18},{... | collective-permute-start | bytes 73736 | tf_op jit(solution)/shard_map/ppermute | solution.py:28
  57.0 3.3 %collective-permute-start.3 = (f32[3,1,32,128]{3,2,1,0:T(8,128)}, f32[3,1,32,128]{3,2,1,0:T(8,128)S(1)}, u32[]{:S(2)}, u32[]{:S(2)}) collective-permute-start(f32[3,1,32,128]{3,2,1,0:T(8,128)} %get-tuple-element.44), channel_id=1, source_target_pairs={{32,0},{64,32},{96,64},{128,96},{160,128},{192,160},{224,192},{33,... | collective-permute-start | bytes 147464 | tf_op jit(solution)/shard_map/ppermute | solution.py:28
  59.2 2.3 copy-start.3
  60.3 1.2 copy-start.15
  60.3 1.2 copy-start.14
  61.8 17.9 %copy-start.22 = (pred[2]{0:T(512)(128)(4,1)S(1)}, pred[2]{0:T(512)(128)(4,1)}, u32[]{:S(2)}) copy-start(pred[2]{0:T(512)(128)(4,1)} %compare_and_fusion.2) | copy-start | bytes 10
  61.8 17.9 %copy-start.23 = (pred[4]{0:T(512)(128)(4,1)S(1)}, pred[4]{0:T(512)(128)(4,1)}, u32[]{:S(2)}) copy-start(pred[4]{0:T(512)(128)(4,1)} %compare_and_fusion.1) | copy-start | bytes 16
  63.0 146.0 %copy-start = (f32[16,32,128]{2,1,0:T(8,128)}, f32[16,32,128]{2,1,0:T(8,128)S(1)}, u32[]{:S(2)}) copy-start(f32[16,32,128]{2,1,0:T(8,128)S(1)} %divide_minimum_fusion) | copy-start | bytes 786436
  63.2 15.0 %collective-permute-start.8 = (f32[16,1,128]{2,1,0:T(1,128)S(1)}, f32[16,1,128]{2,1,0:T(1,128)S(1)}, u32[]{:S(2)}, u32[]{:S(2)}) collective-permute-start(f32[16,1,128]{2,1,0:T(1,128)S(1)} %get-tuple-element.55), channel_id=1, source_target_pairs={{8,0},{16,8},{24,16},{9,1},{17,9},{25,17},{10,2},{18,10},{26,18},{... | collective-permute-start | bytes 24584 | tf_op jit(solution)/shard_map/ppermute | solution.py:28
  65.8 17.9 %collective-permute-start.10 = (f32[16,32,1]{2,1,0:T(8,128)S(1)}, f32[16,32,1]{2,1,0:T(8,128)S(1)}, u32[]{:S(2)}, u32[]{:S(2)}) collective-permute-start(f32[16,32,1]{2,1,0:T(8,128)S(1)} %get-tuple-element.53), channel_id=1, source_target_pairs={{1,0},{2,1},{3,2},{4,3},{5,4},{6,5},{7,6},{9,8},{10,9},{11,10},{12... | collective-permute-start | bytes 6152 | tf_op jit(solution)/shard_map/ppermute | solution.py:28
  67.1 16.6 %collective-permute-start.11 = (f32[16,32,1]{2,1,0:T(8,128)S(1)}, f32[16,32,1]{2,1,0:T(8,128)S(1)}, u32[]{:S(2)}, u32[]{:S(2)}) collective-permute-start(f32[16,32,1]{2,1,0:T(8,128)S(1)} %get-tuple-element.52), channel_id=1, source_target_pairs={{0,1},{1,2},{2,3},{3,4},{4,5},{5,6},{6,7},{8,9},{9,10},{10,11},{11... | collective-permute-start | bytes 6152 | tf_op jit(solution)/shard_map/ppermute | solution.py:27
  72.3 11.4 %collective-permute-start.6 = (f32[1,32,128]{2,1,0:T(8,128)S(1)}, f32[1,32,128]{2,1,0:T(8,128)S(1)}, u32[]{:S(2)}, u32[]{:S(2)}) collective-permute-start(f32[1,32,128]{2,1,0:T(8,128)S(1)} %get-tuple-element.57), channel_id=1, source_target_pairs={{32,0},{64,32},{96,64},{128,96},{160,128},{192,160},{224,192},{33,... | collective-permute-start | bytes 49160 | tf_op jit(solution)/shard_map/ppermute | solution.py:28
  73.6 10.1 %collective-permute-start.7 = (f32[1,32,128]{2,1,0:T(8,128)S(1)}, f32[1,32,128]{2,1,0:T(8,128)S(1)}, u32[]{:S(2)}, u32[]{:S(2)}) collective-permute-start(f32[1,32,128]{2,1,0:T(8,128)S(1)} %get-tuple-element.56), channel_id=1, source_target_pairs={{0,32},{32,64},{64,96},{96,128},{128,160},{160,192},{192,224},{1,3... | collective-permute-start | bytes 49160 | tf_op jit(solution)/shard_map/ppermute | solution.py:27
  78.1 5.5 %collective-permute-start.9 = (f32[16,1,128]{2,1,0:T(1,128)S(1)}, f32[16,1,128]{2,1,0:T(1,128)S(1)}, u32[]{:S(2)}, u32[]{:S(2)}) collective-permute-start(f32[16,1,128]{2,1,0:T(1,128)S(1)} %get-tuple-element.54), channel_id=1, source_target_pairs={{0,8},{8,16},{16,24},{1,9},{9,17},{17,25},{2,10},{10,18},{18,26},{... | collective-permute-start | bytes 24584 | tf_op jit(solution)/shard_map/ppermute | solution.py:27
  84.1 4.0 %copy-start.5 = (f32[16,32,128]{2,1,0:T(8,128)}, f32[16,32,128]{2,1,0:T(8,128)S(1)}, u32[]{:S(2)}) copy-start(f32[16,32,128]{2,1,0:T(8,128)S(1)} %get-tuple-element.11) | copy-start | bytes 786436
  84.1 4.0 %copy-start.7 = (f32[16,32,128]{2,1,0:T(8,128)}, f32[16,32,128]{2,1,0:T(8,128)S(1)}, u32[]{:S(2)}) copy-start(f32[16,32,128]{2,1,0:T(8,128)S(1)} %get-tuple-element.12) | copy-start | bytes 786436
  84.1 4.0 %copy-start.9 = (f32[16,32,128]{2,1,0:T(8,128)}, f32[16,32,128]{2,1,0:T(8,128)S(1)}, u32[]{:S(2)}) copy-start(f32[16,32,128]{2,1,0:T(8,128)S(1)} %get-tuple-element.13) | copy-start | bytes 786436
  84.1 4.0 %copy-start.11 = (f32[16,32,128]{2,1,0:T(8,128)}, f32[16,32,128]{2,1,0:T(8,128)S(1)}, u32[]{:S(2)}) copy-start(f32[16,32,128]{2,1,0:T(8,128)S(1)} %get-tuple-element.14) | copy-start | bytes 786436
  84.1 4.0 %copy-start.13 = (f32[16,32,128]{2,1,0:T(8,128)}, f32[16,32,128]{2,1,0:T(8,128)S(1)}, u32[]{:S(2)}) copy-start(f32[16,32,128]{2,1,0:T(8,128)S(1)} %get-tuple-element.15) | copy-start | bytes 786436
  89.5 20.3 %copy-start.4 = (f32[3,16,32,128]{3,2,1,0:T(8,128)S(1)}, f32[3,16,32,128]{3,2,1,0:T(8,128)}, u32[]{:S(2)}) copy-start(f32[3,16,32,128]{3,2,1,0:T(8,128)} %param.6) | copy-start | bytes 2359300
  89.5 20.3 %copy-start.6 = (f32[16,32,128]{2,1,0:T(8,128)S(1)}, f32[16,32,128]{2,1,0:T(8,128)}, u32[]{:S(2)}) copy-start(f32[16,32,128]{2,1,0:T(8,128)} %copy-done.5) | copy-start | bytes 786436
  89.5 14.3 %collective-permute-start.16 = (f32[3,16,32,1]{2,1,3,0:T(8,128)S(1)}, f32[3,16,32,1]{2,1,3,0:T(8,128)S(1)}, u32[]{:S(2)}, u32[]{:S(2)}) collective-permute-start(f32[3,16,32,1]{2,1,3,0:T(8,128)S(1)} %copy.16), channel_id=1, source_target_pairs={{1,0},{2,1},{3,2},{4,3},{5,4},{6,5},{7,6},{9,8},{10,9},{11,10},{12... | collective-permute-start | bytes 18440 | tf_op jit(solution)/shard_map/ppermute | solution.py:28
  91.9 14.4 %collective-permute-start.17 = (f32[3,16,32,1]{2,1,3,0:T(8,128)S(1)}, f32[3,16,32,1]{2,1,3,0:T(8,128)S(1)}, u32[]{:S(2)}, u32[]{:S(2)}) collective-permute-start(f32[3,16,32,1]{2,1,3,0:T(8,128)S(1)} %copy.18), channel_id=1, source_target_pairs={{0,1},{1,2},{2,3},{3,4},{4,5},{5,6},{6,7},{8,9},{9,10},{10,11},{11... | collective-permute-start | bytes 18440 | tf_op jit(solution)/shard_map/ppermute | solution.py:27
  96.4 13.3 %collective-permute-start.12 = (f32[3,1,32,128]{3,2,1,0:T(8,128)}, f32[3,1,32,128]{3,2,1,0:T(8,128)S(1)}, u32[]{:S(2)}, u32[]{:S(2)}) collective-permute-start(f32[3,1,32,128]{3,2,1,0:T(8,128)} %get-tuple-element.37), channel_id=1, source_target_pairs={{32,0},{64,32},{96,64},{128,96},{160,128},{192,160},{224,192},{33,... | collective-permute-start | bytes 147464 | tf_op jit(solution)/shard_map/ppermute | solution.py:28
  97.7 12.0 %collective-permute-start.13 = (f32[3,1,32,128]{3,2,1,0:T(8,128)}, f32[3,1,32,128]{3,2,1,0:T(8,128)}, u32[]{:S(2)}, u32[]{:S(2)}) collective-permute-start(f32[3,1,32,128]{3,2,1,0:T(8,128)} %get-tuple-element.36), channel_id=1, source_target_pairs={{0,32},{32,64},{64,96},{96,128},{128,160},{160,192},{192,224},{1,3... | collective-permute-start | bytes 147464 | tf_op jit(solution)/shard_map/ppermute | solution.py:27
  101.4 6.2 %collective-permute-start.14 = (f32[3,16,1,128]{3,2,1,0:T(1,128)}, f32[3,16,1,128]{3,2,1,0:T(1,128)S(1)}, u32[]{:S(2)}, u32[]{:S(2)}) collective-permute-start(f32[3,16,1,128]{3,2,1,0:T(1,128)} %get-tuple-element.39), channel_id=1, source_target_pairs={{8,0},{16,8},{24,16},{9,1},{17,9},{25,17},{10,2},{18,10},{26,18},{... | collective-permute-start | bytes 73736 | tf_op jit(solution)/shard_map/ppermute | solution.py:28
  103.8 5.9 %collective-permute-start.15 = (f32[3,16,1,128]{3,2,1,0:T(1,128)}, f32[3,16,1,128]{3,2,1,0:T(1,128)S(1)}, u32[]{:S(2)}, u32[]{:S(2)}) collective-permute-start(f32[3,16,1,128]{3,2,1,0:T(1,128)} %get-tuple-element.38), channel_id=1, source_target_pairs={{0,8},{8,16},{16,24},{1,9},{9,17},{17,25},{2,10},{10,18},{18,26},{... | collective-permute-start | bytes 73736 | tf_op jit(solution)/shard_map/ppermute | solution.py:27
  112.9 30.2 %copy-start.1 = (f32[3,16,32,128]{3,2,1,0:T(8,128)}, f32[3,16,32,128]{3,2,1,0:T(8,128)S(1)}, u32[]{:S(2)}) copy-start(f32[3,16,32,128]{3,2,1,0:T(8,128)S(1)} %fusion.22) | copy-start | bytes 2359300
  115.8 17.1 %collective-permute-start.28 = (f32[3,16,32,1]{2,1,3,0:T(8,128)}, f32[3,16,32,1]{2,1,3,0:T(8,128)S(1)}, u32[]{:S(2)}, u32[]{:S(2)}) collective-permute-start(f32[3,16,32,1]{2,1,3,0:T(8,128)} %copy.24), channel_id=1, source_target_pairs={{1,0},{2,1},{3,2},{4,3},{5,4},{6,5},{7,6},{9,8},{10,9},{11,10},{12... | collective-permute-start | bytes 18440 | tf_op jit(solution)/shard_map/ppermute | solution.py:28
  117.7 25.5 %copy-start.8 = (f32[16,32,128]{2,1,0:T(8,128)S(1)}, f32[16,32,128]{2,1,0:T(8,128)}, u32[]{:S(2)}) copy-start(f32[16,32,128]{2,1,0:T(8,128)} %copy-done.7) | copy-start | bytes 786436
  117.7 25.5 %copy-start.10 = (f32[16,32,128]{2,1,0:T(8,128)S(1)}, f32[16,32,128]{2,1,0:T(8,128)}, u32[]{:S(2)}) copy-start(f32[16,32,128]{2,1,0:T(8,128)} %copy-done.9) | copy-start | bytes 786436
  117.7 25.5 %copy-start.12 = (f32[16,32,128]{2,1,0:T(8,128)S(1)}, f32[16,32,128]{2,1,0:T(8,128)}, u32[]{:S(2)}) copy-start(f32[16,32,128]{2,1,0:T(8,128)} %copy-done.11) | copy-start | bytes 786436
  119.2 16.8 %collective-permute-start.29 = (f32[3,16,32,1]{2,1,3,0:T(8,128)S(1)}, f32[3,16,32,1]{2,1,3,0:T(8,128)S(1)}, u32[]{:S(2)}, u32[]{:S(2)}) collective-permute-start(f32[3,16,32,1]{2,1,3,0:T(8,128)S(1)} %copy.26), channel_id=1, source_target_pairs={{0,1},{1,2},{2,3},{3,4},{4,5},{5,6},{6,7},{8,9},{9,10},{10,11},{11... | collective-permute-start | bytes 18440 | tf_op jit(solution)/shard_map/ppermute | solution.py:27
  124.8 18.4 %collective-permute-start.24 = (f32[3,1,32,128]{3,2,1,0:T(8,128)}, f32[3,1,32,128]{3,2,1,0:T(8,128)S(1)}, u32[]{:S(2)}, u32[]{:S(2)}) collective-permute-start(f32[3,1,32,128]{3,2,1,0:T(8,128)} %get-tuple-element.33), channel_id=1, source_target_pairs={{32,0},{64,32},{96,64},{128,96},{160,128},{192,160},{224,192},{33,... | collective-permute-start | bytes 147464 | tf_op jit(solution)/shard_map/ppermute | solution.py:28
  126.1 17.1 %collective-permute-start.25 = (f32[3,1,32,128]{3,2,1,0:T(8,128)}, f32[3,1,32,128]{3,2,1,0:T(8,128)}, u32[]{:S(2)}, u32[]{:S(2)}) collective-permute-start(f32[3,1,32,128]{3,2,1,0:T(8,128)} %get-tuple-element.32), channel_id=1, source_target_pairs={{0,32},{32,64},{64,96},{96,128},{128,160},{160,192},{192,224},{1,3... | collective-permute-start | bytes 147464 | tf_op jit(solution)/shard_map/ppermute | solution.py:27
  129.7 10.6 %collective-permute-start.26 = (f32[3,16,1,128]{3,2,1,0:T(1,128)}, f32[3,16,1,128]{3,2,1,0:T(1,128)}, u32[]{:S(2)}, u32[]{:S(2)}) collective-permute-start(f32[3,16,1,128]{3,2,1,0:T(1,128)} %get-tuple-element.31), channel_id=1, source_target_pairs={{8,0},{16,8},{24,16},{9,1},{17,9},{25,17},{10,2},{18,10},{26,18},{... | collective-permute-start | bytes 73736 | tf_op jit(solution)/shard_map/ppermute | solution.py:28
  132.8 9.6 %collective-permute-start.27 = (f32[3,16,1,128]{3,2,1,0:T(1,128)}, f32[3,16,1,128]{3,2,1,0:T(1,128)}, u32[]{:S(2)}, u32[]{:S(2)}) collective-permute-start(f32[3,16,1,128]{3,2,1,0:T(1,128)} %get-tuple-element.30), channel_id=1, source_target_pairs={{0,8},{8,16},{16,24},{1,9},{9,17},{17,25},{2,10},{10,18},{18,26},{... | collective-permute-start | bytes 73736 | tf_op jit(solution)/shard_map/ppermute | solution.py:27
  136.1 23.0 %collective-permute-start.18 = (f32[7,32,128]{2,1,0:T(8,128)}, f32[7,32,128]{2,1,0:T(8,128)}, u32[]{:S(2)}, u32[]{:S(2)}) collective-permute-start(f32[7,32,128]{2,1,0:T(8,128)} %get-tuple-element.50), channel_id=1, source_target_pairs={{0,32},{32,64},{64,96},{96,128},{128,160},{160,192},{192,224},{1,3... | collective-permute-start | bytes 344072 | tf_op jit(solution)/shard_map/ppermute | solution.py:48
  140.3 18.7 %collective-permute-start.19 = (f32[7,32,128]{2,1,0:T(8,128)}, f32[7,32,128]{2,1,0:T(8,128)}, u32[]{:S(2)}, u32[]{:S(2)}) collective-permute-start(f32[7,32,128]{2,1,0:T(8,128)} %get-tuple-element.51), channel_id=1, source_target_pairs={{32,0},{64,32},{96,64},{128,96},{160,128},{192,160},{224,192},{33,... | collective-permute-start | bytes 344072 | tf_op jit(solution)/shard_map/ppermute | solution.py:51
  159.9 18.8 %collective-permute-start.20 = (f32[30,7,128]{2,1,0:T(8,128)S(1)}, f32[30,7,128]{2,1,0:T(8,128)S(1)}, u32[]{:S(2)}, u32[]{:S(2)}) collective-permute-start(f32[30,7,128]{2,1,0:T(8,128)S(1)} %get-tuple-element.48), channel_id=1, source_target_pairs={{0,8},{8,16},{16,24},{1,9},{9,17},{17,25},{2,10},{10,18},{18,26},{... | collective-permute-start | bytes 322568 | tf_op jit(solution)/shard_map/ppermute | solution.py:48
  161.2 17.5 %collective-permute-start.21 = (f32[30,7,128]{2,1,0:T(8,128)S(1)}, f32[30,7,128]{2,1,0:T(8,128)S(1)}, u32[]{:S(2)}, u32[]{:S(2)}) collective-permute-start(f32[30,7,128]{2,1,0:T(8,128)S(1)} %get-tuple-element.49), channel_id=1, source_target_pairs={{8,0},{16,8},{24,16},{9,1},{17,9},{25,17},{10,2},{18,10},{26,18},{... | collective-permute-start | bytes 322568 | tf_op jit(solution)/shard_map/ppermute | solution.py:51
  180.3 27.9 %collective-permute-start.22 = (f32[30,46,7]{1,0,2:T(8,128)S(1)}, f32[30,46,7]{1,0,2:T(8,128)S(1)}, u32[]{:S(2)}, u32[]{:S(2)}) collective-permute-start(f32[30,46,7]{1,0,2:T(8,128)S(1)} %copy.20), channel_id=1, source_target_pairs={{0,1},{1,2},{2,3},{3,4},{4,5},{5,6},{6,7},{8,9},{9,10},{10,11},{11... | collective-permute-start | bytes 115928 | tf_op jit(solution)/shard_map/ppermute | solution.py:48
  185.5 23.1 %collective-permute-start.23 = (f32[30,46,7]{1,0,2:T(8,128)S(1)}, f32[30,46,7]{1,0,2:T(8,128)S(1)}, u32[]{:S(2)}, u32[]{:S(2)}) collective-permute-start(f32[30,46,7]{1,0,2:T(8,128)S(1)} %copy.21), channel_id=1, source_target_pairs={{1,0},{2,1},{3,2},{4,3},{5,4},{6,5},{7,6},{9,8},{10,9},{11,10},{12... | collective-permute-start | bytes 115928 | tf_op jit(solution)/shard_map/ppermute | solution.py:51
  213.0 12.8 %copy-start.19 = (pred[14,22]{1,0:T(8,128)(4,1)S(1)}, pred[14,22]{1,0:T(8,128)(4,1)}, u32[]{:S(2)}) copy-start(pred[14,22]{1,0:T(8,128)(4,1)} %broadcast_and_fusion) | copy-start | bytes 928
  219.4 8.1 %copy-start.20 = (pred[6,10]{1,0:T(8,128)(4,1)S(1)}, pred[6,10]{1,0:T(8,128)(4,1)}, u32[]{:S(2)}) copy-start(pred[6,10]{1,0:T(8,128)(4,1)} %broadcast_and_fusion.1) | copy-start | bytes 184
  225.8 3.8 %copy-start.21 = (pred[2,4]{1,0:T(4,128)(4,1)S(1)}, pred[2,4]{1,0:T(4,128)(4,1)}, u32[]{:S(2)}) copy-start(pred[2,4]{1,0:T(4,128)(4,1)} %broadcast_and_fusion.2) | copy-start | bytes 28
where the time goes:
time: 234 us; the launch traced here: 231 us
  starting transfers between devices  78.6 us (34%)
  local copies, waits for them, and re-layouts  67.2 us (29%)
  blocking collectives  44.4 us (19%)
  other arithmetic  32.1 us (14%)
  waiting for transfers between devices  5.66 us (2%)
  between operations  3.48 us (1%)
    psum x4, blocking collectives, by_axis(): return functools.reduce(lax.psum, axes, shard)  44.4 us
    ppermute x12, starting transfers between devices, padded_2(): lax.ppermute(last, axis, up)  38.6 us
    ppermute x12, starting transfers between devices, padded_2(): lax.ppermute(initial, axis, [(b, a) for a, b in up])  23.1 us
    slice x24, local copies, waits for them, and re-layouts, every_other(): lax.slice_in_dim(field, start, start + 2 * coarse_len - 1, 2, dim_index)  16.7 us
    reshape x2, local copies, waits for them, and re-layouts, expand_table(): return spread.reshape(blocks_x * BLOCK, blocks_y * BLOCK, blocks_z * BLOCK)  16.3 us
    add x2, other arithmetic, expand_table(): block_table + jnp.where(phase_block == phase_id, table[phase_id], 0.0)  10 us
    ppermute x3, starting transfers between devices, padded_3(): lax.ppermute(lax.slice_in_dim(block, block.shape[dim] - width, None, axis...  9.16 us
    broadcast_in_dim x2, local copies, waits for them, and re-layouts, expand_table(): jnp.broadcast_to(block_table[:, None, :, None, :, None], (blocks_x, BLOCK...  8.89 us
  transfers between devices with their start and end apart: 30, of which 3 were waited for; matrix products, arithmetic and copies ran while one was open for 26% of the time, Pallas kernels for 0%

commit v1 on v0

v1 whole, which is shorter than its diff:
```python
import functools

import jax
import jax.numpy as jnp
from jax import lax
from jax.experimental import pallas as pl
from jax.experimental.pallas import tpu as pltpu
from jax.sharding import PartitionSpec as P

F32 = jnp.float32
BLOCK = 4
AX = ("gx", "gy", "gz")
NX, NY, NZ = 16, 32, 128
VMEM = pl.BlockSpec(memory_space=pltpu.VMEM)
SMEM = pl.BlockSpec(memory_space=pltpu.SMEM)


def sds(*shape):
    return jax.ShapeDtypeStruct(shape, F32)


def position(axis):
    index = lax.axis_index(axis)
    return lax.rem(index, 2) == 0, index > 0, index < lax.axis_size(axis) - 1


def lanes(rows=8, width=128):
    return lax.broadcasted_iota(jnp.int32, (rows, width), 1)


def subs(rows=8, width=128):
    return lax.broadcasted_iota(jnp.int32, (rows, width), 0)


def roll(value, shift, axis):
    size = value.shape[axis]
    shift = shift % size
    return pltpu.roll(value, shift, axis) if shift else value


def pair_a(value, axis):
    count = lax.axis_size(axis)
    return lax.ppermute(value, axis, [(i, i ^ 1) for i in range(count)])


def pair_b(value, axis):
    count = lax.axis_size(axis)
    return lax.ppermute(
        value, axis, [(i, (i + 1) % count if i % 2 else (i - 1) % count) for i in range(count)]
    )


def params():
    return pltpu.CompilerParams(vmem_limit_bytes=40 << 20)


def cost(flops):
    return pl.CostEstimate(flops=flops, bytes_accessed=1 << 20, transcendentals=0)


def pack_x(vel, forc, phase, send_a, send_b):
    even, _, _ = position("gx")
    for out, first in ((send_a, jnp.where(even, 1, 0)), (send_b, jnp.where(even, 0, 1))):
        for c in range(3):
            for i in range(4):
                out[4 * c + i] = vel[c, 12 * first + i]
            for i in range(2):
                out[12 + 2 * c + i] = forc[c, 14 * first + i]
        out[18, 0:8] = phase[3 * first]


def halo(pair, axis, index):
    even, has_lo, has_hi = position(axis)
    a, b = pair[0][index], pair[1][index]
    lo = jnp.where(has_lo, jnp.where(even, b, a), 0.0)
    hi = jnp.where(has_hi, jnp.where(even, a, b), 0.0)
    return lo, hi


def tile_of(own, c, plane, o, width, rx, base, ry):
    rows = slice(8 * o, 8 * o + 8)
    if o == 4:
        sub = subs()
        if width == 4:
            lo, hi = halo(ry, "gy", c * 12 + plane % 12)
            if plane < 12:
                return jnp.where(sub < 4, hi, roll(lo, 4, 0))
            return jnp.where(sub < 4, roll(hi, 4, 0), lo)
        lo, hi = halo(ry, "gy", 36 + c * 5 + plane % 5)
        k = plane // 5
        return jnp.where(sub < 4, roll(hi, -2 * k, 0), roll(lo, 6 - 2 * k, 0))
    if plane < width:
        return halo(rx, "gx", (base + width * c + plane, rows))[0]
    if plane >= NX + width:
        return halo(rx, "gx", (base + width * c + plane - NX - width, rows))[1]
    return own[c, plane - width, rows]


def phase_rows(phase, rx, b):
    if b == 0:
        return halo(rx, "gx", (18, slice(0, 8)))[0]
    if b == 5:
        return halo(rx, "gx", (18, slice(0, 8)))[1]
    return phase[b - 1]


def phase_tiles(phase, rx, ry):
    lo, hi = halo(ry, "gy", 51)
    sub = subs()
    tiles = []
    for b in range(6):
        tiles.append(phase_rows(phase, rx, b))
        outer = jnp.where(sub == 0, hi[b : b + 1], jnp.where(sub == 1, lo[b : b + 1], 0.0))
        tiles.append(outer)
    return tiles


def pack_y(vel, forc, phase, rx_a, rx_b, send_a, send_b):
    rx = (rx_a, rx_b)
    even, _, _ = position("gy")
    sub = subs()

    def put(index, lo, hi):
        send_a[index] = jnp.where(even, hi, lo)
        send_b[index] = jnp.where(even, lo, hi)

    def u(c, p, o):
        return tile_of(vel, c, p, o, 4, rx, 0, None)

    def f(c, p, o):
        return tile_of(forc, c, p, o, 2, rx, 12, None)

    for c in range(3):
        for p in range(12):
            lo = jnp.where(sub < 4, u(c, p, 0), roll(u(c, p + 12, 0), 4, 0))
            hi = jnp.where(sub < 4, roll(u(c, p, 3), 4, 0), u(c, p + 12, 3))
            put(c * 12 + p, lo, hi)
        for g in range(5):
            lo = f(c, g, 0)
            hi = roll(f(c, g, 3), 2, 0)
            for k in range(1, 4):
                here = (sub >> 1) == k
                lo = jnp.where(here, roll(f(c, g + 5 * k, 0), 2 * k, 0), lo)
                hi = jnp.where(here, roll(f(c, g + 5 * k, 3), 2 * k + 2, 0), hi)
            put(36 + c * 5 + g, lo, hi)
    lo = jnp.zeros((8, 128), F32)
    hi = lo
    for b in range(6):
        tile = phase_rows(phase, rx, b)
        lo = jnp.where(sub == b, tile[0:1], lo)
        hi = jnp.where(sub == b, tile[7:8], hi)
    put(51, lo, hi)


def pack_tiles(tiles):
    lane = lanes()
    group = lane >> 3
    packed = []
    for half in range(2):
        value = jnp.zeros((8, 128), F32)
        for j, tile in enumerate(tiles[16 * half : 16 * half + 16]):
            value = jnp.where(group == j, roll(tile(), 8 * j + 4, 1), value)
        packed.append(value)
    keep = (lane & 4) == 0
    hi = jnp.where(keep, packed[0], roll(packed[1], 4, 1))
    lo = jnp.where(keep, roll(packed[0], -4, 1), packed[1])
    return lo, hi


def unpack_tiles(from_lo, from_hi, count):
    lane = lanes()
    keep = (lane & 4) == 0
    packed = (
        jnp.where(keep, from_lo, roll(from_hi, 4, 1)),
        jnp.where(keep, roll(from_lo, -4, 1), from_hi),
    )
    wanted = (lane < 4) | (lane >= 124)
    return [
        jnp.where(wanted, roll(packed[t // 16], 124 - 8 * (t % 16), 1), 0.0) for t in range(count)
    ]


def pack_z(vel, forc, phase, rx_a, rx_b, ry_a, ry_b, send_a, send_b):
    rx, ry = (rx_a, rx_b), (ry_a, ry_b)
    even, _, _ = position("gz")

    def put(index, lo, hi):
        send_a[index] = jnp.where(even, hi, lo)
        send_b[index] = jnp.where(even, lo, hi)

    for c in range(3):
        for q in range(4):
            put(4 * c + q, *pack_tiles([
                functools.partial(tile_of, vel, c, 6 * q + p, o, 4, rx, 0, ry)
                for p in range(6) for o in range(5)
            ]))
            put(12 + 4 * c + q, *pack_tiles([
                functools.partial(tile_of, forc, c, 5 * q + p, o, 2, rx, 12, ry)
                for p in range(5) for o in range(5)
            ]))
    lane = lanes()
    lo = jnp.zeros((8, 128), F32)
    hi = lo
    for j, tile in enumerate(phase_tiles(phase, rx, ry)):
        lo = jnp.where(lane == j, roll(tile, j, 1), lo)
        hi = jnp.where(lane == j, roll(tile, j - 31, 1), hi)
    put(24, lo, hi)


def shift_up(value):
    last = lanes() == 127
    a, b = roll(value[:, :128], 127, 1), roll(value[:, 128:], 127, 1)
    return jnp.concatenate([jnp.where(last, b, a), jnp.where(last, a, b)], axis=1)


def shift_down(value):
    first = lanes() == 0
    a, b = roll(value[:, :128], 1, 1), roll(value[:, 128:], 1, 1)
    return jnp.concatenate([jnp.where(first, b, a), jnp.where(first, a, b)], axis=1)


def band(rows, row_z, col_m):
    row = row_z(lax.broadcasted_iota(jnp.int32, (rows, 128), 0))
    col = col_m(lax.broadcasted_iota(jnp.int32, (rows, 128), 1))
    at = row - 2 * col + 1
    return jnp.where((at == 0) | (at == 3), 0.125, jnp.where((at == 1) | (at == 2), 0.375, 0.0)).astype(F32)


def exact_dot(a, b):
    return jnp.dot(a, b, preferred_element_type=F32, precision=lax.Precision.HIGHEST)


def four(a, b, c, d):
    return (a + 3.0 * b + 3.0 * c + d) * 0.125


def put_rows(ref, index, o, value):
    ref[index + (slice(8 + 8 * o, 16 + 8 * o),)] = value
    if o == 0:
        ref[index + (slice(48, 56),)] = value
    if o == 4:
        ref[index + (slice(0, 8),)] = value


def local_work(
    vel, forc, phase_ref, rx_a, rx_b, ry_a, ry_b, rz_a, rz_b, pre, yld,
    smoothed, visc_out, one_out, two_out, residual, partial,
    u_ref, f_ref, cells, v_ref, u1, u2, w_m, w_s, y1, c1, t2, t3,
):
    rx, ry, rz = (rx_a, rx_b), (ry_a, ry_b), (rz_a, rz_b)
    lo_x, hi_x = (flag.astype(F32) for flag in position("gx")[1:])
    lo_y, hi_y = (flag.astype(F32) for flag in position("gy")[1:])
    lo_z, hi_z = (flag.astype(F32) for flag in position("gz")[1:])
    lane = lanes()

    for c in range(3):
        for q in range(4):
            tiles = unpack_tiles(*halo(rz, "gz", 4 * c + q), 30)
            for t, side in enumerate(tiles):
                p, o = 6 * q + t // 5, t % 5
                own = tile_of(vel, c, p, o, 4, rx, 0, ry)
                put_rows(u_ref, (c, p), o, jnp.concatenate([own, side], axis=1))
            tiles = unpack_tiles(*halo(rz, "gz", 12 + 4 * c + q), 25)
            for t, side in enumerate(tiles):
                p, o = 5 * q + t // 5, t % 5
                own = tile_of(forc, c, p, o, 2, rx, 12, ry)
                f_ref[c, p, 8 * o : 8 * o + 8] = jnp.concatenate([own, side], axis=1)

    lo, hi = halo(rz, "gz", 24)
    rows = []
    for j, tile in enumerate(phase_tiles(phase_ref, rx, ry)):
        tile = jnp.where(lane == 32, roll(hi, 32 - j, 1), tile)
        rows.append(jnp.where(lane == 33, roll(lo, 33 - j, 1), tile))
    ph = jnp.concatenate(rows, axis=0)
    zi = lax.broadcasted_iota(jnp.int32, (128, 256), 1)
    bz = lax.broadcasted_iota(jnp.int32, (128, 256), 0)
    wide = jnp.where(zi < 128, zi >> 2, jnp.where(zi < 192, 32, 33))
    ph_z = jnp.dot(ph, (wide == bz).astype(F32), preferred_element_type=F32)
    ri = lax.broadcasted_iota(jnp.int32, (40, 16), 0)
    by = lax.broadcasted_iota(jnp.int32, (40, 16), 1)
    tall = (jnp.where(ri < 32, ri >> 2, jnp.where(ri < 36, 8, 9)) == by).astype(F32)
    for b in range(6):
        cells[b] = jnp.dot(tall, ph_z[16 * b : 16 * b + 16], preferred_element_type=F32)

    wide_lane = lanes(8, 256)
    mask_z = jnp.where(
        wide_lane < 128, 1.0, jnp.where(wide_lane < 131, hi_z, jnp.where(wide_lane >= 253, lo_z, 0.0))
    )
    row4 = subs(8, 256)
    mask_zy = mask_z * jnp.where(row4 < 4, hi_y, lo_y)

    def viscosity(vx, _):
        px = vx + 1
        mask_x = jnp.where(vx < 3, lo_x, jnp.where(vx >= 19, hi_x, 1.0))
        bx = (vx + 1) >> 2
        for o in range(5):
            d = []
            for c in range(3):
                mid = u_ref[c, px, 8 + 8 * o : 16 + 8 * o]
                d.append((
                    u_ref[c, px + 1, 8 + 8 * o : 16 + 8 * o] - u_ref[c, px - 1, 8 + 8 * o : 16 + 8 * o],
                    u_ref[c, px, 9 + 8 * o : 17 + 8 * o] - u_ref[c, px, 7 + 8 * o : 15 + 8 * o],
                    shift_up(mid) - shift_down(mid),
                ))
            a01, a02, a12 = d[0][1] + d[1][0], d[0][2] + d[2][0], d[1][2] + d[2][1]
            own = d[0][0] * d[0][0] + d[1][1] * d[1][1] + d[2][2] * d[2][2]
            off = a01 * a01 + a02 * a02 + a12 * a12
            invariant = 1.0 + (own * 0.125 + off * 0.0625)
            phase = cells[bx, 8 * o : 8 * o + 8]
            creep = jnp.full((8, 256), pre[0], F32)
            limit = jnp.full((8, 256), yld[0], F32)
            for k in range(1, 8):
                here = phase == float(k)
                creep = jnp.where(here, pre[k], creep)
                limit = jnp.where(here, yld[k], limit)
            value = jnp.minimum(
                creep * jnp.exp(jnp.log(invariant) * (-1.0 / 3.0)), (0.5 * limit) * lax.rsqrt(invariant)
            )
            put_rows(v_ref, (vx,), o, value * (mask_x * (mask_zy if o == 4 else mask_z)))
        return 0

    lax.fori_loop(0, 22, viscosity, 0)

    def faces(vx, o):
        mid = v_ref[vx, 8 + 8 * o : 16 + 8 * o]
        return mid, (
            mid + v_ref[vx + 1, 8 + 8 * o : 16 + 8 * o],
            mid + v_ref[vx - 1, 8 + 8 * o : 16 + 8 * o],
            mid + v_ref[vx, 9 + 8 * o : 17 + 8 * o],
            mid + v_ref[vx, 7 + 8 * o : 15 + 8 * o],
            mid + shift_up(mid),
            mid + shift_down(mid),
        )

    def around(ref, c, p, o, f):
        mid = ref[c, p, 8 + 8 * o : 16 + 8 * o]
        total = f[0] * ref[c, p + 1, 8 + 8 * o : 16 + 8 * o]
        total = total + f[1] * ref[c, p - 1, 8 + 8 * o : 16 + 8 * o]
        total = total + f[2] * ref[c, p, 9 + 8 * o : 17 + 8 * o]
        total = total + f[3] * ref[c, p, 7 + 8 * o : 15 + 8 * o]
        total = total + f[4] * shift_up(mid)
        return mid, total + f[5] * shift_down(mid)

    def sweep(source, target, first, first_u):
        def body(x, _):
            for o in range(5):
                mid_v, f = faces(x + first, o)
                diag = (f[0] + f[1]) + (f[2] + f[3]) + (f[4] + f[5])
                rate = jnp.where(mid_v > 0.0, 0.8 / diag, 0.0)
                for c in range(3):
                    mid, total = around(source, c, x + first_u, o, f)
                    force = f_ref[c, x + first - 1, 8 * o : 8 * o + 8]
                    put_rows(target, (c, x), o, 0.2 * mid + rate * (2.0 * force + total))
            return 0

        return body

    lax.fori_loop(0, 20, sweep(u_ref, u1, 1, 2), 0)
    lax.fori_loop(0, 18, sweep(u1, u2, 2, 1), 0)

    def last(x, acc):
        for o in range(4):
            _, f = faces(x + 3, o)
            diag = (f[0] + f[1]) + (f[2] + f[3]) + (f[4] + f[5])
            for c in range(3):
                mid, total = around(u2, c, x + 1, o, f)
                force = f_ref[c, x + 2, 8 * o : 8 * o + 8]
                value = (force + 0.5 * (total - diag * mid))[:, :128]
                residual[c, x, 8 * o : 8 * o + 8] = value
                smoothed[c, x, 8 * o : 8 * o + 8] = mid[:, :128]
                acc = acc + value * value
            visc_out[x, 8 * o : 8 * o + 8] = v_ref[x + 3, 8 + 8 * o : 16 + 8 * o, 0:128]
        return acc

    acc = lax.fori_loop(0, NX, last, jnp.zeros((8, 128), F32))
    square = jnp.sum(jnp.sum(acc, axis=1, keepdims=True), axis=0, keepdims=True)

    def coarse_x(k, _):
        value = four(v_ref[2 * k], v_ref[2 * k + 1], v_ref[2 * k + 2], v_ref[2 * k + 3])
        w_m[k] = value[:, :128]
        w_s[k] = value[:, 128:]
        return 0

    lax.fori_loop(0, 10, coarse_x, 0)
    y1[...] = jnp.zeros(y1.shape, F32)
    for k in range(10):
        for ref, at in ((w_m, 0), (w_s, 128)):
            y1[k, 0:18, at : at + 128] = four(*(ref[k, pl.ds(5 + i, 18, stride=2)] for i in range(4)))
    band1 = band(256, lambda r: jnp.where(r < 192, r, r - 256), lambda m: jnp.where(m < 65, m, jnp.where(m == 65, -1, 1000)))
    coarse = exact_dot(y1[...].reshape(240, 256), band1).reshape(10, 24, 128)
    row24, lane24 = subs(24), lanes(24)
    mask_yz = jnp.where(row24 == 0, lo_y, jnp.where(row24 == 17, hi_y, 1.0)) * jnp.where(
        lane24 == 64, hi_z, jnp.where(lane24 == 65, lo_z, 1.0)
    )
    for k in range(10):
        mask = mask_yz * (lo_x if k == 0 else hi_x if k == 9 else 1.0)
        c1[k] = coarse[k] * mask
    for k in range(8):
        one_out[k] = c1[k + 1, 1:17, 0:64]
    rows = []
    for k in range(4):
        t2[...] = four(c1[2 * k], c1[2 * k + 1], c1[2 * k + 2], c1[2 * k + 3])
        rows.append(four(*(t2[pl.ds(i, 8, stride=2)] for i in range(4))))
    band2 = band(128, lambda r: jnp.where(r < 65, r, jnp.where(r == 65, -1, 100000)), lambda m: jnp.where(m < 32, m, 1000))
    coarse = exact_dot(jnp.concatenate(rows, axis=0), band2)
    planes = [coarse[8 * k : 8 * k + 8] for k in range(4)]
    for k in range(4):
        two_out[k] = planes[k][:, 0:32]
    thirds = (
        0.125 * planes[0],
        0.125 * (3.0 * planes[0] + 3.0 * planes[1] + planes[2]),
        0.125 * (planes[1] + 3.0 * planes[2] + 3.0 * planes[3]),
        0.125 * planes[3],
    )
    rows = []
    t3[...] = jnp.zeros(t3.shape, F32)
    for k in range(4):
        t3[4:12] = thirds[k]
        rows.append(four(*(t3[pl.ds(1 + i, 8, stride=2)] for i in range(4))))
    band3 = band(128, lambda r: jnp.where(r < 32, r, 100000), lambda m: jnp.where(m < 18, m - 1, 1000))
    coarse = exact_dot(jnp.concatenate(rows, axis=0), band3)
    for k in range(4):
        partial[k] = jnp.where(subs() == 7, square, coarse[8 * k : 8 * k + 8])


def with_sum(tile, total):
    row = lax.broadcasted_iota(jnp.int32, tile.shape, tile.ndim - 2)
    return jnp.where(row == 7, total, tile)


def finish(partial):
    total = partial[0, 7:8, :]
    even, has_lo, has_hi = position("gx")
    got_a = pair_a(with_sum(jnp.where(even, partial[3], partial[0]), total), "gx")
    total = total + got_a[7:8]
    got_b = pair_b(with_sum(jnp.where(even, partial[0], partial[3]), total), "gx")
    total = total + got_b[7:8]
    lo, hi = jnp.where(even, got_b, got_a), jnp.where(even, got_a, got_b)
    inner = jnp.stack(
        [partial[1] + jnp.where(has_lo, lo, 0.0), partial[2] + jnp.where(has_hi, hi, 0.0)]
    )
    total = total + far("gx", total)
    even, has_lo, has_hi = position("gy")
    got_a = pair_a(with_sum(inner, total), "gy")
    total = total + got_a[0, 7:8]
    got_b = pair_b(with_sum(inner, total), "gy")
    total = total + got_b[0, 7:8]
    lo, hi = jnp.where(even, got_b, got_a), jnp.where(even, got_a, got_b)
    row = lax.broadcasted_iota(jnp.int32, inner.shape, 1)
    inner = (
        inner
        + jnp.where((row == 1) & has_lo, jnp.roll(lo, -4, 1), 0.0)
        + jnp.where((row == 4) & has_hi, jnp.roll(hi, 4, 1), 0.0)
    )
    even, has_lo, has_hi = position("gz")
    got_a = pair_a(with_sum(inner, total), "gz")
    total = total + got_a[0, 7:8]
    got_b = pair_b(with_sum(inner, total), "gz")
    total = total + got_b[0, 7:8]
    lo, hi = jnp.where(even, got_b, got_a), jnp.where(even, got_a, got_b)
    total = total + far("gz", total)
    three = inner[:, 1:5, 1:17]
    z = lax.broadcasted_iota(jnp.int32, three.shape, 2)
    three = (
        three
        + jnp.where((z == 0) & has_lo, lo[:, 1:5, 17:18], 0.0)
        + jnp.where((z == 15) & has_hi, hi[:, 1:5, 0:1], 0.0)
    )
    return total[0, 0], three


def far(axis, total):
    count = lax.axis_size(axis)
    if count == 4:
        return jnp.zeros_like(total)
    return lax.ppermute(total, axis, [(i, (i + count // 2) % count) for i in range(count)])


def pack(kernel, shape, name, *args):
    return pl.pallas_call(
        kernel, out_shape=[sds(*shape)] * 2, in_specs=[VMEM] * len(args), out_specs=[VMEM] * 2,
        compiler_params=params(), name=name,
    )(*args)


def per_device(velocity, forcing, phase_block, prefactor, yield_stress):
    phase = jnp.pad(phase_block.astype(F32), ((0, 0), (0, 0), (0, 96)))
    own = (velocity, forcing, phase)
    send_a, send_b = pack(pack_x, (19, 32, 128), "pack_x", *own)
    rx = (pair_a(send_a, "gx"), pair_b(send_b, "gx"))
    send_a, send_b = pack(pack_y, (52, 8, 128), "pack_y", *own, *rx)
    ry = (pair_a(send_a, "gy"), pair_b(send_b, "gy"))
    send_a, send_b = pack(pack_z, (25, 8, 128), "pack_z", *own, *rx, *ry)
    rz = (pair_a(send_a, "gz"), pair_b(send_b, "gz"))
    smoothed, visc, one, two, residual, partial = pl.pallas_call(
        local_work,
        out_shape=[
            sds(3, NX, NY, NZ), sds(NX, NY, NZ), sds(8, 16, 64), sds(4, 8, 32), sds(3, NX, NY, NZ), sds(4, 8, 128),
        ],
        in_specs=[VMEM] * 9 + [SMEM] * 2,
        out_specs=[VMEM] * 6,
        scratch_shapes=[
            pltpu.VMEM((3, 24, 56, 256), F32), pltpu.VMEM((3, 20, 40, 256), F32), pltpu.VMEM((6, 40, 256), F32),
            pltpu.VMEM((22, 56, 256), F32), pltpu.VMEM((3, 20, 56, 256), F32), pltpu.VMEM((3, 18, 56, 256), F32),
            pltpu.VMEM((10, 56, 128), F32), pltpu.VMEM((10, 56, 128), F32), pltpu.VMEM((10, 24, 256), F32),
            pltpu.VMEM((10, 24, 128), F32), pltpu.VMEM((24, 128), F32), pltpu.VMEM((24, 128), F32),
        ],
        compiler_params=params(), name="local_work",
    )(*own, *rx, *ry, *rz, prefactor, yield_stress)
    total, three = finish(partial)
    cells = 3.0 * NX * NY * NZ
    for axis in AX:
        cells = cells * lax.axis_size(axis)
    return smoothed, visc, one, two, three, residual, jnp.sqrt(total / cells)


def solution(mesh):
    field, cell = P(None, *AX), P(*AX)
    return jax.shard_map(
        per_device,
        mesh=mesh,
        in_specs=(field, field, cell, P(), P()),
        out_specs=(field, cell, cell, cell, cell, field, P()),
        check_vma=False,
    )
```

time: 234 us -> 85.9 us (0.37); the launches traced: 231 us -> 85.7 us
  local copies, waits for them, and re-layouts: 67.2 us -> 2.3 us
  starting transfers between devices: 78.6 us -> 25.2 us
  blocking collectives: 44.4 us -> 0 us
  other arithmetic: 32.1 us -> 2.08 us
  waiting for transfers between devices: 5.66 us -> 34.8 us
  Pallas kernels: 0 us -> 19.3 us
    ppermute x30 -> x14, starting transfers between devices: 78.6 us -> 25.2 us  [the longest x6 16.3 us: pair_b(): lax.ppermute(value, axis, [(i, (i + 1) % count if i % 2 else (i - 1) % co...]
    psum x4 -> x0, blocking collectives: 44.4 us -> none  [by_axis(): return functools.reduce(lax.psum, axes, shard)]
    slice x48 -> x1, local copies, waits for them, and re-layouts: 31.7 us -> 0.01 us  [finish(): jnp.roll(lo, -4, 1)]
    ppermute x30 -> x14, waiting for transfers between devices: 5.66 us -> 34.8 us  [the longest x6 16 us: pair_b(): lax.ppermute(value, axis, [(i, (i + 1) % count if i % 2 else (i - 1) % co...]
    pallas_call x0 -> x4, Pallas kernels: none -> 19.3 us  [the longest x1 17 us: per_device(): pl.pallas_call(local_work, out_shape=[sds(3, NX, NY, NZ), sds(NX, NY, NZ)...]
    add x5 -> x8, other arithmetic: 17.5 us -> 0.71 us  [the longest x1 0.68 us: finish(): three + jnp.where((z == 0) & has_lo, lo[:, 1:5, 17:18], 0.0)]
    reshape x2 -> x0, local copies, waits for them, and re-layouts: 16.3 us -> none  [expand_table(): return spread.reshape(blocks_x * BLOCK, blocks_y * BLOCK, blocks_z * BLOCK)]
    broadcast_in_dim x2 -> x1, local copies, waits for them, and re-layouts: 8.89 us -> 0.01 us  [with_sum(): return jnp.where(row == 7, total, tile)]
  transfers between devices with their start and end apart: 30 -> 14, of which waited for: 3 -> 12; matrix products, arithmetic and copies ran while one was open for 26% -> 1% of each run, Pallas kernels for 0% -> 0%
where the time goes in v1:
time: 85.9 us; the launch traced here: 85.7 us
  waiting for transfers between devices  34.8 us (41%)
  starting transfers between devices  25.2 us (29%)
  Pallas kernels  19.3 us (22%)
  local copies, waits for them, and re-layouts  2.3 us (3%)
  other arithmetic  2.08 us (2%)
  between operations  1.94 us (2%)
    pallas_call x1, Pallas kernels, per_device(): pl.pallas_call(local_work, out_shape=[sds(3, NX, NY, NZ), sds(NX, NY, NZ)...  17 us
    ppermute x6, starting transfers between devices, pair_b(): lax.ppermute(value, axis, [(i, (i + 1) % count if i % 2 else (i - 1) % co...  16.3 us
    ppermute x6, waiting for transfers between devices, pair_b(): lax.ppermute(value, axis, [(i, (i + 1) % count if i % 2 else (i - 1) % co...  16 us
    ppermute x6, waiting for transfers between devices, pair_a(): return lax.ppermute(value, axis, [(i, i ^ 1) for i in range(count)])  13 us
    ppermute x2, waiting for transfers between devices, far(): lax.ppermute(total, axis, [(i, (i + count // 2) % count) for i in range(c...  5.87 us
    ppermute x2, starting transfers between devices, far(): lax.ppermute(total, axis, [(i, (i + count // 2) % count) for i in range(c...  5.84 us
    ppermute x6, starting transfers between devices, pair_a(): return lax.ppermute(value, axis, [(i, i ^ 1) for i in range(count)])  3.07 us
    pallas_call x3, Pallas kernels, pack(): pl.pallas_call(kernel, out_shape=[sds(*shape)] * 2, in_specs=[VMEM] * len...  2.35 us
  transfers between devices with their start and end apart: 14, of which 12 were waited for; matrix products, arithmetic and copies ran while one was open for 1% of the time, Pallas kernels for 0%

profile of v1, /device:TPU:24, one launch (start us, length us, event | category | flops | bytes accessed | tf_op | source)
XLA Modules:
  0.0 85.7 jit_solution(14801788628565063724)
XLA Ops:
  0.6 0.7 convert_element_type.5
  1.4 0.0 copy-start
  1.4 1.1 %copy-done = f32[3,16,32,128]{3,2,1,0:T(8,128)S(1)} copy-done((f32[3,16,32,128]{3,2,1,0:T(8,128)S(1)}, f32[3,16,32,128]{3,2,1,0:T(8,128)}, u32[]{:S(2)}) %copy-start) | copy-done | bytes 786456
  2.5 0.0 copy-start.2
  2.5 1.1 %copy-done.2 = f32[3,16,32,128]{3,2,1,0:T(8,128)S(1)} copy-done((f32[3,16,32,128]{3,2,1,0:T(8,128)S(1)}, f32[3,16,32,128]{3,2,1,0:T(8,128)}, u32[]{:S(2)}) %copy-start.2) | copy-done | bytes 786456
  3.7 0.1 collective-permute-start
  3.8 0.0 copy-start.1
  3.8 0.0 copy-start.3
  3.8 2.8 %collective-permute-start.1 = (f32[19,32,128]{2,1,0:T(8,128)S(1)}, f32[19,32,128]{2,1,0:T(8,128)S(1)}, u32[]{:S(2)}, u32[]{:S(2)}) collective-permute-start(f32[19,32,128]{2,1,0:T(8,128)S(1)} %get-tuple-element.20), channel_id=1, source_target_pairs={{0,224},{32,64},{64,32},{96,128},{128,96},{160,192},{192,160},{224... | collective-permute-start | bytes 933896 | tf_op jit(solution)/shard_map/ppermute | solution.py:48
  6.6 0.0 collective-permute-done.rx_a
  6.6 4.8 %collective-permute-done.1.rx_b = f32[19,32,128]{2,1,0:T(8,128)S(1)} collective-permute-done((f32[19,32,128]{2,1,0:T(8,128)S(1)}, f32[19,32,128]{2,1,0:T(8,128)S(1)}, u32[]{:S(2)}, u32[]{:S(2)}) %collective-permute-start.1) | collective-permute-done | bytes 311328 | tf_op jit(solution)/shard_map/ppermute | solution.py:48
  11.4 0.1 pack_y.1
  11.5 0.8 collective-permute-start.2
  12.3 1.3 %collective-permute-start.3 = (f32[52,8,128]{2,1,0:T(8,128)S(1)}, f32[52,8,128]{2,1,0:T(8,128)S(1)}, u32[]{:S(2)}, u32[]{:S(2)}) collective-permute-start(f32[52,8,128]{2,1,0:T(8,128)S(1)} %get-tuple-element.22), channel_id=1, source_target_pairs={{0,24},{8,16},{16,8},{24,0},{1,25},{9,17},{17,9},{25,1},{2,26},{10... | collective-permute-start | bytes 638984 | tf_op jit(solution)/shard_map/ppermute | solution.py:48
  13.6 4.6 %collective-permute-done.2.ry_a = f32[52,8,128]{2,1,0:T(8,128)S(1)} collective-permute-done((f32[52,8,128]{2,1,0:T(8,128)S(1)}, f32[52,8,128]{2,1,0:T(8,128)S(1)}, u32[]{:S(2)}, u32[]{:S(2)}) %collective-permute-start.2) | collective-permute-done | bytes 213024 | tf_op jit(solution)/shard_map/ppermute | solution.py:43
  18.2 1.7 %collective-permute-done.3.ry_b = f32[52,8,128]{2,1,0:T(8,128)S(1)} collective-permute-done((f32[52,8,128]{2,1,0:T(8,128)S(1)}, f32[52,8,128]{2,1,0:T(8,128)S(1)}, u32[]{:S(2)}, u32[]{:S(2)}) %collective-permute-start.3) | collective-permute-done | bytes 213024 | tf_op jit(solution)/shard_map/ppermute | solution.py:48
  19.9 0.0 copy-done.1
  19.9 0.0 copy-done.3
  19.9 2.2 %pack_z.1 = (f32[25,8,128]{2,1,0:T(8,128)S(1)}, f32[25,8,128]{2,1,0:T(8,128)S(1)}) custom-call(f32[3,16,32,128]{3,2,1,0:T(8,128)S(1)} %copy-done.1, f32[3,16,32,128]{3,2,1,0:T(8,128)S(1)} %copy-done.3, f32[4,8,128]{2,1,0:T(8,128)S(1)} %pad.4.phase.phase_ref, f32[19,32,128]{2,1,0:T(8,128)S(1)} %collective-permute-done.rx_a, ...), custom_call_target="tpu_custom_call" | custom-call | tf_op jit(solution)/shard_map/pack_z/pallas_call | solution.py:480
  22.1 2.0 %collective-permute-start.4 = (f32[25,8,128]{2,1,0:T(8,128)S(1)}, f32[25,8,128]{2,1,0:T(8,128)S(1)}, u32[]{:S(2)}, u32[]{:S(2)}) collective-permute-start(f32[25,8,128]{2,1,0:T(8,128)S(1)} %get-tuple-element.23), channel_id=1, source_target_pairs={{0,1},{1,0},{2,3},{3,2},{4,5},{5,4},{6,7},{7,6},{8,9},{9,8},{10,11... | collective-permute-start | bytes 307208 | tf_op jit(solution)/shard_map/ppermute | solution.py:43
  24.1 0.0 copy-start.4
  24.1 0.0 copy-start.5
  24.1 4.9 %collective-permute-start.5 = (f32[25,8,128]{2,1,0:T(8,128)S(1)}, f32[25,8,128]{2,1,0:T(8,128)S(1)}, u32[]{:S(2)}, u32[]{:S(2)}) collective-permute-start(f32[25,8,128]{2,1,0:T(8,128)S(1)} %get-tuple-element.24), channel_id=1, source_target_pairs={{0,7},{1,2},{2,1},{3,4},{4,3},{5,6},{6,5},{7,0},{8,15},{9,10},{10,... | collective-permute-start | bytes 307208 | tf_op jit(solution)/shard_map/ppermute | solution.py:48
  29.1 0.0 collective-permute-done.4.rz_a
  29.1 2.6 %collective-permute-done.5.rz_b = f32[25,8,128]{2,1,0:T(8,128)S(1)} collective-permute-done((f32[25,8,128]{2,1,0:T(8,128)S(1)}, f32[25,8,128]{2,1,0:T(8,128)S(1)}, u32[]{:S(2)}, u32[]{:S(2)}) %collective-permute-start.5) | collective-permute-done | bytes 102432 | tf_op jit(solution)/shard_map/ppermute | solution.py:48
  31.7 0.0 copy-done.4
  31.7 0.0 copy-done.5
  31.7 17.0 %local_work.1 = (f32[3,16,32,128]{3,2,1,0:T(8,128)}, f32[16,32,128]{2,1,0:T(8,128)}, f32[8,16,64]{2,1,0:T(8,128)}, f32[4,8,32]{2,1,0:T(8,128)}, f32[3,16,32,128]{3,2,1,0:T(8,128)}, /*index=5*/f32[4,8,128]{2,1,0:T(8,128)S(1)}) custom-call(f32[3,16,32,128]{3,2,1,0:T(8,128)S(1)} %copy-done.1, f32[3,16,32,128]{3,2,1,0:T(8,128)S(1)} %copy-done.3, ...), custom_call_target="tpu_custom_call" | custom-call | tf_op jit(solution)/shard_map/local_work/pallas_call | solution.py:495
  48.7 0.1 bitcast_select_fusion.1
  48.8 0.0 collective-permute-start.6
  48.8 1.2 %collective-permute-done.6 = f32[8,128]{1,0:T(8,128)S(1)} collective-permute-done((f32[8,128]{1,0:T(8,128)S(1)}, f32[8,128]{1,0:T(8,128)S(1)}, u32[]{:S(2)}, u32[]{:S(2)}) %collective-permute-start.6) | collective-permute-done | bytes 4128 | tf_op jit(solution)/shard_map/ppermute | solution.py:43
  50.0 0.1 bitcast_select_fusion
  50.0 3.1 %collective-permute-start.7 = (f32[8,128]{1,0:T(8,128)S(1)}, f32[8,128]{1,0:T(8,128)S(1)}, u32[]{:S(2)}, u32[]{:S(2)}) collective-permute-start(f32[8,128]{1,0:T(8,128)S(1)} %bitcast_select_fusion), channel_id=1, source_target_pairs={{0,224},{32,64},{64,32},{96,128},{128,96},{160,192},{192,160},{224... | collective-permute-start | bytes 12296 | tf_op jit(solution)/shard_map/ppermute | solution.py:48
  53.1 1.3 %collective-permute-done.7 = f32[8,128]{1,0:T(8,128)S(1)} collective-permute-done((f32[8,128]{1,0:T(8,128)S(1)}, f32[8,128]{1,0:T(8,128)S(1)}, u32[]{:S(2)}, u32[]{:S(2)}) %collective-permute-start.7) | collective-permute-done | bytes 4128 | tf_op jit(solution)/shard_map/ppermute | solution.py:48
  54.4 1.4 %collective-permute-start.8 = (f32[1,128]{1,0:T(1,128)S(1)}, f32[1,128]{1,0:T(1,128)S(1)}, u32[]{:S(2)}, u32[]{:S(2)}) collective-permute-start(f32[1,128]{1,0:T(1,128)S(1)} %slice_add_fusion.1), channel_id=1, source_target_pairs={{0,128},{32,160},{64,192},{96,224},{128,0},{160,32},{192,64},{224,... | collective-permute-start | bytes 1544 | tf_op jit(solution)/shard_map/ppermute | solution.py:476
  55.8 3.7 %collective-permute-done.8 = f32[1,128]{1,0:T(1,128)S(1)} collective-permute-done((f32[1,128]{1,0:T(1,128)S(1)}, f32[1,128]{1,0:T(1,128)S(1)}, u32[]{:S(2)}, u32[]{:S(2)}) %collective-permute-start.8) | collective-permute-done | bytes 544 | tf_op jit(solution)/shard_map/ppermute | solution.py:476
  59.5 0.1 fusion.3
  59.6 0.1 collective-permute-start.9
  59.7 3.6 %collective-permute-done.9 = f32[2,8,128]{2,1,0:T(8,128)S(1)} collective-permute-done((f32[2,8,128]{2,1,0:T(8,128)S(1)}, f32[2,8,128]{2,1,0:T(8,128)S(1)}, u32[]{:S(2)}, u32[]{:S(2)}) %collective-permute-start.9) | collective-permute-done | bytes 8224 | tf_op jit(solution)/shard_map/ppermute | solution.py:43
  63.3 0.1 fusion.2
  63.4 1.1 %collective-permute-start.10 = (f32[2,8,128]{2,1,0:T(8,128)S(1)}, f32[2,8,128]{2,1,0:T(8,128)S(1)}, u32[]{:S(2)}, u32[]{:S(2)}) collective-permute-start(f32[2,8,128]{2,1,0:T(8,128)S(1)} %fusion.2), channel_id=1, source_target_pairs={{0,24},{8,16},{16,8},{24,0},{1,25},{9,17},{17,9},{25,1},{2,26},{10... | collective-permute-start | bytes 24584 | tf_op jit(solution)/shard_map/ppermute | solution.py:48
  64.4 3.8 %collective-permute-done.10 = f32[2,8,128]{2,1,0:T(8,128)S(1)} collective-permute-done((f32[2,8,128]{2,1,0:T(8,128)S(1)}, f32[2,8,128]{2,1,0:T(8,128)S(1)}, u32[]{:S(2)}, u32[]{:S(2)}) %collective-permute-start.10) | collective-permute-done | bytes 8224 | tf_op jit(solution)/shard_map/ppermute | solution.py:48
  68.3 0.1 broadcast_select_fusion.1
  68.3 0.0 collective-permute-start.11
  68.4 3.6 %collective-permute-done.11 = f32[2,8,128]{2,1,0:T(8,128)S(1)} collective-permute-done((f32[2,8,128]{2,1,0:T(8,128)S(1)}, f32[2,8,128]{2,1,0:T(8,128)S(1)}, u32[]{:S(2)}, u32[]{:S(2)}) %collective-permute-start.11) | collective-permute-done | bytes 8224 | tf_op jit(solution)/shard_map/ppermute | solution.py:43
  72.0 0.1 broadcast_select_fusion
  72.1 3.1 %collective-permute-start.12 = (f32[2,8,128]{2,1,0:T(8,128)S(1)}, f32[2,8,128]{2,1,0:T(8,128)S(1)}, u32[]{:S(2)}, u32[]{:S(2)}) collective-permute-start(f32[2,8,128]{2,1,0:T(8,128)S(1)} %broadcast_select_fusion), channel_id=1, source_target_pairs={{0,7},{1,2},{2,1},{3,4},{4,3},{5,6},{6,5},{7,0},{8,15},{9,10},{10,... | collective-permute-start | bytes 24584 | tf_op jit(solution)/shard_map/ppermute | solution.py:48
  75.2 1.8 %collective-permute-done.12 = f32[2,8,128]{2,1,0:T(8,128)S(1)} collective-permute-done((f32[2,8,128]{2,1,0:T(8,128)S(1)}, f32[2,8,128]{2,1,0:T(8,128)S(1)}, u32[]{:S(2)}, u32[]{:S(2)}) %collective-permute-start.12) | collective-permute-done | bytes 8224 | tf_op jit(solution)/shard_map/ppermute | solution.py:48
  77.0 4.5 %collective-permute-start.13 = (f32[1,128]{1,0:T(1,128)S(1)}, f32[1,128]{1,0:T(1,128)S(1)}, u32[]{:S(2)}, u32[]{:S(2)}) collective-permute-start(f32[1,128]{1,0:T(1,128)S(1)} %fusion.9), channel_id=1, source_target_pairs={{0,4},{1,5},{2,6},{3,7},{4,0},{5,1},{6,2},{7,3},{8,12},{9,13},{10,... | collective-permute-start | bytes 1544 | tf_op jit(solution)/shard_map/ppermute | solution.py:476
  81.4 0.2 fusion.5
  81.6 0.7 fusion.6
  82.3 2.2 %collective-permute-done.13 = f32[1,128]{1,0:T(1,128)S(1)} collective-permute-done((f32[1,128]{1,0:T(1,128)S(1)}, f32[1,128]{1,0:T(1,128)S(1)}, u32[]{:S(2)}, u32[]{:S(2)}) %collective-permute-start.13) | collective-permute-done | bytes 544 | tf_op jit(solution)/shard_map/ppermute | solution.py:476
  (18 shorter events, 0.1 us)
Async XLA Ops:
  1.4 1.1 %copy-start = (f32[3,16,32,128]{3,2,1,0:T(8,128)S(1)}, f32[3,16,32,128]{3,2,1,0:T(8,128)}, u32[]{:S(2)}) copy-start(f32[3,16,32,128]{3,2,1,0:T(8,128)} %vel.7) | copy-start | bytes 2359300
  2.5 1.1 %copy-start.2 = (f32[3,16,32,128]{3,2,1,0:T(8,128)S(1)}, f32[3,16,32,128]{3,2,1,0:T(8,128)}, u32[]{:S(2)}) copy-start(f32[3,16,32,128]{3,2,1,0:T(8,128)} %forc.7) | copy-start | bytes 2359300
  3.7 3.0 %collective-permute-start = (f32[19,32,128]{2,1,0:T(8,128)S(1)}, f32[19,32,128]{2,1,0:T(8,128)S(1)}, u32[]{:S(2)}, u32[]{:S(2)}) collective-permute-start(f32[19,32,128]{2,1,0:T(8,128)S(1)} %get-tuple-element.19), channel_id=1, source_target_pairs={{0,32},{32,0},{64,96},{96,64},{128,160},{160,128},{192,224},{224,1... | collective-permute-start | bytes 933896 | tf_op jit(solution)/shard_map/ppermute | solution.py:43
  3.8 16.1 %copy-start.1 = (f32[3,16,32,128]{3,2,1,0:T(8,128)S(1)}, f32[3,16,32,128]{3,2,1,0:T(8,128)}, u32[]{:S(2)}) copy-start(f32[3,16,32,128]{3,2,1,0:T(8,128)} %vel.7) | copy-start | bytes 2359300
  3.8 16.1 %copy-start.3 = (f32[3,16,32,128]{3,2,1,0:T(8,128)S(1)}, f32[3,16,32,128]{3,2,1,0:T(8,128)}, u32[]{:S(2)}) copy-start(f32[3,16,32,128]{3,2,1,0:T(8,128)} %forc.7) | copy-start | bytes 2359300
  3.8 7.6 %collective-permute-start.1 = (f32[19,32,128]{2,1,0:T(8,128)S(1)}, f32[19,32,128]{2,1,0:T(8,128)S(1)}, u32[]{:S(2)}, u32[]{:S(2)}) collective-permute-start(f32[19,32,128]{2,1,0:T(8,128)S(1)} %get-tuple-element.20), channel_id=1, source_target_pairs={{0,224},{32,64},{64,32},{96,128},{128,96},{160,192},{192,160},{224... | collective-permute-start | bytes 933896 | tf_op jit(solution)/shard_map/ppermute | solution.py:48
  11.5 6.7 %collective-permute-start.2 = (f32[52,8,128]{2,1,0:T(8,128)S(1)}, f32[52,8,128]{2,1,0:T(8,128)S(1)}, u32[]{:S(2)}, u32[]{:S(2)}) collective-permute-start(f32[52,8,128]{2,1,0:T(8,128)S(1)} %get-tuple-element.21), channel_id=1, source_target_pairs={{0,8},{8,0},{16,24},{24,16},{1,9},{9,1},{17,25},{25,17},{2,10},{10... | collective-permute-start | bytes 638984 | tf_op jit(solution)/shard_map/ppermute | solution.py:43
  12.3 7.6 %collective-permute-start.3 = (f32[52,8,128]{2,1,0:T(8,128)S(1)}, f32[52,8,128]{2,1,0:T(8,128)S(1)}, u32[]{:S(2)}, u32[]{:S(2)}) collective-permute-start(f32[52,8,128]{2,1,0:T(8,128)S(1)} %get-tuple-element.22), channel_id=1, source_target_pairs={{0,24},{8,16},{16,8},{24,0},{1,25},{9,17},{17,9},{25,1},{2,26},{10... | collective-permute-start | bytes 638984 | tf_op jit(solution)/shard_map/ppermute | solution.py:48
  22.1 6.9 %collective-permute-start.4 = (f32[25,8,128]{2,1,0:T(8,128)S(1)}, f32[25,8,128]{2,1,0:T(8,128)S(1)}, u32[]{:S(2)}, u32[]{:S(2)}) collective-permute-start(f32[25,8,128]{2,1,0:T(8,128)S(1)} %get-tuple-element.23), channel_id=1, source_target_pairs={{0,1},{1,0},{2,3},{3,2},{4,5},{5,4},{6,7},{7,6},{8,9},{9,8},{10,11... | collective-permute-start | bytes 307208 | tf_op jit(solution)/shard_map/ppermute | solution.py:43
  24.1 7.6 %copy-start.4 = (f32[8]{0:T(128)S(1)}, f32[8]{0:T(128)}, u32[]{:S(2)}) copy-start(f32[8]{0:T(128)} %pre.1) | copy-start | bytes 100
  24.1 7.6 %copy-start.5 = (f32[8]{0:T(128)S(1)}, f32[8]{0:T(128)}, u32[]{:S(2)}) copy-start(f32[8]{0:T(128)} %yld.1) | copy-start | bytes 100
  24.1 7.6 %collective-permute-start.5 = (f32[25,8,128]{2,1,0:T(8,128)S(1)}, f32[25,8,128]{2,1,0:T(8,128)S(1)}, u32[]{:S(2)}, u32[]{:S(2)}) collective-permute-start(f32[25,8,128]{2,1,0:T(8,128)S(1)} %get-tuple-element.24), channel_id=1, source_target_pairs={{0,7},{1,2},{2,1},{3,4},{4,3},{5,6},{6,5},{7,0},{8,15},{9,10},{10,... | collective-permute-start | bytes 307208 | tf_op jit(solution)/shard_map/ppermute | solution.py:48
  48.8 1.2 %collective-permute-start.6 = (f32[8,128]{1,0:T(8,128)S(1)}, f32[8,128]{1,0:T(8,128)S(1)}, u32[]{:S(2)}, u32[]{:S(2)}) collective-permute-start(f32[8,128]{1,0:T(8,128)S(1)} %bitcast_select_fusion.1), channel_id=1, source_target_pairs={{0,32},{32,0},{64,96},{96,64},{128,160},{160,128},{192,224},{224,1... | collective-permute-start | bytes 12296 | tf_op jit(solution)/shard_map/ppermute | solution.py:43
  50.0 4.4 %collective-permute-start.7 = (f32[8,128]{1,0:T(8,128)S(1)}, f32[8,128]{1,0:T(8,128)S(1)}, u32[]{:S(2)}, u32[]{:S(2)}) collective-permute-start(f32[8,128]{1,0:T(8,128)S(1)} %bitcast_select_fusion), channel_id=1, source_target_pairs={{0,224},{32,64},{64,32},{96,128},{128,96},{160,192},{192,160},{224... | collective-permute-start | bytes 12296 | tf_op jit(solution)/shard_map/ppermute | solution.py:48
  54.4 5.1 %collective-permute-start.8 = (f32[1,128]{1,0:T(1,128)S(1)}, f32[1,128]{1,0:T(1,128)S(1)}, u32[]{:S(2)}, u32[]{:S(2)}) collective-permute-start(f32[1,128]{1,0:T(1,128)S(1)} %slice_add_fusion.1), channel_id=1, source_target_pairs={{0,128},{32,160},{64,192},{96,224},{128,0},{160,32},{192,64},{224,... | collective-permute-start | bytes 1544 | tf_op jit(solution)/shard_map/ppermute | solution.py:476
  59.6 3.7 %collective-permute-start.9 = (f32[2,8,128]{2,1,0:T(8,128)S(1)}, f32[2,8,128]{2,1,0:T(8,128)S(1)}, u32[]{:S(2)}, u32[]{:S(2)}) collective-permute-start(f32[2,8,128]{2,1,0:T(8,128)S(1)} %fusion.3), channel_id=1, source_target_pairs={{0,8},{8,0},{16,24},{24,16},{1,9},{9,1},{17,25},{25,17},{2,10},{10... | collective-permute-start | bytes 24584 | tf_op jit(solution)/shard_map/ppermute | solution.py:43
  63.4 4.9 %collective-permute-start.10 = (f32[2,8,128]{2,1,0:T(8,128)S(1)}, f32[2,8,128]{2,1,0:T(8,128)S(1)}, u32[]{:S(2)}, u32[]{:S(2)}) collective-permute-start(f32[2,8,128]{2,1,0:T(8,128)S(1)} %fusion.2), channel_id=1, source_target_pairs={{0,24},{8,16},{16,8},{24,0},{1,25},{9,17},{17,9},{25,1},{2,26},{10... | collective-permute-start | bytes 24584 | tf_op jit(solution)/shard_map/ppermute | solution.py:48
  68.3 3.7 %collective-permute-start.11 = (f32[2,8,128]{2,1,0:T(8,128)S(1)}, f32[2,8,128]{2,1,0:T(8,128)S(1)}, u32[]{:S(2)}, u32[]{:S(2)}) collective-permute-start(f32[2,8,128]{2,1,0:T(8,128)S(1)} %get-tuple-element.33), channel_id=1, source_target_pairs={{0,1},{1,0},{2,3},{3,2},{4,5},{5,4},{6,7},{7,6},{8,9},{9,8},{10,11... | collective-permute-start | bytes 24584 | tf_op jit(solution)/shard_map/ppermute | solution.py:43
  72.1 4.9 %collective-permute-start.12 = (f32[2,8,128]{2,1,0:T(8,128)S(1)}, f32[2,8,128]{2,1,0:T(8,128)S(1)}, u32[]{:S(2)}, u32[]{:S(2)}) collective-permute-start(f32[2,8,128]{2,1,0:T(8,128)S(1)} %broadcast_select_fusion), channel_id=1, source_target_pairs={{0,7},{1,2},{2,1},{3,4},{4,3},{5,6},{6,5},{7,0},{8,15},{9,10},{10,... | collective-permute-start | bytes 24584 | tf_op jit(solution)/shard_map/ppermute | solution.py:48
  77.0 7.5 %collective-permute-start.13 = (f32[1,128]{1,0:T(1,128)S(1)}, f32[1,128]{1,0:T(1,128)S(1)}, u32[]{:S(2)}, u32[]{:S(2)}) collective-permute-start(f32[1,128]{1,0:T(1,128)S(1)} %fusion.9), channel_id=1, source_target_pairs={{0,4},{1,5},{2,6},{3,7},{4,0},{5,1},{6,2},{7,3},{8,12},{9,13},{10,... | collective-permute-start | bytes 1544 | tf_op jit(solution)/shard_map/ppermute | solution.py:476

commit v2 on v1

v2 whole, which is shorter than its diff:
```python
import functools

import jax
import jax.numpy as jnp
from jax import lax
from jax.experimental import pallas as pl
from jax.experimental.pallas import tpu as pltpu
from jax.sharding import PartitionSpec as P

F32 = jnp.float32
BLOCK = 4
AX = ("gx", "gy", "gz")
NX, NY, NZ = 16, 32, 128
VMEM = pl.BlockSpec(memory_space=pltpu.VMEM)
SMEM = pl.BlockSpec(memory_space=pltpu.SMEM)


def sds(*shape):
    return jax.ShapeDtypeStruct(shape, F32)


def position(axis):
    index = lax.axis_index(axis)
    return lax.rem(index, 2) == 0, index > 0, index < lax.axis_size(axis) - 1


def lanes(rows=8, width=128):
    return lax.broadcasted_iota(jnp.int32, (rows, width), 1)


def subs(rows=8, width=128):
    return lax.broadcasted_iota(jnp.int32, (rows, width), 0)


def roll(value, shift, axis):
    size = value.shape[axis]
    shift = shift % size
    return pltpu.roll(value, shift, axis) if shift else value


def pair_a(value, axis):
    count = lax.axis_size(axis)
    return lax.ppermute(value, axis, [(i, i ^ 1) for i in range(count)])


def pair_b(value, axis):
    count = lax.axis_size(axis)
    return lax.ppermute(
        value, axis, [(i, (i + 1) % count if i % 2 else (i - 1) % count) for i in range(count)]
    )


def params():
    return pltpu.CompilerParams(vmem_limit_bytes=40 << 20)


def cost(flops):
    return pl.CostEstimate(flops=flops, bytes_accessed=1 << 20, transcendentals=0)


def pack_x(vel, forc, phase, send_a, send_b):
    even, _, _ = position("gx")
    for out, first in ((send_a, jnp.where(even, 1, 0)), (send_b, jnp.where(even, 0, 1))):
        for c in range(3):
            for i in range(4):
                out[4 * c + i] = vel[c, 12 * first + i]
            for i in range(2):
                out[12 + 2 * c + i] = forc[c, 14 * first + i]
        out[18, 0:8] = phase[3 * first]


def halo(pair, axis, index):
    even, has_lo, has_hi = position(axis)
    a, b = pair[0][index], pair[1][index]
    lo = jnp.where(has_lo, jnp.where(even, b, a), 0.0)
    hi = jnp.where(has_hi, jnp.where(even, a, b), 0.0)
    return lo, hi


def tile_of(own, c, plane, o, width, rx, base, ry):
    rows = slice(8 * o, 8 * o + 8)
    if o == 4:
        sub = subs()
        if width == 4:
            lo, hi = halo(ry, "gy", c * 12 + plane % 12)
            if plane < 12:
                return jnp.where(sub < 4, hi, roll(lo, 4, 0))
            return jnp.where(sub < 4, roll(hi, 4, 0), lo)
        lo, hi = halo(ry, "gy", 36 + c * 5 + plane % 5)
        k = plane // 5
        return jnp.where(sub < 4, roll(hi, -2 * k, 0), roll(lo, 6 - 2 * k, 0))
    if plane < width:
        return halo(rx, "gx", (base + width * c + plane, rows))[0]
    if plane >= NX + width:
        return halo(rx, "gx", (base + width * c + plane - NX - width, rows))[1]
    return own[c, plane - width, rows]


def phase_rows(phase, rx, b):
    if b == 0:
        return halo(rx, "gx", (18, slice(0, 8)))[0]
    if b == 5:
        return halo(rx, "gx", (18, slice(0, 8)))[1]
    return phase[b - 1]


def phase_tiles(phase, rx, ry):
    lo, hi = halo(ry, "gy", 51)
    sub = subs()
    tiles = []
    for b in range(6):
        tiles.append(phase_rows(phase, rx, b))
        outer = jnp.where(sub == 0, hi[b : b + 1], jnp.where(sub == 1, lo[b : b + 1], 0.0))
        tiles.append(outer)
    return tiles


def pack_y(vel, forc, phase, rx_a, rx_b, send_a, send_b):
    rx = (rx_a, rx_b)
    even, _, _ = position("gy")
    sub = subs()

    def put(index, lo, hi):
        send_a[index] = jnp.where(even, hi, lo)
        send_b[index] = jnp.where(even, lo, hi)

    def u(c, p, o):
        return tile_of(vel, c, p, o, 4, rx, 0, None)

    def f(c, p, o):
        return tile_of(forc, c, p, o, 2, rx, 12, None)

    for c in range(3):
        for p in range(12):
            lo = jnp.where(sub < 4, u(c, p, 0), roll(u(c, p + 12, 0), 4, 0))
            hi = jnp.where(sub < 4, roll(u(c, p, 3), 4, 0), u(c, p + 12, 3))
            put(c * 12 + p, lo, hi)
        for g in range(5):
            lo = f(c, g, 0)
            hi = roll(f(c, g, 3), 2, 0)
            for k in range(1, 4):
                here = (sub >> 1) == k
                lo = jnp.where(here, roll(f(c, g + 5 * k, 0), 2 * k, 0), lo)
                hi = jnp.where(here, roll(f(c, g + 5 * k, 3), 2 * k + 2, 0), hi)
            put(36 + c * 5 + g, lo, hi)
    lo = jnp.zeros((8, 128), F32)
    hi = lo
    for b in range(6):
        tile = phase_rows(phase, rx, b)
        lo = jnp.where(sub == b, tile[0:1], lo)
        hi = jnp.where(sub == b, tile[7:8], hi)
    put(51, lo, hi)


def slots():
    lane = lanes()
    return lane >> 5, lane & 31


def edge_tile(tile, i, low_plane, planes):
    slot, pos = slots()
    value = jnp.zeros((8, 128), F32)
    for g in range(4):
        plane = 6 * g + i - low_plane
        if not 0 <= plane < planes:
            continue
        own = tile(plane)
        here = slot == g
        value = jnp.where(here & (pos < 16), roll(own, 32 * g + 4, 1), value)
        value = jnp.where(here & (pos >= 16), roll(own, 32 * g + 28, 1), value)
    return jnp.where(((pos >= 4) & (pos < 12)) | ((pos >= 20) & (pos < 28)), value, 0.0)


def edge_own(vel, forc, rx_a, rx_b, eu, ef):
    rx = (rx_a, rx_b)
    for c in range(3):
        for i in range(6):
            for o in range(4):
                rows = slice(8 * o, 8 * o + 8)
                eu[c, i, rows] = edge_tile(lambda p: tile_of(vel, c, p, o, 4, rx, 0, None), i, 0, 24)
                ef[c, i, rows] = edge_tile(lambda p: tile_of(forc, c, p, o, 2, rx, 12, None), i, 2, 20)


def pack_z(phase, rx_a, rx_b, ry_a, ry_b, eu, ef, send_a, send_b, eu4, ef4, tiles):
    rx, ry = (rx_a, rx_b), (ry_a, ry_b)
    even, _, _ = position("gz")

    def put(index, lo, hi):
        send_a[index] = jnp.where(even, hi, lo)
        send_b[index] = jnp.where(even, lo, hi)

    lane = lanes()
    place = (lane & 31) >> 2
    for c in range(3):
        for i in range(6):
            eu4[c, i] = edge_tile(lambda p: tile_of(None, c, p, 4, 4, rx, 0, ry), i, 0, 24)
            ef4[c, i] = edge_tile(lambda p: tile_of(None, c, p, 4, 2, rx, 12, ry), i, 2, 20)
    for base, own, own4 in ((0, eu, eu4), (12, ef, ef4)):
        for w in range(12):
            lo = jnp.zeros((8, 128), F32)
            hi = lo
            for k in range(min(8, 90 - 8 * w)):
                n = 8 * w + k
                c, i, o = n // 30, n // 5 % 6, n % 5
                tile = own4[c, i] if o == 4 else own[c, i, 8 * o : 8 * o + 8]
                lo = jnp.where(place == k, roll(tile, 4 * k - 4, 1), lo)
                hi = jnp.where(place == k, roll(tile, 4 * k - 24, 1), hi)
            put(base + w, lo, hi)
    lo = jnp.zeros((8, 128), F32)
    hi = lo
    for j, tile in enumerate(phase_tiles(phase, rx, ry)):
        tiles[j] = tile
        lo = jnp.where(lane == j, roll(tile, j, 1), lo)
        hi = jnp.where(lane == j, roll(tile, j - 31, 1), hi)
    put(24, lo, hi)


def exact_dot(a, b):
    return jnp.dot(a, b, preferred_element_type=F32, precision=lax.Precision.HIGHEST)


def four(a, b, c, d):
    return (a + 3.0 * b + 3.0 * c + d) * 0.125


def put_rows(ref, index, o, value):
    ref[index + (slice(8 + 8 * o, 16 + 8 * o),)] = value
    if o == 0:
        ref[index + (slice(48, 56),)] = value
    if o == 4:
        ref[index + (slice(0, 8),)] = value


def tables(tiles, wide, pre, yld, creep, limit):
    block = lax.broadcasted_iota(jnp.int32, (128, 128), 0)
    spread = jnp.dot(
        jnp.concatenate(tiles, axis=0), (wide == block).astype(F32), preferred_element_type=F32
    )
    row = lax.broadcasted_iota(jnp.int32, (40, 16), 0)
    by = lax.broadcasted_iota(jnp.int32, (40, 16), 1)
    tall = (jnp.where(row < 32, row >> 2, jnp.where(row < 36, 8, 9)) == by).astype(F32)
    for b in range(6):
        phase = jnp.dot(tall, spread[16 * b : 16 * b + 16], preferred_element_type=F32)
        first = jnp.full(phase.shape, pre[0], F32)
        second = jnp.full(phase.shape, yld[0], F32)
        for k in range(1, 8):
            here = phase == float(k)
            first = jnp.where(here, pre[k], first)
            second = jnp.where(here, yld[k], second)
        creep[b] = first
        limit[b] = 0.5 * second


def viscosity_tile(u, creep, limit):
    d = []
    for c in range(3):
        mid = u(c, 0, 0)
        d.append((u(c, 1, 0) - u(c, -1, 0), u(c, 0, 1) - u(c, 0, -1), roll(mid, 127, 1) - roll(mid, 1, 1)))
    a01, a02, a12 = d[0][1] + d[1][0], d[0][2] + d[2][0], d[1][2] + d[2][1]
    own = d[0][0] * d[0][0] + d[1][1] * d[1][1] + d[2][2] * d[2][2]
    off = a01 * a01 + a02 * a02 + a12 * a12
    invariant = 1.0 + (own * 0.125 + off * 0.0625)
    return jnp.minimum(creep * jnp.exp(jnp.log(invariant) * (-1.0 / 3.0)), limit * lax.rsqrt(invariant))


def around(ref, index, o):
    head, p = index[:-1], index[-1]
    mid = ref[head + (p, slice(8 + 8 * o, 16 + 8 * o))]
    return mid, (
        ref[head + (p + 1, slice(8 + 8 * o, 16 + 8 * o))],
        ref[head + (p - 1, slice(8 + 8 * o, 16 + 8 * o))],
        ref[head + (p, slice(9 + 8 * o, 17 + 8 * o))],
        ref[head + (p, slice(7 + 8 * o, 15 + 8 * o))],
        roll(mid, 127, 1),
        roll(mid, 1, 1),
    )


def faces(v_ref, vx, o):
    mid, near = around(v_ref, (vx,), o)
    f = [mid + value for value in near]
    return mid, f, (f[0] + f[1]) + (f[2] + f[3]) + (f[4] + f[5])


def weighted(ref, index, o, f):
    mid, near = around(ref, index, o)
    total = f[0] * near[0]
    for k in range(1, 6):
        total = total + f[k] * near[k]
    return mid, total


def relax(mid_v, diag):
    return jnp.where(mid_v > 0.0, 0.8 / diag, 0.0)


def flags(axis):
    return tuple(flag.astype(F32) for flag in position(axis)[1:])


def main_work(
    vel, forc, phase_ref, rx_a, rx_b, ry_a, ry_b, pre, yld,
    v_ref, u2, residual, square,
    u_ref, f_ref, creep, limit, u1,
):
    rx, ry = (rx_a, rx_b), (ry_a, ry_b)
    lo_x, hi_x = flags("gx")
    lo_y, hi_y = flags("gy")
    for c in range(3):
        for p in range(24):
            for o in range(5):
                put_rows(u_ref, (c, p), o, tile_of(vel, c, p, o, 4, rx, 0, ry))
        for p in range(20):
            for o in range(5):
                f_ref[c, p, 8 * o : 8 * o + 8] = tile_of(forc, c, p, o, 2, rx, 12, ry)
    wide = lax.broadcasted_iota(jnp.int32, (128, 128), 1) >> 2
    tables(phase_tiles(phase_ref, rx, ry), wide, pre, yld, creep, limit)
    mask_y = jnp.where(subs() < 4, hi_y, lo_y)

    def viscosity(vx, _):
        mask_x = jnp.where(vx < 3, lo_x, jnp.where(vx >= 19, hi_x, 1.0))
        bx = (vx + 1) >> 2
        for o in range(5):
            value = viscosity_tile(
                lambda c, dx, dy: u_ref[c, vx + 1 + dx, 8 + 8 * o + dy : 16 + 8 * o + dy],
                creep[bx, 8 * o : 8 * o + 8], limit[bx, 8 * o : 8 * o + 8],
            )
            put_rows(v_ref, (vx,), o, value * (mask_y * mask_x if o == 4 else mask_x))
        return 0

    lax.fori_loop(0, 22, viscosity, 0)

    def sweep(source, target, first, first_u):
        def body(x, _):
            for o in range(5):
                mid_v, f, diag = faces(v_ref, x + first, o)
                rate = relax(mid_v, diag)
                for c in range(3):
                    mid, total = weighted(source, (c, x + first_u), o, f)
                    force = f_ref[c, x + first - 1, 8 * o : 8 * o + 8]
                    put_rows(target, (c, x), o, 0.2 * mid + rate * (2.0 * force + total))
            return 0

        return body

    lax.fori_loop(0, 20, sweep(u_ref, u1, 1, 2), 0)
    lax.fori_loop(0, 18, sweep(u1, u2, 2, 1), 0)

    def last(x, acc):
        for o in range(4):
            _, f, diag = faces(v_ref, x + 3, o)
            for c in range(3):
                mid, total = weighted(u2, (c, x + 1), o, f)
                value = f_ref[c, x + 2, 8 * o : 8 * o + 8] + 0.5 * (total - diag * mid)
                residual[c, x, 8 * o : 8 * o + 8] = value
                acc = acc + value * value
        return acc

    acc = lax.fori_loop(0, NX, last, jnp.zeros((8, 128), F32))
    lane = lanes()
    square[...] = jnp.where((lane >= 4) & (lane < 124), acc, 0.0)


def put_edge(ref, index, i, o, value):
    put_rows(ref, index + (i + 1,), o, value)


def wrap_planes(ref, lead):
    for index in lead:
        for r in range(7):
            rows = slice(8 * r, 8 * r + 8)
            ref[index + (0, rows)] = roll(ref[index + (6, rows)], 32, 1)
            ref[index + (7, rows)] = roll(ref[index + (1, rows)], -32, 1)


def edge_work(
    rz_a, rz_b, eu, ef, eu4, ef4, phases, square, pre, yld,
    v_out, u_out, r_out, total_out,
    u_ref, f_ref, creep, limit, creep_e, limit_e, v_ref, u1, u2,
):
    rz = (rz_a, rz_b)
    lo_x, hi_x = flags("gx")
    lo_y, hi_y = flags("gy")
    lo_z, hi_z = flags("gz")
    lane = lanes()
    slot, pos = slots()
    lead = ((0,), (1,), (2,))
    for base, own, own4 in ((0, eu, eu4), (12, ef, ef4)):
        for w in range(12):
            lo, hi = halo(rz, "gz", base + w)
            for k in range(min(8, 90 - 8 * w)):
                n = 8 * w + k
                c, i, o = n // 30, n // 5 % 6, n % 5
                tile = own4[c, i] if o == 4 else own[c, i, 8 * o : 8 * o + 8]
                tile = jnp.where(pos < 4, roll(lo, -4 * k, 1), tile)
                tile = jnp.where(pos >= 28, roll(hi, 28 - 4 * k, 1), tile)
                if base == 0:
                    put_edge(u_ref, (c,), i, o, tile)
                else:
                    f_ref[c, i, 8 * o : 8 * o + 8] = tile
    wrap_planes(u_ref, lead)

    lo, hi = halo(rz, "gz", 24)
    tiles = []
    for j in range(12):
        tile = jnp.where(lane == 32, roll(hi, 32 - j, 1), phases[j])
        tiles.append(jnp.where(lane == 33, roll(lo, 33 - j, 1), tile))
    at = lax.broadcasted_iota(jnp.int32, (128, 128), 1) & 31
    wide = jnp.where(at < 4, 33, jnp.where(at < 12, (at - 4) >> 2, jnp.where(at < 20, 127, 25 + (at >> 2))))
    tables(tiles, wide, pre, yld, creep, limit)
    for i in range(6):
        first, second = creep[i // 4], limit[i // 4]
        slot40 = lanes(40) >> 5
        for g in range(1, 4):
            b = (6 * g + i) // 4
            first = jnp.where(slot40 == g, creep[b], first)
            second = jnp.where(slot40 == g, limit[b], second)
        creep_e[i] = first
        limit_e[i] = second

    mask_z = jnp.where(pos < 4, lo_z, jnp.where(pos >= 28, hi_z, jnp.where((pos < 12) | (pos >= 20), 1.0, 0.0)))
    mask_y = jnp.where(subs() < 4, hi_y, lo_y)

    def viscosity(i, _):
        px = 6 * slot + i
        mask = mask_z * jnp.where(px < 4, lo_x, jnp.where(px >= 20, hi_x, 1.0))
        for o in range(5):
            value = viscosity_tile(
                lambda c, dx, dy: u_ref[c, i + 1 + dx, 8 + 8 * o + dy : 16 + 8 * o + dy],
                creep_e[i, 8 * o : 8 * o + 8], limit_e[i, 8 * o : 8 * o + 8],
            )
            value = value * (mask * mask_y if o == 4 else mask)
            put_edge(v_ref, (), i, o, value)
            v_out[i, 8 * o : 8 * o + 8] = value
        return 0

    lax.fori_loop(0, 6, viscosity, 0)
    wrap_planes(v_ref, ((),))

    def sweep(source, target):
        def body(i, _):
            for o in range(5):
                mid_v, f, diag = faces(v_ref, i + 1, o)
                rate = relax(mid_v, diag)
                for c in range(3):
                    mid, total = weighted(source, (c, i + 1), o, f)
                    force = f_ref[c, i, 8 * o : 8 * o + 8]
                    put_edge(target, (c,), i, o, 0.2 * mid + rate * (2.0 * force + total))
            return 0

        lax.fori_loop(0, 6, body, 0)
        wrap_planes(target, lead)

    sweep(u_ref, u1)
    sweep(u1, u2)

    def last(i, acc):
        px = 6 * slot + i
        count = (px >= 4) & (px < 20) & (((pos >= 4) & (pos < 8)) | ((pos >= 24) & (pos < 28)))
        for o in range(4):
            _, f, diag = faces(v_ref, i + 1, o)
            for c in range(3):
                mid, total = weighted(u2, (c, i + 1), o, f)
                value = f_ref[c, i, 8 * o : 8 * o + 8] + 0.5 * (total - diag * mid)
                r_out[c, i, 8 * o : 8 * o + 8] = value
                u_out[c, i, 8 * o : 8 * o + 8] = mid
                acc = acc + jnp.where(count, value * value, 0.0)
        return acc

    acc = lax.fori_loop(0, 6, last, square[...])
    total = jnp.sum(jnp.sum(acc, axis=1, keepdims=True), axis=0, keepdims=True)
    total_out[...] = jnp.broadcast_to(total, (1, 128))


def band(rows, row_z, col_m):
    row = row_z(lax.broadcasted_iota(jnp.int32, (rows, 128), 0))
    col = col_m(lax.broadcasted_iota(jnp.int32, (rows, 128), 1))
    at = row - 2 * col + 1
    return jnp.where((at == 0) | (at == 3), 0.125, jnp.where((at == 1) | (at == 2), 0.375, 0.0)).astype(F32)


def merge(own, edge, g):
    lane = lanes()
    value = jnp.where(lane < 4, roll(edge, -32 * g - 4, 1), own)
    return jnp.where(lane >= 124, roll(edge, 100 - 32 * g, 1), value)


def collect(
    v_ref, u2, residual_in, ve, ue, re,
    smoothed, visc_out, one_out, two_out, residual, partial,
    v_m, v_s, w_m, w_s, y1, c1, t2, t3,
):
    lo_x, hi_x = flags("gx")
    lo_y, hi_y = flags("gy")
    lo_z, hi_z = flags("gz")
    lane = lanes()
    for vx in range(22):
        g, i = (vx + 1) // 6, (vx + 1) % 6
        for o in range(5):
            edge = ve[i, 8 * o : 8 * o + 8]
            value = merge(v_ref[vx, 8 + 8 * o : 16 + 8 * o], edge, g)
            put_rows(v_m, (vx,), o, value)
            side = jnp.where(lane < 4, roll(edge, -28 - 32 * g, 1), 0.0)
            put_rows(v_s, (vx,), o, jnp.where(lane >= 124, roll(edge, 124 - 32 * g, 1), side))
            if 3 <= vx < 19 and o < 4:
                visc_out[vx - 3, 8 * o : 8 * o + 8] = value
    for x in range(NX):
        g, i = (x + 4) // 6, (x + 4) % 6
        for c in range(3):
            for o in range(4):
                rows = slice(8 * o, 8 * o + 8)
                smoothed[c, x, rows] = merge(u2[c, x + 1, 8 + 8 * o : 16 + 8 * o], ue[c, i, rows], g)
                residual[c, x, rows] = merge(residual_in[c, x, rows], re[c, i, rows], g)

    def coarse_x(k, _):
        w_m[k] = four(v_m[2 * k], v_m[2 * k + 1], v_m[2 * k + 2], v_m[2 * k + 3])
        w_s[k] = four(v_s[2 * k], v_s[2 * k + 1], v_s[2 * k + 2], v_s[2 * k + 3])
        return 0

    lax.fori_loop(0, 10, coarse_x, 0)
    y1[...] = jnp.zeros(y1.shape, F32)
    for k in range(10):
        for ref, at in ((w_m, 0), (w_s, 128)):
            y1[k, 0:18, at : at + 128] = four(*(ref[k, pl.ds(5 + i, 18, stride=2)] for i in range(4)))
    band1 = band(256, lambda r: jnp.where(r < 192, r, r - 256), lambda m: jnp.where(m < 65, m, jnp.where(m == 65, -1, 1000)))
    coarse = exact_dot(y1[...].reshape(240, 256), band1).reshape(10, 24, 128)
    row24, lane24 = subs(24), lanes(24)
    mask_yz = jnp.where(row24 == 0, lo_y, jnp.where(row24 == 17, hi_y, 1.0)) * jnp.where(
        lane24 == 64, hi_z, jnp.where(lane24 == 65, lo_z, 1.0)
    )
    for k in range(10):
        mask = mask_yz * (lo_x if k == 0 else hi_x if k == 9 else 1.0)
        c1[k] = coarse[k] * mask
    for k in range(8):
        one_out[k] = c1[k + 1, 1:17, 0:64]
    rows = []
    for k in range(4):
        t2[...] = four(c1[2 * k], c1[2 * k + 1], c1[2 * k + 2], c1[2 * k + 3])
        rows.append(four(*(t2[pl.ds(i, 8, stride=2)] for i in range(4))))
    band2 = band(128, lambda r: jnp.where(r < 65, r, jnp.where(r == 65, -1, 100000)), lambda m: jnp.where(m < 32, m, 1000))
    coarse = exact_dot(jnp.concatenate(rows, axis=0), band2)
    planes = [coarse[8 * k : 8 * k + 8] for k in range(4)]
    for k in range(4):
        two_out[k] = planes[k][:, 0:32]
    thirds = (
        0.125 * planes[0],
        0.125 * (3.0 * planes[0] + 3.0 * planes[1] + planes[2]),
        0.125 * (planes[1] + 3.0 * planes[2] + 3.0 * planes[3]),
        0.125 * planes[3],
    )
    rows = []
    t3[...] = jnp.zeros(t3.shape, F32)
    for k in range(4):
        t3[4:12] = thirds[k]
        rows.append(four(*(t3[pl.ds(1 + i, 8, stride=2)] for i in range(4))))
    band3 = band(128, lambda r: jnp.where(r < 32, r, 100000), lambda m: jnp.where(m < 18, m - 1, 1000))
    coarse = exact_dot(jnp.concatenate(rows, axis=0), band3)
    for k in range(4):
        partial[k] = coarse[8 * k : 8 * k + 8]


def with_sum(tile, total):
    row = lax.broadcasted_iota(jnp.int32, tile.shape, tile.ndim - 2)
    return jnp.where(row == 7, total, tile)


def finish(partial, total):
    even, has_lo, has_hi = position("gx")
    got_a = pair_a(with_sum(jnp.where(even, partial[3], partial[0]), total), "gx")
    total = total + got_a[7:8]
    got_b = pair_b(with_sum(jnp.where(even, partial[0], partial[3]), total), "gx")
    total = total + got_b[7:8]
    lo, hi = jnp.where(even, got_b, got_a), jnp.where(even, got_a, got_b)
    inner = jnp.stack(
        [partial[1] + jnp.where(has_lo, lo, 0.0), partial[2] + jnp.where(has_hi, hi, 0.0)]
    )
    even, has_lo, has_hi = position("gy")
    got_a = pair_a(with_sum(inner, total), "gy")
    total = total + got_a[0, 7:8]
    got_b = pair_b(with_sum(inner, total), "gy")
    total = total + got_b[0, 7:8]
    lo, hi = jnp.where(even, got_b, got_a), jnp.where(even, got_a, got_b)
    row = lax.broadcasted_iota(jnp.int32, inner.shape, 1)
    inner = (
        inner
        + jnp.where((row == 1) & has_lo, jnp.roll(lo, -4, 1), 0.0)
        + jnp.where((row == 4) & has_hi, jnp.roll(hi, 4, 1), 0.0)
    )
    even, has_lo, has_hi = position("gz")
    got_a = pair_a(with_sum(inner, total), "gz")
    total = total + got_a[0, 7:8]
    got_b = pair_b(with_sum(inner, total), "gz")
    total = total + got_b[0, 7:8]
    lo, hi = jnp.where(even, got_b, got_a), jnp.where(even, got_a, got_b)
    three = inner[:, 1:5, 1:17]
    z = lax.broadcasted_iota(jnp.int32, three.shape, 2)
    three = (
        three
        + jnp.where((z == 0) & has_lo, lo[:, 1:5, 17:18], 0.0)
        + jnp.where((z == 15) & has_hi, hi[:, 1:5, 0:1], 0.0)
    )
    return total[0, 0], three


def far(axis, total):
    count = lax.axis_size(axis)
    if count == 4:
        return jnp.zeros_like(total)
    return lax.ppermute(total, axis, [(i, (i + count // 2) % count) for i in range(count)])


def pack(kernel, shape, name, *args):
    return pl.pallas_call(
        kernel, out_shape=[sds(*shape)] * 2, in_specs=[VMEM] * len(args), out_specs=[VMEM] * 2,
        compiler_params=params(), name=name,
    )(*args)


def per_device(velocity, forcing, phase_block, prefactor, yield_stress):
    phase = jnp.pad(phase_block.astype(F32), ((0, 0), (0, 0), (0, 96)))
    own = (velocity, forcing, phase)
    send_a, send_b = pack(pack_x, (19, 32, 128), "pack_x", *own)
    rx = (pair_a(send_a, "gx"), pair_b(send_b, "gx"))
    send_a, send_b = pack(pack_y, (52, 8, 128), "pack_y", *own, *rx)
    ry = (pair_a(send_a, "gy"), pair_b(send_b, "gy"))
    eu, ef = pl.pallas_call(
        edge_own, out_shape=[sds(3, 6, 32, 128)] * 2, in_specs=[VMEM] * 4, out_specs=[VMEM] * 2,
        compiler_params=params(), cost_estimate=cost(3 << 23), name="edge_own",
    )(velocity, forcing, *rx)
    send_a, send_b, eu4, ef4, tiles = pl.pallas_call(
        pack_z, out_shape=[sds(25, 8, 128)] * 2 + [sds(3, 6, 8, 128)] * 2 + [sds(12, 8, 128)],
        in_specs=[VMEM] * 7, out_specs=[VMEM] * 5, compiler_params=params(), name="pack_z",
    )(phase, *rx, *ry, eu, ef)
    rz = (pair_a(send_a, "gz"), pair_b(send_b, "gz"))
    v, u2, res, square = pl.pallas_call(
        main_work,
        out_shape=[sds(22, 56, 128), sds(3, 18, 56, 128), sds(3, NX, NY, NZ), sds(8, 128)],
        in_specs=[VMEM] * 7 + [SMEM] * 2, out_specs=[VMEM] * 4,
        scratch_shapes=[
            pltpu.VMEM((3, 24, 56, 128), F32), pltpu.VMEM((3, 20, 40, 128), F32),
            pltpu.VMEM((6, 40, 128), F32), pltpu.VMEM((6, 40, 128), F32), pltpu.VMEM((3, 20, 56, 128), F32),
        ],
        compiler_params=params(), cost_estimate=cost(1 << 25), name="main_work",
    )(*own, *rx, *ry, prefactor, yield_stress)
    ve, ue, re, total = pl.pallas_call(
        edge_work,
        out_shape=[sds(6, 40, 128), sds(3, 6, 32, 128), sds(3, 6, 32, 128), sds(1, 128)],
        in_specs=[VMEM] * 8 + [SMEM] * 2, out_specs=[VMEM] * 4,
        scratch_shapes=[
            pltpu.VMEM((3, 8, 56, 128), F32), pltpu.VMEM((3, 6, 40, 128), F32),
            *[pltpu.VMEM((6, 40, 128), F32)] * 4,
            pltpu.VMEM((8, 56, 128), F32), pltpu.VMEM((3, 8, 56, 128), F32), pltpu.VMEM((3, 8, 56, 128), F32),
        ],
        compiler_params=params(), cost_estimate=cost(1 << 23), name="edge_work",
    )(*rz, eu, ef, eu4, ef4, tiles, square, prefactor, yield_stress)
    total = total + far("gx", total)
    total = total + far("gz", total)
    smoothed, visc, one, two, residual, partial = pl.pallas_call(
        collect,
        out_shape=[
            sds(3, NX, NY, NZ), sds(NX, NY, NZ), sds(8, 16, 64), sds(4, 8, 32), sds(3, NX, NY, NZ), sds(4, 8, 128),
        ],
        in_specs=[VMEM] * 6, out_specs=[VMEM] * 6,
        scratch_shapes=[
            pltpu.VMEM((22, 56, 128), F32), pltpu.VMEM((22, 56, 128), F32),
            pltpu.VMEM((10, 56, 128), F32), pltpu.VMEM((10, 56, 128), F32), pltpu.VMEM((10, 24, 256), F32),
            pltpu.VMEM((10, 24, 128), F32), pltpu.VMEM((24, 128), F32), pltpu.VMEM((24, 128), F32),
        ],
        compiler_params=params(), cost_estimate=cost(1 << 23), name="collect",
    )(v, u2, res, ve, ue, re)
    total, three = finish(partial, total)
    cells = 3.0 * NX * NY * NZ
    for axis in AX:
        cells = cells * lax.axis_size(axis)
    return smoothed, visc, one, two, three, residual, jnp.sqrt(total / cells)


def solution(mesh):
    field, cell = P(None, *AX), P(*AX)
    return jax.shard_map(
        per_device,
        mesh=mesh,
        in_specs=(field, field, cell, P(), P()),
        out_specs=(field, cell, cell, cell, cell, field, P()),
        check_vma=False,
    )
```

time: 85.9 us -> 81.1 us (0.944)
  waiting for transfers between devices: 34.8 us -> 27.7 us
  local copies, waits for them, and re-layouts: 2.3 us -> 5.95 us
  starting transfers between devices: 25.2 us -> 23.9 us
    unnamed x12 -> x20, local copies, waits for them, and re-layouts: 2.29 us -> 5.93 us
    ppermute x2, waiting for transfers between devices: 5.87 us -> 3.08 us  [far(): lax.ppermute(total, axis, [(i, (i + count // 2) % count) for i in range(c...]
    ppermute x6, waiting for transfers between devices: 13 us -> 10.5 us  [pair_a(): return lax.ppermute(value, axis, [(i, i ^ 1) for i in range(count)])]
    pallas_call x3 -> x2, Pallas kernels: 2.35 us -> 0.13 us  [pack(): pl.pallas_call(kernel, out_shape=[sds(*shape)] * 2, in_specs=[VMEM] * len...]
    pallas_call x1 -> x5, Pallas kernels: 17 us -> 19 us  [the longest x1 10 us: per_device(): pl.pallas_call(main_work, out_shape=[sds(22, 56, 128), sds(3, 18, 56, 128...]
    ppermute x6, waiting for transfers between devices: 16 us -> 14.1 us  [pair_b(): lax.ppermute(value, axis, [(i, (i + 1) % count if i % 2 else (i - 1) % co...]
    ppermute x2, starting transfers between devices: 5.84 us -> 4.13 us  [far(): lax.ppermute(total, axis, [(i, (i + count // 2) % count) for i in range(c...]
    ppermute x6, starting transfers between devices: 3.07 us -> 4.38 us  [pair_a(): return lax.ppermute(value, axis, [(i, i ^ 1) for i in range(count)])]
  transfers between devices with their start and end apart: 14 -> 14, of which waited for: 12 -> 11; matrix products, arithmetic and copies ran while one was open for 1% -> 0% of each run, Pallas kernels for 0% -> 17%
where the time goes in v2:
time: 81.1 us; the launch traced here: 80.8 us
  waiting for transfers between devices  27.7 us (34%)
  starting transfers between devices  23.9 us (29%)
  Pallas kernels  19.2 us (24%)
  local copies, waits for them, and re-layouts  5.95 us (7%)
  other arithmetic  2.08 us (3%)
  between operations  1.95 us (2%)
    ppermute x6, starting transfers between devices, pair_b(): lax.ppermute(value, axis, [(i, (i + 1) % count if i % 2 else (i - 1) % co...  15.4 us
    ppermute x6, waiting for transfers between devices, pair_b(): lax.ppermute(value, axis, [(i, (i + 1) % count if i % 2 else (i - 1) % co...  14.1 us
    ppermute x6, waiting for transfers between devices, pair_a(): return lax.ppermute(value, axis, [(i, i ^ 1) for i in range(count)])  10.5 us
    pallas_call x1, Pallas kernels, per_device(): pl.pallas_call(main_work, out_shape=[sds(22, 56, 128), sds(3, 18, 56, 128...  10 us
    unnamed x20, local copies, waits for them, and re-layouts  5.93 us
    ppermute x6, starting transfers between devices, pair_a(): return lax.ppermute(value, axis, [(i, i ^ 1) for i in range(count)])  4.38 us
    pallas_call x1, Pallas kernels, per_device(): pl.pallas_call(edge_work, out_shape=[sds(6, 40, 128), sds(3, 6, 32, 128),...  4.24 us
    ppermute x2, starting transfers between devices, far(): lax.ppermute(total, axis, [(i, (i + count // 2) % count) for i in range(c...  4.13 us
  transfers between devices with their start and end apart: 14, of which 11 were waited for; matrix products, arithmetic and copies ran while one was open for 0% of the time, Pallas kernels for 17%

profile of v2, /device:TPU:24, one launch (start us, length us, event | category | flops | bytes accessed | tf_op | source)
XLA Modules:
  0.0 80.8 jit_solution(13002556923633893472)
XLA Ops:
  0.6 0.7 convert_element_type.5
  1.4 0.0 copy-start
  1.4 1.1 %copy-done = f32[3,16,32,128]{3,2,1,0:T(8,128)S(1)} copy-done((f32[3,16,32,128]{3,2,1,0:T(8,128)S(1)}, f32[3,16,32,128]{3,2,1,0:T(8,128)}, u32[]{:S(2)}) %copy-start) | copy-done | bytes 786456
  2.5 0.0 copy-start.2
  2.5 1.1 %copy-done.2 = f32[3,16,32,128]{3,2,1,0:T(8,128)S(1)} copy-done((f32[3,16,32,128]{3,2,1,0:T(8,128)S(1)}, f32[3,16,32,128]{3,2,1,0:T(8,128)}, u32[]{:S(2)}) %copy-start.2) | copy-done | bytes 786456
  3.6 0.0 copy-start.1
  3.6 0.0 copy-start.3
  3.7 0.1 collective-permute-start
  3.8 2.9 %collective-permute-start.1 = (f32[19,32,128]{2,1,0:T(8,128)S(1)}, f32[19,32,128]{2,1,0:T(8,128)S(1)}, u32[]{:S(2)}, u32[]{:S(2)}) collective-permute-start(f32[19,32,128]{2,1,0:T(8,128)S(1)} %get-tuple-element.33), channel_id=1, source_target_pairs={{0,224},{32,64},{64,32},{96,128},{128,96},{160,192},{192,160},{224... | collective-permute-start | bytes 933896 | tf_op jit(solution)/shard_map/ppermute | solution.py:48
  6.6 0.0 collective-permute-done.rx_a
  6.6 4.8 %collective-permute-done.1.rx_b = f32[19,32,128]{2,1,0:T(8,128)S(1)} collective-permute-done((f32[19,32,128]{2,1,0:T(8,128)S(1)}, f32[19,32,128]{2,1,0:T(8,128)S(1)}, u32[]{:S(2)}, u32[]{:S(2)}) %collective-permute-start.1) | collective-permute-done | bytes 311328 | tf_op jit(solution)/shard_map/ppermute | solution.py:48
  11.4 0.1 pack_y.1
  11.5 0.8 %collective-permute-start.2 = (f32[52,8,128]{2,1,0:T(8,128)S(1)}, f32[52,8,128]{2,1,0:T(8,128)S(1)}, u32[]{:S(2)}, u32[]{:S(2)}) collective-permute-start(f32[52,8,128]{2,1,0:T(8,128)S(1)} %get-tuple-element.34), channel_id=1, source_target_pairs={{0,8},{8,0},{16,24},{24,16},{1,9},{9,1},{17,25},{25,17},{2,10},{10... | collective-permute-start | bytes 638984 | tf_op jit(solution)/shard_map/ppermute | solution.py:43
  12.3 1.3 %collective-permute-start.3 = (f32[52,8,128]{2,1,0:T(8,128)S(1)}, f32[52,8,128]{2,1,0:T(8,128)S(1)}, u32[]{:S(2)}, u32[]{:S(2)}) collective-permute-start(f32[52,8,128]{2,1,0:T(8,128)S(1)} %get-tuple-element.35), channel_id=1, source_target_pairs={{0,24},{8,16},{16,8},{24,0},{1,25},{9,17},{17,9},{25,1},{2,26},{10... | collective-permute-start | bytes 638984 | tf_op jit(solution)/shard_map/ppermute | solution.py:48
  13.6 0.0 copy-done.1
  13.6 0.0 copy-done.3
  13.6 0.0 copy-start.8
  13.6 0.0 copy-start.9
  13.6 1.2 %edge_own.1 = (f32[3,6,32,128]{3,2,1,0:T(8,128)S(1)}, f32[3,6,32,128]{3,2,1,0:T(8,128)S(1)}) custom-call(f32[3,16,32,128]{3,2,1,0:T(8,128)S(1)} %copy-done.1, f32[3,16,32,128]{3,2,1,0:T(8,128)S(1)} %copy-done.3, f32[19,32,128]{2,1,0:T(8,128)S(1)} %collective-permute-done.rx_a, f32[19,32,128]{2,1,0:T(8,128)S(1)} %collective-permute-done.1.rx_b), custom_call_target="tpu_custom_call" | custom-call | flops 25165824 | bytes 1048576 | tf_op jit(solution)/shard_map/edge_own/pallas_call | solution.py:626
  14.8 3.4 %collective-permute-done.2.ry_a = f32[52,8,128]{2,1,0:T(8,128)S(1)} collective-permute-done((f32[52,8,128]{2,1,0:T(8,128)S(1)}, f32[52,8,128]{2,1,0:T(8,128)S(1)}, u32[]{:S(2)}, u32[]{:S(2)}) %collective-permute-start.2) | collective-permute-done | bytes 213024 | tf_op jit(solution)/shard_map/ppermute | solution.py:43
  18.2 1.7 %collective-permute-done.3.ry_b = f32[52,8,128]{2,1,0:T(8,128)S(1)} collective-permute-done((f32[52,8,128]{2,1,0:T(8,128)S(1)}, f32[52,8,128]{2,1,0:T(8,128)S(1)}, u32[]{:S(2)}, u32[]{:S(2)}) %collective-permute-start.3) | collective-permute-done | bytes 213024 | tf_op jit(solution)/shard_map/ppermute | solution.py:48
  19.9 0.7 pack_z.1
  20.6 2.0 %collective-permute-start.4 = (f32[25,8,128]{2,1,0:T(8,128)S(1)}, f32[25,8,128]{2,1,0:T(8,128)S(1)}, u32[]{:S(2)}, u32[]{:S(2)}) collective-permute-start(f32[25,8,128]{2,1,0:T(8,128)S(1)} %get-tuple-element.41), channel_id=1, source_target_pairs={{0,1},{1,0},{2,3},{3,2},{4,5},{5,4},{6,7},{7,6},{8,9},{9,8},{10,11... | collective-permute-start | bytes 307208 | tf_op jit(solution)/shard_map/ppermute | solution.py:43
  22.6 4.9 %collective-permute-start.5 = (f32[25,8,128]{2,1,0:T(8,128)S(1)}, f32[25,8,128]{2,1,0:T(8,128)S(1)}, u32[]{:S(2)}, u32[]{:S(2)}) collective-permute-start(f32[25,8,128]{2,1,0:T(8,128)S(1)} %get-tuple-element.42), channel_id=1, source_target_pairs={{0,7},{1,2},{2,1},{3,4},{4,3},{5,6},{6,5},{7,0},{8,15},{9,10},{10,... | collective-permute-start | bytes 307208 | tf_op jit(solution)/shard_map/ppermute | solution.py:48
  27.6 0.0 copy-done.8
  27.6 0.0 copy-done.9
  27.6 10.0 %main_work.1 = (f32[22,56,128]{2,1,0:T(8,128)S(1)}, f32[3,18,56,128]{3,2,1,0:T(8,128)S(1)}, f32[3,16,32,128]{3,2,1,0:T(8,128)S(1)}, f32[8,128]{1,0:T(8,128)S(1)}) custom-call(f32[3,16,32,128]{3,2,1,0:T(8,128)S(1)} %copy-done.1, f32[3,16,32,128]{3,2,1,0:T(8,128)S(1)} %copy-done.3, f32[4,8,128]{2,1,0:T(8,128)S(1)} %pad.4.phase.phase_ref, ...), custom_call_target="tpu_custom_call" | custom-call | flops 33554432 | bytes 1048576 | tf_op jit(solution)/shard_map/main_work/pallas_call | solution.py:635
  37.6 0.0 copy-start.4
  37.6 1.2 %copy-done.4 = f32[3,18,56,128]{3,2,1,0:T(8,128)} copy-done((f32[3,18,56,128]{3,2,1,0:T(8,128)}, f32[3,18,56,128]{3,2,1,0:T(8,128)S(1)}, u32[]{:S(2)}) %copy-start.4) | copy-done | bytes 1548312
  38.8 0.0 copy-start.6
  38.8 0.0 collective-permute-done.4.rz_a
  38.8 0.0 collective-permute-done.5.rz_b
  38.8 4.2 %edge_work.1 = (f32[6,40,128]{2,1,0:T(8,128)S(1)}, f32[3,6,32,128]{3,2,1,0:T(8,128)S(1)}, f32[3,6,32,128]{3,2,1,0:T(8,128)S(1)}, f32[1,128]{1,0:T(1,128)S(1)}) custom-call(f32[25,8,128]{2,1,0:T(8,128)S(1)} %collective-permute-done.4.rz_a, f32[25,8,128]{2,1,0:T(8,128)S(1)} %collective-permute-done.5.rz_b, f32[3,6,32,128]{3,2,1,0:T(8,128)S(1)} %get-tuple-element.39.eu, ...), custom_call_target="tpu_custom_call" | custom-call | flops 8388608 | bytes 1048576 | tf_op jit(solution)/shard_map/edge_work/pallas_call | solution.py:645
  43.0 0.0 copy-done.6
  43.0 2.8 %collective-permute-start.6 = (f32[1,128]{1,0:T(1,128)S(1)}, f32[1,128]{1,0:T(1,128)S(1)}, u32[]{:S(2)}, u32[]{:S(2)}) collective-permute-start(f32[1,128]{1,0:T(1,128)S(1)} %get-tuple-element.55), channel_id=1, source_target_pairs={{0,128},{32,160},{64,192},{96,224},{128,0},{160,32},{192,64},{224,... | collective-permute-start | bytes 1544 | tf_op jit(solution)/shard_map/ppermute | solution.py:609
  45.8 2.3 %collective-permute-done.6 = f32[1,128]{1,0:T(1,128)S(1)} collective-permute-done((f32[1,128]{1,0:T(1,128)S(1)}, f32[1,128]{1,0:T(1,128)S(1)}, u32[]{:S(2)}, u32[]{:S(2)}) %collective-permute-start.6) | collective-permute-done | bytes 544 | tf_op jit(solution)/shard_map/ppermute | solution.py:609
  48.1 1.4 %collective-permute-start.7 = (f32[1,128]{1,0:T(1,128)S(1)}, f32[1,128]{1,0:T(1,128)S(1)}, u32[]{:S(2)}, u32[]{:S(2)}) collective-permute-start(f32[1,128]{1,0:T(1,128)S(1)} %add.52), channel_id=1, source_target_pairs={{0,4},{1,5},{2,6},{3,7},{4,0},{5,1},{6,2},{7,3},{8,12},{9,13},{10,... | collective-permute-start | bytes 1544 | tf_op jit(solution)/shard_map/ppermute | solution.py:609
  49.5 0.0 copy-start.5
  49.5 1.4 %copy-done.5 = f32[3,18,56,128]{3,2,1,0:T(8,128)S(1)} copy-done((f32[3,18,56,128]{3,2,1,0:T(8,128)S(1)}, f32[3,18,56,128]{3,2,1,0:T(8,128)}, u32[]{:S(2)}) %copy-start.5) | copy-done | bytes 1548312
  50.9 0.0 copy-start.7
  50.9 1.1 %copy-done.7 = f32[22,56,128]{2,1,0:T(8,128)S(1)} copy-done((f32[22,56,128]{2,1,0:T(8,128)S(1)}, f32[22,56,128]{2,1,0:T(8,128)}, u32[]{:S(2)}) %copy-start.7) | copy-done | bytes 630808
  52.0 2.9 %collect.1 = (f32[3,16,32,128]{3,2,1,0:T(8,128)}, f32[16,32,128]{2,1,0:T(8,128)}, f32[8,16,64]{2,1,0:T(8,128)}, f32[4,8,32]{2,1,0:T(8,128)}, f32[3,16,32,128]{3,2,1,0:T(8,128)}, /*index=5*/f32[4,8,128]{2,1,0:T(8,128)S(1)}) custom-call(f32[22,56,128]{2,1,0:T(8,128)S(1)} %copy-done.7, f32[3,18,56,128]{3,2,1,0:T(8,128)S(1)} %copy-done.5, ...), custom_call_target="tpu_custom_call" | custom-call | flops 8388608 | bytes 1048576 | tf_op jit(solution)/shard_map/collect/pallas_call | solution.py:658
  54.9 0.7 collective-permute-done.7
  55.6 0.1 bitcast_select_fusion.1
  55.7 0.0 collective-permute-start.8
  55.7 1.2 %collective-permute-done.8 = f32[8,128]{1,0:T(8,128)S(1)} collective-permute-done((f32[8,128]{1,0:T(8,128)S(1)}, f32[8,128]{1,0:T(8,128)S(1)}, u32[]{:S(2)}, u32[]{:S(2)}) %collective-permute-start.8) | collective-permute-done | bytes 4128 | tf_op jit(solution)/shard_map/ppermute | solution.py:43
  56.9 0.1 bitcast_select_fusion
  57.0 2.7 %collective-permute-start.9 = (f32[8,128]{1,0:T(8,128)S(1)}, f32[8,128]{1,0:T(8,128)S(1)}, u32[]{:S(2)}, u32[]{:S(2)}) collective-permute-start(f32[8,128]{1,0:T(8,128)S(1)} %bitcast_select_fusion), channel_id=1, source_target_pairs={{0,224},{32,64},{64,32},{96,128},{128,96},{160,192},{192,160},{224... | collective-permute-start | bytes 12296 | tf_op jit(solution)/shard_map/ppermute | solution.py:48
  59.7 1.5 %collective-permute-done.9 = f32[8,128]{1,0:T(8,128)S(1)} collective-permute-done((f32[8,128]{1,0:T(8,128)S(1)}, f32[8,128]{1,0:T(8,128)S(1)}, u32[]{:S(2)}, u32[]{:S(2)}) %collective-permute-start.9) | collective-permute-done | bytes 4128 | tf_op jit(solution)/shard_map/ppermute | solution.py:48
  61.2 0.1 fusion.3
  61.3 0.1 collective-permute-start.10
  61.4 3.6 %collective-permute-done.10 = f32[2,8,128]{2,1,0:T(8,128)S(1)} collective-permute-done((f32[2,8,128]{2,1,0:T(8,128)S(1)}, f32[2,8,128]{2,1,0:T(8,128)S(1)}, u32[]{:S(2)}, u32[]{:S(2)}) %collective-permute-start.10) | collective-permute-done | bytes 8224 | tf_op jit(solution)/shard_map/ppermute | solution.py:43
  65.0 0.1 fusion.2
  65.1 1.1 %collective-permute-start.11 = (f32[2,8,128]{2,1,0:T(8,128)S(1)}, f32[2,8,128]{2,1,0:T(8,128)S(1)}, u32[]{:S(2)}, u32[]{:S(2)}) collective-permute-start(f32[2,8,128]{2,1,0:T(8,128)S(1)} %fusion.2), channel_id=1, source_target_pairs={{0,24},{8,16},{16,8},{24,0},{1,25},{9,17},{17,9},{25,1},{2,26},{10... | collective-permute-start | bytes 24584 | tf_op jit(solution)/shard_map/ppermute | solution.py:48
  66.2 3.8 %collective-permute-done.11 = f32[2,8,128]{2,1,0:T(8,128)S(1)} collective-permute-done((f32[2,8,128]{2,1,0:T(8,128)S(1)}, f32[2,8,128]{2,1,0:T(8,128)S(1)}, u32[]{:S(2)}, u32[]{:S(2)}) %collective-permute-start.11) | collective-permute-done | bytes 8224 | tf_op jit(solution)/shard_map/ppermute | solution.py:48
  70.0 0.1 broadcast_select_fusion.1
  70.1 1.3 %collective-permute-start.12 = (f32[2,8,128]{2,1,0:T(8,128)S(1)}, f32[2,8,128]{2,1,0:T(8,128)S(1)}, u32[]{:S(2)}, u32[]{:S(2)}) collective-permute-start(f32[2,8,128]{2,1,0:T(8,128)S(1)} %get-tuple-element.59), channel_id=1, source_target_pairs={{0,1},{1,0},{2,3},{3,2},{4,5},{5,4},{6,7},{7,6},{8,9},{9,8},{10,11... | collective-permute-start | bytes 24584 | tf_op jit(solution)/shard_map/ppermute | solution.py:43
  71.4 2.4 %collective-permute-done.12 = f32[2,8,128]{2,1,0:T(8,128)S(1)} collective-permute-done((f32[2,8,128]{2,1,0:T(8,128)S(1)}, f32[2,8,128]{2,1,0:T(8,128)S(1)}, u32[]{:S(2)}, u32[]{:S(2)}) %collective-permute-start.12) | collective-permute-done | bytes 8224 | tf_op jit(solution)/shard_map/ppermute | solution.py:43
  73.7 0.1 broadcast_select_fusion
  73.8 2.5 %collective-permute-start.13 = (f32[2,8,128]{2,1,0:T(8,128)S(1)}, f32[2,8,128]{2,1,0:T(8,128)S(1)}, u32[]{:S(2)}, u32[]{:S(2)}) collective-permute-start(f32[2,8,128]{2,1,0:T(8,128)S(1)} %broadcast_select_fusion), channel_id=1, source_target_pairs={{0,7},{1,2},{2,1},{3,4},{4,3},{5,6},{6,5},{7,0},{8,15},{9,10},{10,... | collective-permute-start | bytes 24584 | tf_op jit(solution)/shard_map/ppermute | solution.py:48
  76.3 2.4 %collective-permute-done.13 = f32[2,8,128]{2,1,0:T(8,128)S(1)} collective-permute-done((f32[2,8,128]{2,1,0:T(8,128)S(1)}, f32[2,8,128]{2,1,0:T(8,128)S(1)}, u32[]{:S(2)}, u32[]{:S(2)}) %collective-permute-start.13) | collective-permute-done | bytes 8224 | tf_op jit(solution)/shard_map/ppermute | solution.py:48
  78.8 0.2 fusion.5
  79.0 0.7 fusion.6
  (17 shorter events, 0.1 us)
Async XLA Ops:
  1.4 1.1 %copy-start = (f32[3,16,32,128]{3,2,1,0:T(8,128)S(1)}, f32[3,16,32,128]{3,2,1,0:T(8,128)}, u32[]{:S(2)}) copy-start(f32[3,16,32,128]{3,2,1,0:T(8,128)} %vel.7) | copy-start | bytes 2359300
  2.5 1.1 %copy-start.2 = (f32[3,16,32,128]{3,2,1,0:T(8,128)S(1)}, f32[3,16,32,128]{3,2,1,0:T(8,128)}, u32[]{:S(2)}) copy-start(f32[3,16,32,128]{3,2,1,0:T(8,128)} %forc.7) | copy-start | bytes 2359300
  3.6 10.0 %copy-start.1 = (f32[3,16,32,128]{3,2,1,0:T(8,128)S(1)}, f32[3,16,32,128]{3,2,1,0:T(8,128)}, u32[]{:S(2)}) copy-start(f32[3,16,32,128]{3,2,1,0:T(8,128)} %vel.7) | copy-start | bytes 2359300
  3.6 10.0 %copy-start.3 = (f32[3,16,32,128]{3,2,1,0:T(8,128)S(1)}, f32[3,16,32,128]{3,2,1,0:T(8,128)}, u32[]{:S(2)}) copy-start(f32[3,16,32,128]{3,2,1,0:T(8,128)} %forc.7) | copy-start | bytes 2359300
  3.7 3.0 %collective-permute-start = (f32[19,32,128]{2,1,0:T(8,128)S(1)}, f32[19,32,128]{2,1,0:T(8,128)S(1)}, u32[]{:S(2)}, u32[]{:S(2)}) collective-permute-start(f32[19,32,128]{2,1,0:T(8,128)S(1)} %get-tuple-element.32), channel_id=1, source_target_pairs={{0,32},{32,0},{64,96},{96,64},{128,160},{160,128},{192,224},{224,1... | collective-permute-start | bytes 933896 | tf_op jit(solution)/shard_map/ppermute | solution.py:43
  3.8 7.6 %collective-permute-start.1 = (f32[19,32,128]{2,1,0:T(8,128)S(1)}, f32[19,32,128]{2,1,0:T(8,128)S(1)}, u32[]{:S(2)}, u32[]{:S(2)}) collective-permute-start(f32[19,32,128]{2,1,0:T(8,128)S(1)} %get-tuple-element.33), channel_id=1, source_target_pairs={{0,224},{32,64},{64,32},{96,128},{128,96},{160,192},{192,160},{224... | collective-permute-start | bytes 933896 | tf_op jit(solution)/shard_map/ppermute | solution.py:48
  11.5 6.7 %collective-permute-start.2 = (f32[52,8,128]{2,1,0:T(8,128)S(1)}, f32[52,8,128]{2,1,0:T(8,128)S(1)}, u32[]{:S(2)}, u32[]{:S(2)}) collective-permute-start(f32[52,8,128]{2,1,0:T(8,128)S(1)} %get-tuple-element.34), channel_id=1, source_target_pairs={{0,8},{8,0},{16,24},{24,16},{1,9},{9,1},{17,25},{25,17},{2,10},{10... | collective-permute-start | bytes 638984 | tf_op jit(solution)/shard_map/ppermute | solution.py:43
  12.3 7.6 %collective-permute-start.3 = (f32[52,8,128]{2,1,0:T(8,128)S(1)}, f32[52,8,128]{2,1,0:T(8,128)S(1)}, u32[]{:S(2)}, u32[]{:S(2)}) collective-permute-start(f32[52,8,128]{2,1,0:T(8,128)S(1)} %get-tuple-element.35), channel_id=1, source_target_pairs={{0,24},{8,16},{16,8},{24,0},{1,25},{9,17},{17,9},{25,1},{2,26},{10... | collective-permute-start | bytes 638984 | tf_op jit(solution)/shard_map/ppermute | solution.py:48
  13.6 14.0 %copy-start.8 = (f32[8]{0:T(128)S(1)}, f32[8]{0:T(128)}, u32[]{:S(2)}) copy-start(f32[8]{0:T(128)} %pre.3) | copy-start | bytes 100
  13.6 14.0 %copy-start.9 = (f32[8]{0:T(128)S(1)}, f32[8]{0:T(128)}, u32[]{:S(2)}) copy-start(f32[8]{0:T(128)} %yld.3) | copy-start | bytes 100
  20.6 18.2 %collective-permute-start.4 = (f32[25,8,128]{2,1,0:T(8,128)S(1)}, f32[25,8,128]{2,1,0:T(8,128)S(1)}, u32[]{:S(2)}, u32[]{:S(2)}) collective-permute-start(f32[25,8,128]{2,1,0:T(8,128)S(1)} %get-tuple-element.41), channel_id=1, source_target_pairs={{0,1},{1,0},{2,3},{3,2},{4,5},{5,4},{6,7},{7,6},{8,9},{9,8},{10,11... | collective-permute-start | bytes 307208 | tf_op jit(solution)/shard_map/ppermute | solution.py:43
  22.6 16.1 %collective-permute-start.5 = (f32[25,8,128]{2,1,0:T(8,128)S(1)}, f32[25,8,128]{2,1,0:T(8,128)S(1)}, u32[]{:S(2)}, u32[]{:S(2)}) collective-permute-start(f32[25,8,128]{2,1,0:T(8,128)S(1)} %get-tuple-element.42), channel_id=1, source_target_pairs={{0,7},{1,2},{2,1},{3,4},{4,3},{5,6},{6,5},{7,0},{8,15},{9,10},{10,... | collective-permute-start | bytes 307208 | tf_op jit(solution)/shard_map/ppermute | solution.py:48
  37.6 1.2 %copy-start.4 = (f32[3,18,56,128]{3,2,1,0:T(8,128)}, f32[3,18,56,128]{3,2,1,0:T(8,128)S(1)}, u32[]{:S(2)}) copy-start(f32[3,18,56,128]{3,2,1,0:T(8,128)S(1)} %get-tuple-element.37.u2) | copy-start | bytes 4644868
  38.8 4.3 %copy-start.6 = (f32[22,56,128]{2,1,0:T(8,128)}, f32[22,56,128]{2,1,0:T(8,128)S(1)}, u32[]{:S(2)}) copy-start(f32[22,56,128]{2,1,0:T(8,128)S(1)} %get-tuple-element.36.v_ref) | copy-start | bytes 1892356
  43.0 5.1 %collective-permute-start.6 = (f32[1,128]{1,0:T(1,128)S(1)}, f32[1,128]{1,0:T(1,128)S(1)}, u32[]{:S(2)}, u32[]{:S(2)}) collective-permute-start(f32[1,128]{1,0:T(1,128)S(1)} %get-tuple-element.55), channel_id=1, source_target_pairs={{0,128},{32,160},{64,192},{96,224},{128,0},{160,32},{192,64},{224,... | collective-permute-start | bytes 1544 | tf_op jit(solution)/shard_map/ppermute | solution.py:609
  48.1 7.5 %collective-permute-start.7 = (f32[1,128]{1,0:T(1,128)S(1)}, f32[1,128]{1,0:T(1,128)S(1)}, u32[]{:S(2)}, u32[]{:S(2)}) collective-permute-start(f32[1,128]{1,0:T(1,128)S(1)} %add.52), channel_id=1, source_target_pairs={{0,4},{1,5},{2,6},{3,7},{4,0},{5,1},{6,2},{7,3},{8,12},{9,13},{10,... | collective-permute-start | bytes 1544 | tf_op jit(solution)/shard_map/ppermute | solution.py:609
  49.5 1.4 %copy-start.5 = (f32[3,18,56,128]{3,2,1,0:T(8,128)S(1)}, f32[3,18,56,128]{3,2,1,0:T(8,128)}, u32[]{:S(2)}) copy-start(f32[3,18,56,128]{3,2,1,0:T(8,128)} %copy-done.4) | copy-start | bytes 4644868
  50.9 1.1 %copy-start.7 = (f32[22,56,128]{2,1,0:T(8,128)S(1)}, f32[22,56,128]{2,1,0:T(8,128)}, u32[]{:S(2)}) copy-start(f32[22,56,128]{2,1,0:T(8,128)} %copy-done.6) | copy-start | bytes 1892356
  55.7 1.2 %collective-permute-start.8 = (f32[8,128]{1,0:T(8,128)S(1)}, f32[8,128]{1,0:T(8,128)S(1)}, u32[]{:S(2)}, u32[]{:S(2)}) collective-permute-start(f32[8,128]{1,0:T(8,128)S(1)} %bitcast_select_fusion.1), channel_id=1, source_target_pairs={{0,32},{32,0},{64,96},{96,64},{128,160},{160,128},{192,224},{224,1... | collective-permute-start | bytes 12296 | tf_op jit(solution)/shard_map/ppermute | solution.py:43
  57.0 4.3 %collective-permute-start.9 = (f32[8,128]{1,0:T(8,128)S(1)}, f32[8,128]{1,0:T(8,128)S(1)}, u32[]{:S(2)}, u32[]{:S(2)}) collective-permute-start(f32[8,128]{1,0:T(8,128)S(1)} %bitcast_select_fusion), channel_id=1, source_target_pairs={{0,224},{32,64},{64,32},{96,128},{128,96},{160,192},{192,160},{224... | collective-permute-start | bytes 12296 | tf_op jit(solution)/shard_map/ppermute | solution.py:48
  61.3 3.7 %collective-permute-start.10 = (f32[2,8,128]{2,1,0:T(8,128)S(1)}, f32[2,8,128]{2,1,0:T(8,128)S(1)}, u32[]{:S(2)}, u32[]{:S(2)}) collective-permute-start(f32[2,8,128]{2,1,0:T(8,128)S(1)} %fusion.3), channel_id=1, source_target_pairs={{0,8},{8,0},{16,24},{24,16},{1,9},{9,1},{17,25},{25,17},{2,10},{10... | collective-permute-start | bytes 24584 | tf_op jit(solution)/shard_map/ppermute | solution.py:43
  65.1 4.9 %collective-permute-start.11 = (f32[2,8,128]{2,1,0:T(8,128)S(1)}, f32[2,8,128]{2,1,0:T(8,128)S(1)}, u32[]{:S(2)}, u32[]{:S(2)}) collective-permute-start(f32[2,8,128]{2,1,0:T(8,128)S(1)} %fusion.2), channel_id=1, source_target_pairs={{0,24},{8,16},{16,8},{24,0},{1,25},{9,17},{17,9},{25,1},{2,26},{10... | collective-permute-start | bytes 24584 | tf_op jit(solution)/shard_map/ppermute | solution.py:48
  70.1 3.7 %collective-permute-start.12 = (f32[2,8,128]{2,1,0:T(8,128)S(1)}, f32[2,8,128]{2,1,0:T(8,128)S(1)}, u32[]{:S(2)}, u32[]{:S(2)}) collective-permute-start(f32[2,8,128]{2,1,0:T(8,128)S(1)} %get-tuple-element.59), channel_id=1, source_target_pairs={{0,1},{1,0},{2,3},{3,2},{4,5},{5,4},{6,7},{7,6},{8,9},{9,8},{10,11... | collective-permute-start | bytes 24584 | tf_op jit(solution)/shard_map/ppermute | solution.py:43
  73.8 4.9 %collective-permute-start.13 = (f32[2,8,128]{2,1,0:T(8,128)S(1)}, f32[2,8,128]{2,1,0:T(8,128)S(1)}, u32[]{:S(2)}, u32[]{:S(2)}) collective-permute-start(f32[2,8,128]{2,1,0:T(8,128)S(1)} %broadcast_select_fusion), channel_id=1, source_target_pairs={{0,7},{1,2},{2,1},{3,4},{4,3},{5,6},{6,5},{7,0},{8,15},{9,10},{10,... | collective-permute-start | bytes 24584 | tf_op jit(solution)/shard_map/ppermute | solution.py:48

commit v3 on v2

--- a/solution.py
+++ b/solution.py
@@ -12,6 +12,7 @@
 AX = ("gx", "gy", "gz")
 NX, NY, NZ = 16, 32, 128
 VMEM = pl.BlockSpec(memory_space=pltpu.VMEM)
+LIM = 8
 SMEM = pl.BlockSpec(memory_space=pltpu.SMEM)
 
 
@@ -50,16 +51,53 @@
     )
 
 
-def params():
-    return pltpu.CompilerParams(vmem_limit_bytes=40 << 20)
+def params(mib):
+    return pltpu.CompilerParams(vmem_limit_bytes=mib << 20)
 
 
 def cost(flops):
     return pl.CostEstimate(flops=flops, bytes_accessed=1 << 20, transcendentals=0)
 
 
-def pack_x(vel, forc, phase, send_a, send_b):
+def put_pair(pair, axis, index, lo, hi):
+    even = position(axis)[0]
+    pair[0][index] = jnp.where(even, hi, lo)
+    pair[1][index] = jnp.where(even, lo, hi)
+
+
+def pack_rows4(pair, index, tile, p, q):
+    sub = subs()
+    lo = jnp.where(sub < 4, tile(p, 0), roll(tile(q, 0), 4, 0))
+    hi = jnp.where(sub < 4, roll(tile(p, 3), 4, 0), tile(q, 3))
+    put_pair(pair, "gy", index, lo, hi)
+
+
+def pack_rows2(pair, index, tile, planes):
+    sub = subs()
+    lo = tile(planes[0], 0)
+    hi = roll(tile(planes[0], 3), 2, 0)
+    for k in range(1, 4):
+        here = (sub >> 1) == k
+        lo = jnp.where(here, roll(tile(planes[k], 0), 2 * k, 0), lo)
+        hi = jnp.where(here, roll(tile(planes[k], 3), 2 * k + 2, 0), hi)
+    put_pair(pair, "gy", index, lo, hi)
+
+
+def pack_phase(pair, index, tiles):
+    sub = subs()
+    lo = jnp.zeros((8, 128), F32)
+    hi = lo
+    for b, tile in enumerate(tiles):
+        lo = jnp.where(sub == b, tile[0:1], lo)
+        hi = jnp.where(sub == b, tile[7:8], hi)
+    put_pair(pair, "gy", index, lo, hi)
+
+
+def pack_xy(vel, forc, blocks, send_a, send_b, own_a, own_b, phase):
     even, _, _ = position("gx")
+    phase[...] = jnp.zeros(phase.shape, F32)
+    for b in range(4):
+        phase[b, :, 0:32] = blocks[b].astype(F32)
     for out, first in ((send_a, jnp.where(even, 1, 0)), (send_b, jnp.where(even, 0, 1))):
         for c in range(3):
             for i in range(4):
@@ -67,6 +105,22 @@
             for i in range(2):
                 out[12 + 2 * c + i] = forc[c, 14 * first + i]
         out[18, 0:8] = phase[3 * first]
+    pair = (own_a, own_b)
+    for c in range(3):
+        for g in range(8):
+            pack_rows4(pair, 8 * c + g, lambda p, o: vel[c, p, 8 * o : 8 * o + 8], g, g + 8)
+        for g in range(4):
+            pack_rows2(pair, 24 + 4 * c + g, lambda p, o: forc[c, p, 8 * o : 8 * o + 8], [g + 4 * k for k in range(4)])
+    pack_phase(pair, 36, [phase[b] for b in range(4)])
+
+
+def pack_y(rx_a, rx_b, corner_a, corner_b):
+    rx, pair = (rx_a, rx_b), (corner_a, corner_b)
+    for c in range(3):
+        for i in range(4):
+            pack_rows4(pair, 4 * c + i, lambda p, o: tile_of(None, c, p, o, 4, rx, 0, None), i, 20 + i)
+        pack_rows2(pair, 12 + c, lambda p, o: tile_of(None, c, p, o, 2, rx, 12, None), [0, 1, 18, 19])
+    pack_phase(pair, 15, [phase_rows(None, rx, 0), phase_rows(None, rx, 5)])
 
 
 def halo(pair, axis, index):
@@ -81,13 +135,17 @@
     rows = slice(8 * o, 8 * o + 8)
     if o == 4:
         sub = subs()
+        inside = width <= plane < NX + width
+        pair = ry[0] if inside else ry[1]
+        at = plane - width if inside else plane if plane < width else plane - NX
         if width == 4:
-            lo, hi = halo(ry, "gy", c * 12 + plane % 12)
-            if plane < 12:
+            half = 8 if inside else 4
+            lo, hi = halo(pair, "gy", half * c + at % half)
+            if at < half:
                 return jnp.where(sub < 4, hi, roll(lo, 4, 0))
             return jnp.where(sub < 4, roll(hi, 4, 0), lo)
-        lo, hi = halo(ry, "gy", 36 + c * 5 + plane % 5)
-        k = plane // 5
+        lo, hi = halo(pair, "gy", 24 + 4 * c + at % 4 if inside else 12 + c)
+        k = at // 4 if inside else at
         return jnp.where(sub < 4, roll(hi, -2 * k, 0), roll(lo, 6 - 2 * k, 0))
     if plane < width:
         return halo(rx, "gx", (base + width * c + plane, rows))[0]
@@ -105,51 +163,16 @@
 
 
 def phase_tiles(phase, rx, ry):
-    lo, hi = halo(ry, "gy", 51)
+    own, corner = halo(ry[0], "gy", 36), halo(ry[1], "gy", 15)
     sub = subs()
     tiles = []
     for b in range(6):
         tiles.append(phase_rows(phase, rx, b))
-        outer = jnp.where(sub == 0, hi[b : b + 1], jnp.where(sub == 1, lo[b : b + 1], 0.0))
+        lo, hi = own if 0 < b < 5 else corner
+        row = b - 1 if 0 < b < 5 else b // 5
+        outer = jnp.where(sub == 0, hi[row : row + 1], jnp.where(sub == 1, lo[row : row + 1], 0.0))
         tiles.append(outer)
     return tiles
-
-
-def pack_y(vel, forc, phase, rx_a, rx_b, send_a, send_b):
-    rx = (rx_a, rx_b)
-    even, _, _ = position("gy")
-    sub = subs()
-
-    def put(index, lo, hi):
-        send_a[index] = jnp.where(even, hi, lo)
-        send_b[index] = jnp.where(even, lo, hi)
-
-    def u(c, p, o):
-        return tile_of(vel, c, p, o, 4, rx, 0, None)
-
-    def f(c, p, o):
-        return tile_of(forc, c, p, o, 2, rx, 12, None)
-
-    for c in range(3):
-        for p in range(12):
-            lo = jnp.where(sub < 4, u(c, p, 0), roll(u(c, p + 12, 0), 4, 0))
-            hi = jnp.where(sub < 4, roll(u(c, p, 3), 4, 0), u(c, p + 12, 3))
-            put(c * 12 + p, lo, hi)
-        for g in range(5):
-            lo = f(c, g, 0)
-            hi = roll(f(c, g, 3), 2, 0)
-            for k in range(1, 4):
-                here = (sub >> 1) == k
-                lo = jnp.where(here, roll(f(c, g + 5 * k, 0), 2 * k, 0), lo)
-                hi = jnp.where(here, roll(f(c, g + 5 * k, 3), 2 * k + 2, 0), hi)
-            put(36 + c * 5 + g, lo, hi)
-    lo = jnp.zeros((8, 128), F32)
-    hi = lo
-    for b in range(6):
-        tile = phase_rows(phase, rx, b)
-        lo = jnp.where(sub == b, tile[0:1], lo)
-        hi = jnp.where(sub == b, tile[7:8], hi)
-    put(51, lo, hi)
 
 
 def slots():
@@ -181,8 +204,8 @@
                 ef[c, i, rows] = edge_tile(lambda p: tile_of(forc, c, p, o, 2, rx, 12, None), i, 2, 20)
 
 
-def pack_z(phase, rx_a, rx_b, ry_a, ry_b, eu, ef, send_a, send_b, eu4, ef4, tiles):
-    rx, ry = (rx_a, rx_b), (ry_a, ry_b)
+def pack_z(phase, rx_a, rx_b, ryo_a, ryo_b, ryc_a, ryc_b, eu, ef, send_a, send_b, eu4, ef4, tiles):
+    rx, ry = (rx_a, rx_b), ((ryo_a, ryo_b), (ryc_a, ryc_b))
     even, _, _ = position("gz")
 
     def put(index, lo, hi):
@@ -299,11 +322,11 @@
 
 
 def main_work(
-    vel, forc, phase_ref, rx_a, rx_b, ry_a, ry_b, pre, yld,
+    vel, forc, phase_ref, rx_a, rx_b, ryo_a, ryo_b, ryc_a, ryc_b, pre, yld,
     v_ref, u2, residual, square,
     u_ref, f_ref, creep, limit, u1,
 ):
-    rx, ry = (rx_a, rx_b), (ry_a, ry_b)
+    rx, ry = (rx_a, rx_b), ((ryo_a, ryo_b), (ryc_a, ryc_b))
     lo_x, hi_x = flags("gx")
     lo_y, hi_y = flags("gy")
     for c in range(3):
@@ -328,7 +351,7 @@
             put_rows(v_ref, (vx,), o, value * (mask_y * mask_x if o == 4 else mask_x))
         return 0
 
-    lax.fori_loop(0, 22, viscosity, 0)
+    lax.fori_loop(0, 22, viscosity, 0, unroll=2)
 
     def sweep(source, target, first, first_u):
         def body(x, _):
@@ -343,8 +366,8 @@
 
         return body
 
-    lax.fori_loop(0, 20, sweep(u_ref, u1, 1, 2), 0)
-    lax.fori_loop(0, 18, sweep(u1, u2, 2, 1), 0)
+    lax.fori_loop(0, 20, sweep(u_ref, u1, 1, 2), 0, unroll=2)
+    lax.fori_loop(0, 18, sweep(u1, u2, 2, 1), 0, unroll=2)
 
     def last(x, acc):
         for o in range(4):
@@ -356,7 +379,7 @@
                 acc = acc + value * value
         return acc
 
-    acc = lax.fori_loop(0, NX, last, jnp.zeros((8, 128), F32))
+    acc = lax.fori_loop(0, NX, last, jnp.zeros((8, 128), F32), unroll=2)
     lane = lanes()
     square[...] = jnp.where((lane >= 4) & (lane < 124), acc, 0.0)
 
@@ -434,7 +457,7 @@
             v_out[i, 8 * o : 8 * o + 8] = value
         return 0
 
-    lax.fori_loop(0, 6, viscosity, 0)
+    lax.fori_loop(0, 6, viscosity, 0, unroll=3)
     wrap_planes(v_ref, ((),))
 
     def sweep(source, target):
@@ -448,7 +471,7 @@
                     put_edge(target, (c,), i, o, 0.2 * mid + rate * (2.0 * force + total))
             return 0
 
-        lax.fori_loop(0, 6, body, 0)
+        lax.fori_loop(0, 6, body, 0, unroll=3)
         wrap_planes(target, lead)
 
     sweep(u_ref, u1)
@@ -467,7 +490,7 @@
                 acc = acc + jnp.where(count, value * value, 0.0)
         return acc
 
-    acc = lax.fori_loop(0, 6, last, square[...])
+    acc = lax.fori_loop(0, 6, last, square[...], unroll=3)
     total = jnp.sum(jnp.sum(acc, axis=1, keepdims=True), axis=0, keepdims=True)
     total_out[...] = jnp.broadcast_to(total, (1, 128))
 
@@ -609,38 +632,37 @@
     return lax.ppermute(total, axis, [(i, (i + count // 2) % count) for i in range(count)])
 
 
-def pack(kernel, shape, name, *args):
-    return pl.pallas_call(
-        kernel, out_shape=[sds(*shape)] * 2, in_specs=[VMEM] * len(args), out_specs=[VMEM] * 2,
-        compiler_params=params(), name=name,
-    )(*args)
-
-
 def per_device(velocity, forcing, phase_block, prefactor, yield_stress):
-    phase = jnp.pad(phase_block.astype(F32), ((0, 0), (0, 0), (0, 96)))
+    send_a, send_b, own_a, own_b, phase = pl.pallas_call(
+        pack_xy, out_shape=[sds(19, 32, 128)] * 2 + [sds(37, 8, 128)] * 2 + [sds(4, 8, 128)],
+        in_specs=[VMEM] * 3, out_specs=[VMEM] * 5, compiler_params=params(LIM), name="pack_xy",
+    )(velocity, forcing, phase_block)
     own = (velocity, forcing, phase)
-    send_a, send_b = pack(pack_x, (19, 32, 128), "pack_x", *own)
     rx = (pair_a(send_a, "gx"), pair_b(send_b, "gx"))
-    send_a, send_b = pack(pack_y, (52, 8, 128), "pack_y", *own, *rx)
-    ry = (pair_a(send_a, "gy"), pair_b(send_b, "gy"))
+    ry = (pair_a(own_a, "gy"), pair_b(own_b, "gy"))
+    corner_a, corner_b = pl.pallas_call(
+        pack_y, out_shape=[sds(16, 8, 128)] * 2, in_specs=[VMEM] * 2, out_specs=[VMEM] * 2,
+        compiler_params=params(LIM), name="pack_y",
+    )(*rx)
+    ry = ry + (pair_a(corner_a, "gy"), pair_b(corner_b, "gy"))
     eu, ef = pl.pallas_call(
         edge_own, out_shape=[sds(3, 6, 32, 128)] * 2, in_specs=[VMEM] * 4, out_specs=[VMEM] * 2,
-        compiler_params=params(), cost_estimate=cost(3 << 23), name="edge_own",
+        compiler_params=params(LIM), cost_estimate=cost(3 << 23), name="edge_own",
     )(velocity, forcing, *rx)
     send_a, send_b, eu4, ef4, tiles = pl.pallas_call(
         pack_z, out_shape=[sds(25, 8, 128)] * 2 + [sds(3, 6, 8, 128)] * 2 + [sds(12, 8, 128)],
-        in_specs=[VMEM] * 7, out_specs=[VMEM] * 5, compiler_params=params(), name="pack_z",
+        in_specs=[VMEM] * 9, out_specs=[VMEM] * 5, compiler_params=params(LIM), name="pack_z",
     )(phase, *rx, *ry, eu, ef)
     rz = (pair_a(send_a, "gz"), pair_b(send_b, "gz"))
     v, u2, res, square = pl.pallas_call(
         main_work,
         out_shape=[sds(22, 56, 128), sds(3, 18, 56, 128), sds(3, NX, NY, NZ), sds(8, 128)],
-        in_specs=[VMEM] * 7 + [SMEM] * 2, out_specs=[VMEM] * 4,
+        in_specs=[VMEM] * 9 + [SMEM] * 2, out_specs=[VMEM] * 4,
         scratch_shapes=[
             pltpu.VMEM((3, 24, 56, 128), F32), pltpu.VMEM((3, 20, 40, 128), F32),
             pltpu.VMEM((6, 40, 128), F32), pltpu.VMEM((6, 40, 128), F32), pltpu.VMEM((3, 20, 56, 128), F32),
         ],
-        compiler_params=params(), cost_estimate=cost(1 << 25), name="main_work",
+        compiler_params=params(LIM), cost_estimate=cost(1 << 25), name="main_work",
     )(*own, *rx, *ry, prefactor, yield_stress)
     ve, ue, re, total = pl.pallas_call(
         edge_work,
@@ -651,7 +673,7 @@
             *[pltpu.VMEM((6, 40, 128), F32)] * 4,
             pltpu.VMEM((8, 56, 128), F32), pltpu.VMEM((3, 8, 56, 128), F32), pltpu.VMEM((3, 8, 56, 128), F32),
         ],
-        compiler_params=params(), cost_estimate=cost(1 << 23), name="edge_work",
+        compiler_params=params(LIM), cost_estimate=cost(1 << 23), name="edge_work",
     )(*rz, eu, ef, eu4, ef4, tiles, square, prefactor, yield_stress)
     total = total + far("gx", total)
     total = total + far("gz", total)
@@ -666,7 +688,7 @@
             pltpu.VMEM((10, 56, 128), F32), pltpu.VMEM((10, 56, 128), F32), pltpu.VMEM((10, 24, 256), F32),
             pltpu.VMEM((10, 24, 128), F32), pltpu.VMEM((24, 128), F32), pltpu.VMEM((24, 128), F32),
         ],
-        compiler_params=params(), cost_estimate=cost(1 << 23), name="collect",
+        compiler_params=params(LIM), cost_estimate=cost(1 << 23), name="collect",
     )(v, u2, res, ve, ue, re)
     total, three = finish(partial, total)
     cells = 3.0 * NX * NY * NZ

time: 81.1 us -> 75 us (0.925)
  Pallas kernels: 19.2 us -> 15 us
  waiting for transfers between devices: 27.7 us -> 25.6 us
    pallas_call x1, Pallas kernels: 10 us -> 7.05 us  [per_device(): pl.pallas_call(main_work, out_shape=[sds(22, 56, 128), sds(3, 18, 56, 128...]
    ppermute x6 -> x7, waiting for transfers between devices: 10.5 us -> 8.11 us  [pair_a(): return lax.ppermute(value, axis, [(i, i ^ 1) for i in range(count)])]
    pallas_call x1, Pallas kernels: 4.24 us -> 3.04 us  [per_device(): pl.pallas_call(edge_work, out_shape=[sds(6, 40, 128), sds(3, 6, 32, 128),...]
    ppermute x6 -> x7, starting transfers between devices: 4.38 us -> 5.11 us  [pair_a(): return lax.ppermute(value, axis, [(i, i ^ 1) for i in range(count)])]
    unnamed x20 -> x22, local copies, waits for them, and re-layouts: 5.93 us -> 6.64 us
    ppermute x6 -> x7, waiting for transfers between devices: 14.1 us -> 13.7 us  [pair_b(): lax.ppermute(value, axis, [(i, (i + 1) % count if i % 2 else (i - 1) % co...]
    ppermute x6 -> x7, starting transfers between devices: 15.4 us -> 15.6 us  [pair_b(): lax.ppermute(value, axis, [(i, (i + 1) % count if i % 2 else (i - 1) % co...]
  transfers between devices with their start and end apart: 14 -> 16, of which waited for: 11 -> 11; matrix products, arithmetic and copies ran while one was open for 0% -> 0% of each run, Pallas kernels for 17% -> 15%
where the time goes in v3:
time: 75 us; the launch traced here: 74.7 us
  waiting for transfers between devices  25.6 us (34%)
  starting transfers between devices  24.1 us (32%)
  Pallas kernels  15 us (20%)
  local copies, waits for them, and re-layouts  6.65 us (9%)
  between operations  1.98 us (3%)
  other arithmetic  1.36 us (2%)
    ppermute x7, starting transfers between devices, pair_b(): lax.ppermute(value, axis, [(i, (i + 1) % count if i % 2 else (i - 1) % co...  15.6 us
    ppermute x7, waiting for transfers between devices, pair_b(): lax.ppermute(value, axis, [(i, (i + 1) % count if i % 2 else (i - 1) % co...  13.7 us
    ppermute x7, waiting for transfers between devices, pair_a(): return lax.ppermute(value, axis, [(i, i ^ 1) for i in range(count)])  8.11 us
    pallas_call x1, Pallas kernels, per_device(): pl.pallas_call(main_work, out_shape=[sds(22, 56, 128), sds(3, 18, 56, 128...  7.05 us
    unnamed x22, local copies, waits for them, and re-layouts  6.64 us
    ppermute x7, starting transfers between devices, pair_a(): return lax.ppermute(value, axis, [(i, i ^ 1) for i in range(count)])  5.11 us
    ppermute x2, waiting for transfers between devices, far(): lax.ppermute(total, axis, [(i, (i + count // 2) % count) for i in range(c...  3.84 us
    ppermute x2, starting transfers between devices, far(): lax.ppermute(total, axis, [(i, (i + count // 2) % count) for i in range(c...  3.36 us
  transfers between devices with their start and end apart: 16, of which 11 were waited for; matrix products, arithmetic and copies ran while one was open for 0% of the time, Pallas kernels for 15%

profile of v3, /device:TPU:24, one launch (start us, length us, event | category | flops | bytes accessed | tf_op | source)
XLA Modules:
  0.0 74.7 jit_solution(11398199609190241260)
XLA Ops:
  0.6 0.0 copy-start
  0.6 1.1 %copy-done = f32[3,16,32,128]{3,2,1,0:T(8,128)S(1)} copy-done((f32[3,16,32,128]{3,2,1,0:T(8,128)S(1)}, f32[3,16,32,128]{3,2,1,0:T(8,128)}, u32[]{:S(2)}) %copy-start) | copy-done | bytes 786456
  1.8 0.0 copy-start.2
  1.8 1.1 %copy-done.2 = f32[3,16,32,128]{3,2,1,0:T(8,128)S(1)} copy-done((f32[3,16,32,128]{3,2,1,0:T(8,128)S(1)}, f32[3,16,32,128]{3,2,1,0:T(8,128)}, u32[]{:S(2)}) %copy-start.2) | copy-done | bytes 786456
  2.9 0.0 copy-start.8
  2.9 0.7 copy-done.8
  3.6 0.0 copy-start.1
  3.6 0.0 copy-start.3
  3.6 0.1 pack_xy.1
  3.7 0.1 collective-permute-start
  3.8 2.9 %collective-permute-start.1 = (f32[19,32,128]{2,1,0:T(8,128)S(1)}, f32[19,32,128]{2,1,0:T(8,128)S(1)}, u32[]{:S(2)}, u32[]{:S(2)}) collective-permute-start(f32[19,32,128]{2,1,0:T(8,128)S(1)} %get-tuple-element.37), channel_id=1, source_target_pairs={{0,224},{32,64},{64,32},{96,128},{128,96},{160,192},{192,160},{224... | collective-permute-start | bytes 933896 | tf_op jit(solution)/shard_map/ppermute | solution.py:49
  6.7 0.7 collective-permute-start.2
  7.4 1.1 %collective-permute-start.3 = (f32[37,8,128]{2,1,0:T(8,128)S(1)}, f32[37,8,128]{2,1,0:T(8,128)S(1)}, u32[]{:S(2)}, u32[]{:S(2)}) collective-permute-start(f32[37,8,128]{2,1,0:T(8,128)S(1)} %get-tuple-element.39), channel_id=1, source_target_pairs={{0,24},{8,16},{16,8},{24,0},{1,25},{9,17},{17,9},{25,1},{2,26},{10... | collective-permute-start | bytes 454664 | tf_op jit(solution)/shard_map/ppermute | solution.py:49
  8.5 0.0 collective-permute-done.rx_a
  8.5 3.0 %collective-permute-done.1.rx_b = f32[19,32,128]{2,1,0:T(8,128)S(1)} collective-permute-done((f32[19,32,128]{2,1,0:T(8,128)S(1)}, f32[19,32,128]{2,1,0:T(8,128)S(1)}, u32[]{:S(2)}, u32[]{:S(2)}) %collective-permute-start.1) | collective-permute-done | bytes 311328 | tf_op jit(solution)/shard_map/ppermute | solution.py:49
  11.5 0.8 %collective-permute-start.4 = (f32[16,8,128]{2,1,0:T(8,128)S(1)}, f32[16,8,128]{2,1,0:T(8,128)S(1)}, u32[]{:S(2)}, u32[]{:S(2)}) collective-permute-start(f32[16,8,128]{2,1,0:T(8,128)S(1)} %get-tuple-element.40), channel_id=1, source_target_pairs={{0,8},{8,0},{16,24},{24,16},{1,9},{9,1},{17,25},{25,17},{2,10},{10... | collective-permute-start | bytes 196616 | tf_op jit(solution)/shard_map/ppermute | solution.py:44
  12.3 1.3 %collective-permute-start.5 = (f32[16,8,128]{2,1,0:T(8,128)S(1)}, f32[16,8,128]{2,1,0:T(8,128)S(1)}, u32[]{:S(2)}, u32[]{:S(2)}) collective-permute-start(f32[16,8,128]{2,1,0:T(8,128)S(1)} %get-tuple-element.41), channel_id=1, source_target_pairs={{0,24},{8,16},{16,8},{24,0},{1,25},{9,17},{17,9},{25,1},{2,26},{10... | collective-permute-start | bytes 196616 | tf_op jit(solution)/shard_map/ppermute | solution.py:49
  13.6 0.0 copy-done.1
  13.6 0.0 copy-done.3
  13.6 0.0 copy-start.9
  13.6 1.2 %edge_own.1 = (f32[3,6,32,128]{3,2,1,0:T(8,128)S(1)}, f32[3,6,32,128]{3,2,1,0:T(8,128)S(1)}) custom-call(f32[3,16,32,128]{3,2,1,0:T(8,128)S(1)} %copy-done.1, f32[3,16,32,128]{3,2,1,0:T(8,128)S(1)} %copy-done.3, f32[19,32,128]{2,1,0:T(8,128)S(1)} %collective-permute-done.rx_a, f32[19,32,128]{2,1,0:T(8,128)S(1)} %collective-permute-done.1.rx_b), custom_call_target="tpu_custom_call" | custom-call | flops 25165824 | bytes 1048576 | tf_op jit(solution)/shard_map/edge_own/pallas_call | solution.py:648
  14.8 0.0 collective-permute-done.2.ryo_a
  14.8 0.0 collective-permute-done.3.ryo_b
  14.8 1.0 %collective-permute-done.4.ryc_a = f32[16,8,128]{2,1,0:T(8,128)S(1)} collective-permute-done((f32[16,8,128]{2,1,0:T(8,128)S(1)}, f32[16,8,128]{2,1,0:T(8,128)S(1)}, u32[]{:S(2)}, u32[]{:S(2)}) %collective-permute-start.4) | collective-permute-done | bytes 65568 | tf_op jit(solution)/shard_map/ppermute | solution.py:44
  15.8 2.0 %collective-permute-done.5.ryc_b = f32[16,8,128]{2,1,0:T(8,128)S(1)} collective-permute-done((f32[16,8,128]{2,1,0:T(8,128)S(1)}, f32[16,8,128]{2,1,0:T(8,128)S(1)}, u32[]{:S(2)}, u32[]{:S(2)}) %collective-permute-start.5) | collective-permute-done | bytes 65568 | tf_op jit(solution)/shard_map/ppermute | solution.py:49
  17.8 0.7 pack_z.1
  18.5 2.0 %collective-permute-start.6 = (f32[25,8,128]{2,1,0:T(8,128)S(1)}, f32[25,8,128]{2,1,0:T(8,128)S(1)}, u32[]{:S(2)}, u32[]{:S(2)}) collective-permute-start(f32[25,8,128]{2,1,0:T(8,128)S(1)} %get-tuple-element.47), channel_id=1, source_target_pairs={{0,1},{1,0},{2,3},{3,2},{4,5},{5,4},{6,7},{7,6},{8,9},{9,8},{10,11... | collective-permute-start | bytes 307208 | tf_op jit(solution)/shard_map/ppermute | solution.py:44
  20.5 4.9 %collective-permute-start.7 = (f32[25,8,128]{2,1,0:T(8,128)S(1)}, f32[25,8,128]{2,1,0:T(8,128)S(1)}, u32[]{:S(2)}, u32[]{:S(2)}) collective-permute-start(f32[25,8,128]{2,1,0:T(8,128)S(1)} %get-tuple-element.48), channel_id=1, source_target_pairs={{0,7},{1,2},{2,1},{3,4},{4,3},{5,6},{6,5},{7,0},{8,15},{9,10},{10,... | collective-permute-start | bytes 307208 | tf_op jit(solution)/shard_map/ppermute | solution.py:49
  25.5 0.0 copy-done.9
  25.5 0.0 copy-done.10
  25.5 7.0 %main_work.1 = (f32[22,56,128]{2,1,0:T(8,128)S(1)}, f32[3,18,56,128]{3,2,1,0:T(8,128)S(1)}, f32[3,16,32,128]{3,2,1,0:T(8,128)S(1)}, f32[8,128]{1,0:T(8,128)S(1)}) custom-call(f32[3,16,32,128]{3,2,1,0:T(8,128)S(1)} %copy-done.1, f32[3,16,32,128]{3,2,1,0:T(8,128)S(1)} %copy-done.3, f32[4,8,128]{2,1,0:T(8,128)S(1)} %get-tuple-element.35.phase_ref.phase, ...), custom_call_target="tpu_custom_call" | custom-call | flops 33554432 | bytes 1048576 | tf_op jit(solution)/shard_map/main_work/pallas_call | solution.py:657
  32.5 0.0 copy-start.4
  32.5 1.2 %copy-done.4 = f32[3,18,56,128]{3,2,1,0:T(8,128)} copy-done((f32[3,18,56,128]{3,2,1,0:T(8,128)}, f32[3,18,56,128]{3,2,1,0:T(8,128)S(1)}, u32[]{:S(2)}) %copy-start.4) | copy-done | bytes 1548312
  33.7 0.0 collective-permute-done.6.rz_a
  33.7 0.0 collective-permute-done.7.rz_b
  33.7 3.0 %edge_work.1 = (f32[6,40,128]{2,1,0:T(8,128)S(1)}, f32[3,6,32,128]{3,2,1,0:T(8,128)S(1)}, f32[3,6,32,128]{3,2,1,0:T(8,128)S(1)}, f32[1,128]{1,0:T(1,128)S(1)}) custom-call(f32[25,8,128]{2,1,0:T(8,128)S(1)} %collective-permute-done.6.rz_a, f32[25,8,128]{2,1,0:T(8,128)S(1)} %collective-permute-done.7.rz_b, f32[3,6,32,128]{3,2,1,0:T(8,128)S(1)} %get-tuple-element.45.eu, ...), custom_call_target="tpu_custom_call" | custom-call | flops 8388608 | bytes 1048576 | tf_op jit(solution)/shard_map/edge_work/pallas_call | solution.py:667
  36.8 0.0 copy-done.6
  36.8 2.0 %collective-permute-start.8 = (f32[1,128]{1,0:T(1,128)S(1)}, f32[1,128]{1,0:T(1,128)S(1)}, u32[]{:S(2)}, u32[]{:S(2)}) collective-permute-start(f32[1,128]{1,0:T(1,128)S(1)} %get-tuple-element.61), channel_id=1, source_target_pairs={{0,128},{32,160},{64,192},{96,224},{128,0},{160,32},{192,64},{224,... | collective-permute-start | bytes 1544 | tf_op jit(solution)/shard_map/ppermute | solution.py:632
  38.8 3.1 %collective-permute-done.8 = f32[1,128]{1,0:T(1,128)S(1)} collective-permute-done((f32[1,128]{1,0:T(1,128)S(1)}, f32[1,128]{1,0:T(1,128)S(1)}, u32[]{:S(2)}, u32[]{:S(2)}) %collective-permute-start.8) | collective-permute-done | bytes 544 | tf_op jit(solution)/shard_map/ppermute | solution.py:632
  41.9 1.4 %collective-permute-start.9 = (f32[1,128]{1,0:T(1,128)S(1)}, f32[1,128]{1,0:T(1,128)S(1)}, u32[]{:S(2)}, u32[]{:S(2)}) collective-permute-start(f32[1,128]{1,0:T(1,128)S(1)} %add.50), channel_id=1, source_target_pairs={{0,4},{1,5},{2,6},{3,7},{4,0},{5,1},{6,2},{7,3},{8,12},{9,13},{10,... | collective-permute-start | bytes 1544 | tf_op jit(solution)/shard_map/ppermute | solution.py:632
  43.2 1.4 %copy-done.5 = f32[3,18,56,128]{3,2,1,0:T(8,128)S(1)} copy-done((f32[3,18,56,128]{3,2,1,0:T(8,128)S(1)}, f32[3,18,56,128]{3,2,1,0:T(8,128)}, u32[]{:S(2)}) %copy-start.5) | copy-done | bytes 1548312
  44.6 1.1 %copy-done.7 = f32[22,56,128]{2,1,0:T(8,128)S(1)} copy-done((f32[22,56,128]{2,1,0:T(8,128)S(1)}, f32[22,56,128]{2,1,0:T(8,128)}, u32[]{:S(2)}) %copy-start.7) | copy-done | bytes 630808
  45.7 2.9 %collect.1 = (f32[3,16,32,128]{3,2,1,0:T(8,128)}, f32[16,32,128]{2,1,0:T(8,128)}, f32[8,16,64]{2,1,0:T(8,128)}, f32[4,8,32]{2,1,0:T(8,128)}, f32[3,16,32,128]{3,2,1,0:T(8,128)}, /*index=5*/f32[4,8,128]{2,1,0:T(8,128)S(1)}) custom-call(f32[22,56,128]{2,1,0:T(8,128)S(1)} %copy-done.7, f32[3,18,56,128]{3,2,1,0:T(8,128)S(1)} %copy-done.5, ...), custom_call_target="tpu_custom_call" | custom-call | flops 8388608 | bytes 1048576 | tf_op jit(solution)/shard_map/collect/pallas_call | solution.py:680
  48.6 0.7 collective-permute-done.9
  49.4 0.1 bitcast_select_fusion.1
  49.4 0.0 collective-permute-start.10
  49.5 1.2 %collective-permute-done.10 = f32[8,128]{1,0:T(8,128)S(1)} collective-permute-done((f32[8,128]{1,0:T(8,128)S(1)}, f32[8,128]{1,0:T(8,128)S(1)}, u32[]{:S(2)}, u32[]{:S(2)}) %collective-permute-start.10) | collective-permute-done | bytes 4128 | tf_op jit(solution)/shard_map/ppermute | solution.py:44
  50.6 0.1 bitcast_select_fusion
  50.7 1.8 %collective-permute-start.11 = (f32[8,128]{1,0:T(8,128)S(1)}, f32[8,128]{1,0:T(8,128)S(1)}, u32[]{:S(2)}, u32[]{:S(2)}) collective-permute-start(f32[8,128]{1,0:T(8,128)S(1)} %bitcast_select_fusion), channel_id=1, source_target_pairs={{0,224},{32,64},{64,32},{96,128},{128,96},{160,192},{192,160},{224... | collective-permute-start | bytes 12296 | tf_op jit(solution)/shard_map/ppermute | solution.py:49
  52.6 2.6 %collective-permute-done.11 = f32[8,128]{1,0:T(8,128)S(1)} collective-permute-done((f32[8,128]{1,0:T(8,128)S(1)}, f32[8,128]{1,0:T(8,128)S(1)}, u32[]{:S(2)}, u32[]{:S(2)}) %collective-permute-start.11) | collective-permute-done | bytes 4128 | tf_op jit(solution)/shard_map/ppermute | solution.py:49
  55.2 0.1 fusion.3
  55.2 0.1 collective-permute-start.12
  55.3 3.6 %collective-permute-done.12 = f32[2,8,128]{2,1,0:T(8,128)S(1)} collective-permute-done((f32[2,8,128]{2,1,0:T(8,128)S(1)}, f32[2,8,128]{2,1,0:T(8,128)S(1)}, u32[]{:S(2)}, u32[]{:S(2)}) %collective-permute-start.12) | collective-permute-done | bytes 8224 | tf_op jit(solution)/shard_map/ppermute | solution.py:44
  58.9 0.1 fusion.2
  59.0 1.1 %collective-permute-start.13 = (f32[2,8,128]{2,1,0:T(8,128)S(1)}, f32[2,8,128]{2,1,0:T(8,128)S(1)}, u32[]{:S(2)}, u32[]{:S(2)}) collective-permute-start(f32[2,8,128]{2,1,0:T(8,128)S(1)} %fusion.2), channel_id=1, source_target_pairs={{0,24},{8,16},{16,8},{24,0},{1,25},{9,17},{17,9},{25,1},{2,26},{10... | collective-permute-start | bytes 24584 | tf_op jit(solution)/shard_map/ppermute | solution.py:49
  60.1 3.8 %collective-permute-done.13 = f32[2,8,128]{2,1,0:T(8,128)S(1)} collective-permute-done((f32[2,8,128]{2,1,0:T(8,128)S(1)}, f32[2,8,128]{2,1,0:T(8,128)S(1)}, u32[]{:S(2)}, u32[]{:S(2)}) %collective-permute-start.13) | collective-permute-done | bytes 8224 | tf_op jit(solution)/shard_map/ppermute | solution.py:49
  63.9 0.1 broadcast_select_fusion.1
  64.0 1.3 %collective-permute-start.14 = (f32[2,8,128]{2,1,0:T(8,128)S(1)}, f32[2,8,128]{2,1,0:T(8,128)S(1)}, u32[]{:S(2)}, u32[]{:S(2)}) collective-permute-start(f32[2,8,128]{2,1,0:T(8,128)S(1)} %get-tuple-element.65), channel_id=1, source_target_pairs={{0,1},{1,0},{2,3},{3,2},{4,5},{5,4},{6,7},{7,6},{8,9},{9,8},{10,11... | collective-permute-start | bytes 24584 | tf_op jit(solution)/shard_map/ppermute | solution.py:44
  65.3 2.4 %collective-permute-done.14 = f32[2,8,128]{2,1,0:T(8,128)S(1)} collective-permute-done((f32[2,8,128]{2,1,0:T(8,128)S(1)}, f32[2,8,128]{2,1,0:T(8,128)S(1)}, u32[]{:S(2)}, u32[]{:S(2)}) %collective-permute-start.14) | collective-permute-done | bytes 8224 | tf_op jit(solution)/shard_map/ppermute | solution.py:44
  67.7 0.1 broadcast_select_fusion
  67.8 2.5 %collective-permute-start.15 = (f32[2,8,128]{2,1,0:T(8,128)S(1)}, f32[2,8,128]{2,1,0:T(8,128)S(1)}, u32[]{:S(2)}, u32[]{:S(2)}) collective-permute-start(f32[2,8,128]{2,1,0:T(8,128)S(1)} %broadcast_select_fusion), channel_id=1, source_target_pairs={{0,7},{1,2},{2,1},{3,4},{4,3},{5,6},{6,5},{7,0},{8,15},{9,10},{10,... | collective-permute-start | bytes 24584 | tf_op jit(solution)/shard_map/ppermute | solution.py:49
  70.3 2.4 %collective-permute-done.15 = f32[2,8,128]{2,1,0:T(8,128)S(1)} collective-permute-done((f32[2,8,128]{2,1,0:T(8,128)S(1)}, f32[2,8,128]{2,1,0:T(8,128)S(1)}, u32[]{:S(2)}, u32[]{:S(2)}) %collective-permute-start.15) | collective-permute-done | bytes 8224 | tf_op jit(solution)/shard_map/ppermute | solution.py:49
  72.7 0.2 fusion.5
  72.9 0.7 fusion.6
  (20 shorter events, 0.1 us)
Async XLA Ops:
  0.6 1.1 %copy-start = (f32[3,16,32,128]{3,2,1,0:T(8,128)S(1)}, f32[3,16,32,128]{3,2,1,0:T(8,128)}, u32[]{:S(2)}) copy-start(f32[3,16,32,128]{3,2,1,0:T(8,128)} %vel.5) | copy-start | bytes 2359300
  1.8 1.1 %copy-start.2 = (f32[3,16,32,128]{3,2,1,0:T(8,128)S(1)}, f32[3,16,32,128]{3,2,1,0:T(8,128)}, u32[]{:S(2)}) copy-start(f32[3,16,32,128]{3,2,1,0:T(8,128)} %forc.5) | copy-start | bytes 2359300
  2.9 0.7 copy-start.8
  3.6 10.0 %copy-start.1 = (f32[3,16,32,128]{3,2,1,0:T(8,128)S(1)}, f32[3,16,32,128]{3,2,1,0:T(8,128)}, u32[]{:S(2)}) copy-start(f32[3,16,32,128]{3,2,1,0:T(8,128)} %vel.5) | copy-start | bytes 2359300
  3.6 10.0 %copy-start.3 = (f32[3,16,32,128]{3,2,1,0:T(8,128)S(1)}, f32[3,16,32,128]{3,2,1,0:T(8,128)}, u32[]{:S(2)}) copy-start(f32[3,16,32,128]{3,2,1,0:T(8,128)} %forc.5) | copy-start | bytes 2359300
  3.7 4.8 %collective-permute-start = (f32[19,32,128]{2,1,0:T(8,128)S(1)}, f32[19,32,128]{2,1,0:T(8,128)S(1)}, u32[]{:S(2)}, u32[]{:S(2)}) collective-permute-start(f32[19,32,128]{2,1,0:T(8,128)S(1)} %get-tuple-element.36), channel_id=1, source_target_pairs={{0,32},{32,0},{64,96},{96,64},{128,160},{160,128},{192,224},{224,1... | collective-permute-start | bytes 933896 | tf_op jit(solution)/shard_map/ppermute | solution.py:44
  3.8 7.6 %collective-permute-start.1 = (f32[19,32,128]{2,1,0:T(8,128)S(1)}, f32[19,32,128]{2,1,0:T(8,128)S(1)}, u32[]{:S(2)}, u32[]{:S(2)}) collective-permute-start(f32[19,32,128]{2,1,0:T(8,128)S(1)} %get-tuple-element.37), channel_id=1, source_target_pairs={{0,224},{32,64},{64,32},{96,128},{128,96},{160,192},{192,160},{224... | collective-permute-start | bytes 933896 | tf_op jit(solution)/shard_map/ppermute | solution.py:49
  6.7 8.1 %collective-permute-start.2 = (f32[37,8,128]{2,1,0:T(8,128)S(1)}, f32[37,8,128]{2,1,0:T(8,128)S(1)}, u32[]{:S(2)}, u32[]{:S(2)}) collective-permute-start(f32[37,8,128]{2,1,0:T(8,128)S(1)} %get-tuple-element.38), channel_id=1, source_target_pairs={{0,8},{8,0},{16,24},{24,16},{1,9},{9,1},{17,25},{25,17},{2,10},{10... | collective-permute-start | bytes 454664 | tf_op jit(solution)/shard_map/ppermute | solution.py:44
  7.4 7.4 %collective-permute-start.3 = (f32[37,8,128]{2,1,0:T(8,128)S(1)}, f32[37,8,128]{2,1,0:T(8,128)S(1)}, u32[]{:S(2)}, u32[]{:S(2)}) collective-permute-start(f32[37,8,128]{2,1,0:T(8,128)S(1)} %get-tuple-element.39), channel_id=1, source_target_pairs={{0,24},{8,16},{16,8},{24,0},{1,25},{9,17},{17,9},{25,1},{2,26},{10... | collective-permute-start | bytes 454664 | tf_op jit(solution)/shard_map/ppermute | solution.py:49
  11.5 4.4 %collective-permute-start.4 = (f32[16,8,128]{2,1,0:T(8,128)S(1)}, f32[16,8,128]{2,1,0:T(8,128)S(1)}, u32[]{:S(2)}, u32[]{:S(2)}) collective-permute-start(f32[16,8,128]{2,1,0:T(8,128)S(1)} %get-tuple-element.40), channel_id=1, source_target_pairs={{0,8},{8,0},{16,24},{24,16},{1,9},{9,1},{17,25},{25,17},{2,10},{10... | collective-permute-start | bytes 196616 | tf_op jit(solution)/shard_map/ppermute | solution.py:44
  12.3 5.5 %collective-permute-start.5 = (f32[16,8,128]{2,1,0:T(8,128)S(1)}, f32[16,8,128]{2,1,0:T(8,128)S(1)}, u32[]{:S(2)}, u32[]{:S(2)}) collective-permute-start(f32[16,8,128]{2,1,0:T(8,128)S(1)} %get-tuple-element.41), channel_id=1, source_target_pairs={{0,24},{8,16},{16,8},{24,0},{1,25},{9,17},{17,9},{25,1},{2,26},{10... | collective-permute-start | bytes 196616 | tf_op jit(solution)/shard_map/ppermute | solution.py:49
  13.6 11.9 %copy-start.9 = (f32[8]{0:T(128)S(1)}, f32[8]{0:T(128)}, u32[]{:S(2)}) copy-start(f32[8]{0:T(128)} %pre.3) | copy-start | bytes 100
  13.6 11.9 %copy-start.10 = (f32[8]{0:T(128)S(1)}, f32[8]{0:T(128)}, u32[]{:S(2)}) copy-start(f32[8]{0:T(128)} %yld.3) | copy-start | bytes 100
  18.5 15.2 %collective-permute-start.6 = (f32[25,8,128]{2,1,0:T(8,128)S(1)}, f32[25,8,128]{2,1,0:T(8,128)S(1)}, u32[]{:S(2)}, u32[]{:S(2)}) collective-permute-start(f32[25,8,128]{2,1,0:T(8,128)S(1)} %get-tuple-element.47), channel_id=1, source_target_pairs={{0,1},{1,0},{2,3},{3,2},{4,5},{5,4},{6,7},{7,6},{8,9},{9,8},{10,11... | collective-permute-start | bytes 307208 | tf_op jit(solution)/shard_map/ppermute | solution.py:44
  20.5 13.2 %collective-permute-start.7 = (f32[25,8,128]{2,1,0:T(8,128)S(1)}, f32[25,8,128]{2,1,0:T(8,128)S(1)}, u32[]{:S(2)}, u32[]{:S(2)}) collective-permute-start(f32[25,8,128]{2,1,0:T(8,128)S(1)} %get-tuple-element.48), channel_id=1, source_target_pairs={{0,7},{1,2},{2,1},{3,4},{4,3},{5,6},{6,5},{7,0},{8,15},{9,10},{10,... | collective-permute-start | bytes 307208 | tf_op jit(solution)/shard_map/ppermute | solution.py:49
  32.5 1.2 %copy-start.4 = (f32[3,18,56,128]{3,2,1,0:T(8,128)}, f32[3,18,56,128]{3,2,1,0:T(8,128)S(1)}, u32[]{:S(2)}) copy-start(f32[3,18,56,128]{3,2,1,0:T(8,128)S(1)} %get-tuple-element.43.u2) | copy-start | bytes 4644868
  33.7 3.1 %copy-start.6 = (f32[22,56,128]{2,1,0:T(8,128)}, f32[22,56,128]{2,1,0:T(8,128)S(1)}, u32[]{:S(2)}) copy-start(f32[22,56,128]{2,1,0:T(8,128)S(1)} %get-tuple-element.42.v_ref) | copy-start | bytes 1892356
  36.8 5.1 %collective-permute-start.8 = (f32[1,128]{1,0:T(1,128)S(1)}, f32[1,128]{1,0:T(1,128)S(1)}, u32[]{:S(2)}, u32[]{:S(2)}) collective-permute-start(f32[1,128]{1,0:T(1,128)S(1)} %get-tuple-element.61), channel_id=1, source_target_pairs={{0,128},{32,160},{64,192},{96,224},{128,0},{160,32},{192,64},{224,... | collective-permute-start | bytes 1544 | tf_op jit(solution)/shard_map/ppermute | solution.py:632
  41.9 7.5 %collective-permute-start.9 = (f32[1,128]{1,0:T(1,128)S(1)}, f32[1,128]{1,0:T(1,128)S(1)}, u32[]{:S(2)}, u32[]{:S(2)}) collective-permute-start(f32[1,128]{1,0:T(1,128)S(1)} %add.50), channel_id=1, source_target_pairs={{0,4},{1,5},{2,6},{3,7},{4,0},{5,1},{6,2},{7,3},{8,12},{9,13},{10,... | collective-permute-start | bytes 1544 | tf_op jit(solution)/shard_map/ppermute | solution.py:632
  43.2 1.4 %copy-start.5 = (f32[3,18,56,128]{3,2,1,0:T(8,128)S(1)}, f32[3,18,56,128]{3,2,1,0:T(8,128)}, u32[]{:S(2)}) copy-start(f32[3,18,56,128]{3,2,1,0:T(8,128)} %copy-done.4) | copy-start | bytes 4644868
  44.6 1.1 %copy-start.7 = (f32[22,56,128]{2,1,0:T(8,128)S(1)}, f32[22,56,128]{2,1,0:T(8,128)}, u32[]{:S(2)}) copy-start(f32[22,56,128]{2,1,0:T(8,128)} %copy-done.6) | copy-start | bytes 1892356
  49.4 1.2 %collective-permute-start.10 = (f32[8,128]{1,0:T(8,128)S(1)}, f32[8,128]{1,0:T(8,128)S(1)}, u32[]{:S(2)}, u32[]{:S(2)}) collective-permute-start(f32[8,128]{1,0:T(8,128)S(1)} %bitcast_select_fusion.1), channel_id=1, source_target_pairs={{0,32},{32,0},{64,96},{96,64},{128,160},{160,128},{192,224},{224,1... | collective-permute-start | bytes 12296 | tf_op jit(solution)/shard_map/ppermute | solution.py:44
  50.7 4.4 %collective-permute-start.11 = (f32[8,128]{1,0:T(8,128)S(1)}, f32[8,128]{1,0:T(8,128)S(1)}, u32[]{:S(2)}, u32[]{:S(2)}) collective-permute-start(f32[8,128]{1,0:T(8,128)S(1)} %bitcast_select_fusion), channel_id=1, source_target_pairs={{0,224},{32,64},{64,32},{96,128},{128,96},{160,192},{192,160},{224... | collective-permute-start | bytes 12296 | tf_op jit(solution)/shard_map/ppermute | solution.py:49
  55.2 3.7 %collective-permute-start.12 = (f32[2,8,128]{2,1,0:T(8,128)S(1)}, f32[2,8,128]{2,1,0:T(8,128)S(1)}, u32[]{:S(2)}, u32[]{:S(2)}) collective-permute-start(f32[2,8,128]{2,1,0:T(8,128)S(1)} %fusion.3), channel_id=1, source_target_pairs={{0,8},{8,0},{16,24},{24,16},{1,9},{9,1},{17,25},{25,17},{2,10},{10... | collective-permute-start | bytes 24584 | tf_op jit(solution)/shard_map/ppermute | solution.py:44
  59.0 4.9 %collective-permute-start.13 = (f32[2,8,128]{2,1,0:T(8,128)S(1)}, f32[2,8,128]{2,1,0:T(8,128)S(1)}, u32[]{:S(2)}, u32[]{:S(2)}) collective-permute-start(f32[2,8,128]{2,1,0:T(8,128)S(1)} %fusion.2), channel_id=1, source_target_pairs={{0,24},{8,16},{16,8},{24,0},{1,25},{9,17},{17,9},{25,1},{2,26},{10... | collective-permute-start | bytes 24584 | tf_op jit(solution)/shard_map/ppermute | solution.py:49
  64.0 3.7 %collective-permute-start.14 = (f32[2,8,128]{2,1,0:T(8,128)S(1)}, f32[2,8,128]{2,1,0:T(8,128)S(1)}, u32[]{:S(2)}, u32[]{:S(2)}) collective-permute-start(f32[2,8,128]{2,1,0:T(8,128)S(1)} %get-tuple-element.65), channel_id=1, source_target_pairs={{0,1},{1,0},{2,3},{3,2},{4,5},{5,4},{6,7},{7,6},{8,9},{9,8},{10,11... | collective-permute-start | bytes 24584 | tf_op jit(solution)/shard_map/ppermute | solution.py:44
  67.8 4.9 %collective-permute-start.15 = (f32[2,8,128]{2,1,0:T(8,128)S(1)}, f32[2,8,128]{2,1,0:T(8,128)S(1)}, u32[]{:S(2)}, u32[]{:S(2)}) collective-permute-start(f32[2,8,128]{2,1,0:T(8,128)S(1)} %broadcast_select_fusion), channel_id=1, source_target_pairs={{0,7},{1,2},{2,1},{3,4},{4,3},{5,6},{6,5},{7,0},{8,15},{9,10},{10,... | collective-permute-start | bytes 24584 | tf_op jit(solution)/shard_map/ppermute | solution.py:49

commit v4 on v3

--- a/solution.py
+++ b/solution.py
@@ -12,7 +12,8 @@
 AX = ("gx", "gy", "gz")
 NX, NY, NZ = 16, 32, 128
 VMEM = pl.BlockSpec(memory_space=pltpu.VMEM)
-LIM = 8
+HBM = pl.BlockSpec(memory_space=pltpu.HBM)
+LIM = 9
 SMEM = pl.BlockSpec(memory_space=pltpu.SMEM)
 
 
@@ -93,25 +94,36 @@
     put_pair(pair, "gy", index, lo, hi)
 
 
-def pack_xy(vel, forc, blocks, send_a, send_b, own_a, own_b, phase):
+def pack_xy(vel, forc, blocks_in, send_a, send_b, own_a, own_b, phase, blocks, vel_y, forc_y, sems):
     even, _, _ = position("gx")
+    pairs = [(blocks_in, blocks)]
+    for k in range(2):
+        pairs.append((vel.at[:, :, 24 * k : 24 * k + 8], vel_y.at[k]))
+        pairs.append((forc.at[:, :, 24 * k : 24 * k + 8], forc_y.at[k]))
+    for out, first in ((send_a, jnp.where(even, 1, 0)), (send_b, jnp.where(even, 0, 1))):
+        for c in range(3):
+            pairs.append((vel.at[c, pl.ds(12 * first, 4)], out.at[4 * c : 4 * c + 4]))
+            pairs.append((forc.at[c, pl.ds(14 * first, 2)], out.at[12 + 2 * c : 14 + 2 * c]))
+    copies = [pltpu.make_async_copy(source, target, sems.at[k]) for k, (source, target) in enumerate(pairs)]
+    for copy in copies:
+        copy.start()
     phase[...] = jnp.zeros(phase.shape, F32)
+    copies[0].wait()
     for b in range(4):
         phase[b, :, 0:32] = blocks[b].astype(F32)
-    for out, first in ((send_a, jnp.where(even, 1, 0)), (send_b, jnp.where(even, 0, 1))):
-        for c in range(3):
-            for i in range(4):
-                out[4 * c + i] = vel[c, 12 * first + i]
-            for i in range(2):
-                out[12 + 2 * c + i] = forc[c, 14 * first + i]
-        out[18, 0:8] = phase[3 * first]
+    send_a[18, 0:8] = jnp.where(even, phase[3], phase[0])
+    send_b[18, 0:8] = jnp.where(even, phase[0], phase[3])
+    for copy in copies[1:5]:
+        copy.wait()
     pair = (own_a, own_b)
     for c in range(3):
         for g in range(8):
-            pack_rows4(pair, 8 * c + g, lambda p, o: vel[c, p, 8 * o : 8 * o + 8], g, g + 8)
+            pack_rows4(pair, 8 * c + g, lambda p, o: vel_y[o // 3, c, p], g, g + 8)
         for g in range(4):
-            pack_rows2(pair, 24 + 4 * c + g, lambda p, o: forc[c, p, 8 * o : 8 * o + 8], [g + 4 * k for k in range(4)])
+            pack_rows2(pair, 24 + 4 * c + g, lambda p, o: forc_y[o // 3, c, p], [g + 4 * k for k in range(4)])
     pack_phase(pair, 36, [phase[b] for b in range(4)])
+    for copy in copies[5:]:
+        copy.wait()
 
 
 def pack_y(rx_a, rx_b, corner_a, corner_b):
@@ -323,8 +335,8 @@
 
 def main_work(
     vel, forc, phase_ref, rx_a, rx_b, ryo_a, ryo_b, ryc_a, ryc_b, pre, yld,
-    v_ref, u2, residual, square,
-    u_ref, f_ref, creep, limit, u1,
+    v_own, u_own, residual, square,
+    u_ref, f_ref, creep, limit, v_ref, u1, u2, sems,
 ):
     rx, ry = (rx_a, rx_b), ((ryo_a, ryo_b), (ryc_a, ryc_b))
     lo_x, hi_x = flags("gx")
@@ -348,10 +360,13 @@
                 lambda c, dx, dy: u_ref[c, vx + 1 + dx, 8 + 8 * o + dy : 16 + 8 * o + dy],
                 creep[bx, 8 * o : 8 * o + 8], limit[bx, 8 * o : 8 * o + 8],
             )
-            put_rows(v_ref, (vx,), o, value * (mask_y * mask_x if o == 4 else mask_x))
+            value = value * (mask_y * mask_x if o == 4 else mask_x)
+            put_rows(v_ref, (vx,), o, value)
         return 0
 
     lax.fori_loop(0, 22, viscosity, 0, unroll=2)
+    copy_v = pltpu.make_async_copy(v_ref.at[:, 8:48], v_own, sems.at[0])
+    copy_v.start()
 
     def sweep(source, target, first, first_u):
         def body(x, _):
@@ -366,8 +381,10 @@
 
         return body
 
-    lax.fori_loop(0, 20, sweep(u_ref, u1, 1, 2), 0, unroll=2)
-    lax.fori_loop(0, 18, sweep(u1, u2, 2, 1), 0, unroll=2)
+    lax.fori_loop(0, 20, sweep(u_ref, u1, 1, 2), 0, unroll=4)
+    lax.fori_loop(0, 18, sweep(u1, u2, 2, 1), 0, unroll=3)
+    copy_u = pltpu.make_async_copy(u2.at[:, 1:17, 8:40], u_own, sems.at[1])
+    copy_u.start()
 
     def last(x, acc):
         for o in range(4):
@@ -379,9 +396,11 @@
                 acc = acc + value * value
         return acc
 
-    acc = lax.fori_loop(0, NX, last, jnp.zeros((8, 128), F32), unroll=2)
+    acc = lax.fori_loop(0, NX, last, jnp.zeros((8, 128), F32), unroll=4)
     lane = lanes()
     square[...] = jnp.where((lane >= 4) & (lane < 124), acc, 0.0)
+    copy_v.wait()
+    copy_u.wait()
 
 
 def put_edge(ref, index, i, o, value):
@@ -457,7 +476,7 @@
             v_out[i, 8 * o : 8 * o + 8] = value
         return 0
 
-    lax.fori_loop(0, 6, viscosity, 0, unroll=3)
+    lax.fori_loop(0, 6, viscosity, 0, unroll=6)
     wrap_planes(v_ref, ((),))
 
     def sweep(source, target):
@@ -471,7 +490,7 @@
                     put_edge(target, (c,), i, o, 0.2 * mid + rate * (2.0 * force + total))
             return 0
 
-        lax.fori_loop(0, 6, body, 0, unroll=3)
+        lax.fori_loop(0, 6, body, 0, unroll=6)
         wrap_planes(target, lead)
 
     sweep(u_ref, u1)
@@ -490,7 +509,7 @@
                 acc = acc + jnp.where(count, value * value, 0.0)
         return acc
 
-    acc = lax.fori_loop(0, 6, last, square[...], unroll=3)
+    acc = lax.fori_loop(0, 6, last, square[...], unroll=6)
     total = jnp.sum(jnp.sum(acc, axis=1, keepdims=True), axis=0, keepdims=True)
     total_out[...] = jnp.broadcast_to(total, (1, 128))
 
@@ -509,7 +528,7 @@
 
 
 def collect(
-    v_ref, u2, residual_in, ve, ue, re,
+    v_own, u_own, residual_in, ve, ue, re,
     smoothed, visc_out, one_out, two_out, residual, partial,
     v_m, v_s, w_m, w_s, y1, c1, t2, t3,
 ):
@@ -521,7 +540,7 @@
         g, i = (vx + 1) // 6, (vx + 1) % 6
         for o in range(5):
             edge = ve[i, 8 * o : 8 * o + 8]
-            value = merge(v_ref[vx, 8 + 8 * o : 16 + 8 * o], edge, g)
+            value = merge(v_own[vx, 8 * o : 8 * o + 8], edge, g)
             put_rows(v_m, (vx,), o, value)
             side = jnp.where(lane < 4, roll(edge, -28 - 32 * g, 1), 0.0)
             put_rows(v_s, (vx,), o, jnp.where(lane >= 124, roll(edge, 124 - 32 * g, 1), side))
@@ -532,7 +551,7 @@
         for c in range(3):
             for o in range(4):
                 rows = slice(8 * o, 8 * o + 8)
-                smoothed[c, x, rows] = merge(u2[c, x + 1, 8 + 8 * o : 16 + 8 * o], ue[c, i, rows], g)
+                smoothed[c, x, rows] = merge(u_own[c, x, rows], ue[c, i, rows], g)
                 residual[c, x, rows] = merge(residual_in[c, x, rows], re[c, i, rows], g)
 
     def coarse_x(k, _):
@@ -635,8 +654,13 @@
 def per_device(velocity, forcing, phase_block, prefactor, yield_stress):
     send_a, send_b, own_a, own_b, phase = pl.pallas_call(
         pack_xy, out_shape=[sds(19, 32, 128)] * 2 + [sds(37, 8, 128)] * 2 + [sds(4, 8, 128)],
-        in_specs=[VMEM] * 3, out_specs=[VMEM] * 5, compiler_params=params(LIM), name="pack_xy",
-    )(velocity, forcing, phase_block)
+        in_specs=[HBM] * 3, out_specs=[VMEM] * 5,
+        scratch_shapes=[
+            pltpu.VMEM((4, 8, 32), jnp.int32), pltpu.VMEM((2, 3, 16, 8, 128), F32),
+            pltpu.VMEM((2, 3, 16, 8, 128), F32), pltpu.SemaphoreType.DMA((17,)),
+        ],
+        compiler_params=params(LIM), name="pack_xy",
+    )(*(pltpu.with_memory_space_constraint(value, pltpu.HBM) for value in (velocity, forcing, phase_block)))
     own = (velocity, forcing, phase)
     rx = (pair_a(send_a, "gx"), pair_b(send_b, "gx"))
     ry = (pair_a(own_a, "gy"), pair_b(own_b, "gy"))
@@ -656,11 +680,12 @@
     rz = (pair_a(send_a, "gz"), pair_b(send_b, "gz"))
     v, u2, res, square = pl.pallas_call(
         main_work,
-        out_shape=[sds(22, 56, 128), sds(3, 18, 56, 128), sds(3, NX, NY, NZ), sds(8, 128)],
-        in_specs=[VMEM] * 9 + [SMEM] * 2, out_specs=[VMEM] * 4,
+        out_shape=[pltpu.HBM((22, 40, 128), F32), pltpu.HBM((3, NX, NY, NZ), F32), sds(3, NX, NY, NZ), sds(8, 128)],
+        in_specs=[VMEM] * 9 + [SMEM] * 2, out_specs=[HBM] * 2 + [VMEM] * 2,
         scratch_shapes=[
             pltpu.VMEM((3, 24, 56, 128), F32), pltpu.VMEM((3, 20, 40, 128), F32),
-            pltpu.VMEM((6, 40, 128), F32), pltpu.VMEM((6, 40, 128), F32), pltpu.VMEM((3, 20, 56, 128), F32),
+            pltpu.VMEM((6, 40, 128), F32), pltpu.VMEM((6, 40, 128), F32), pltpu.VMEM((22, 56, 128), F32),
+            pltpu.VMEM((3, 20, 56, 128), F32), pltpu.VMEM((3, 18, 56, 128), F32), pltpu.SemaphoreType.DMA((2,)),
         ],
         compiler_params=params(LIM), cost_estimate=cost(1 << 25), name="main_work",
     )(*own, *rx, *ry, prefactor, yield_stress)

time: 75 us -> 70.8 us (0.944)
  local copies, waits for them, and re-layouts: 6.65 us -> 1.05 us
  waiting for transfers between devices: 25.6 us -> 29.2 us
  starting transfers between devices: 24.1 us -> 21.8 us
    unnamed x22 -> x12, local copies, waits for them, and re-layouts: 6.64 us -> 1.04 us
    ppermute x7, starting transfers between devices: 15.6 us -> 13.9 us  [pair_b(): lax.ppermute(value, axis, [(i, (i + 1) % count if i % 2 else (i - 1) % co...]
    pallas_call x1, Pallas kernels: 0.09 us -> 1.62 us  [per_device(): pl.pallas_call(pack_xy, out_shape=[sds(19, 32, 128)] * 2 + [sds(37, 8, 12...]
    ppermute x7, waiting for transfers between devices: 13.7 us -> 15.1 us  [pair_b(): lax.ppermute(value, axis, [(i, (i + 1) % count if i % 2 else (i - 1) % co...]
    ppermute x7, starting transfers between devices: 5.11 us -> 3.83 us  [pair_a(): return lax.ppermute(value, axis, [(i, i ^ 1) for i in range(count)])]
    ppermute x7, waiting for transfers between devices: 8.11 us -> 9.38 us  [pair_a(): return lax.ppermute(value, axis, [(i, i ^ 1) for i in range(count)])]
    ppermute x2, waiting for transfers between devices: 3.84 us -> 4.66 us  [far(): lax.ppermute(total, axis, [(i, (i + count // 2) % count) for i in range(c...]
    pallas_call x1, Pallas kernels: 7.05 us -> 6.26 us  [per_device(): pl.pallas_call(main_work, out_shape=[pltpu.HBM((22, 40, 128), F32), pltpu...]
where the time goes in v4:
time: 70.8 us; the launch traced here: 70.7 us
  waiting for transfers between devices  29.2 us (41%)
  starting transfers between devices  21.8 us (31%)
  Pallas kernels  15.3 us (22%)
  between operations  2.01 us (3%)
  other arithmetic  1.36 us (2%)
  local copies, waits for them, and re-layouts  1.05 us (1%)
    ppermute x7, waiting for transfers between devices, pair_b(): lax.ppermute(value, axis, [(i, (i + 1) % count if i % 2 else (i - 1) % co...  15.1 us
    ppermute x7, starting transfers between devices, pair_b(): lax.ppermute(value, axis, [(i, (i + 1) % count if i % 2 else (i - 1) % co...  13.9 us
    ppermute x7, waiting for transfers between devices, pair_a(): return lax.ppermute(value, axis, [(i, i ^ 1) for i in range(count)])  9.38 us
    pallas_call x1, Pallas kernels, per_device(): pl.pallas_call(main_work, out_shape=[pltpu.HBM((22, 40, 128), F32), pltpu...  6.26 us
    ppermute x2, waiting for transfers between devices, far(): lax.ppermute(total, axis, [(i, (i + count // 2) % count) for i in range(c...  4.66 us
    ppermute x2, starting transfers between devices, far(): lax.ppermute(total, axis, [(i, (i + count // 2) % count) for i in range(c...  3.97 us
    ppermute x7, starting transfers between devices, pair_a(): return lax.ppermute(value, axis, [(i, i ^ 1) for i in range(count)])  3.83 us
    pallas_call x1, Pallas kernels, per_device(): pl.pallas_call(collect, out_shape=[sds(3, NX, NY, NZ), sds(NX, NY, NZ), s...  2.91 us
  transfers between devices with their start and end apart: 16, of which 11 were waited for; matrix products, arithmetic and copies ran while one was open for 0% of the time, Pallas kernels for 15%

profile of v4, /device:TPU:24, one launch (start us, length us, event | category | flops | bytes accessed | tf_op | source)
XLA Modules:
  0.0 70.7 jit_solution(6314137041301953500)
XLA Ops:
  0.6 0.0 copy-start
  0.6 0.0 copy-start.1
  0.7 1.6 %pack_xy.1 = (f32[19,32,128]{2,1,0:T(8,128)S(1)}, f32[19,32,128]{2,1,0:T(8,128)S(1)}, f32[37,8,128]{2,1,0:T(8,128)S(1)}, f32[37,8,128]{2,1,0:T(8,128)S(1)}, f32[4,8,128]{2,1,0:T(8,128)S(1)}) custom-call(f32[3,16,32,128]{3,2,1,0:T(8,128)} %vel.5, f32[3,16,32,128]{3,2,1,0:T(8,128)} %forc.5, s32[4,8,32]{2,1,0:T(8,128)} %blocks_in.1), custom_call_target="tpu_custom_call" | custom-call | tf_op jit(solution)/shard_map/pack_xy/pallas_call | solution.py:655
  2.3 0.1 collective-permute-start
  2.4 2.9 %collective-permute-start.1 = (f32[19,32,128]{2,1,0:T(8,128)S(1)}, f32[19,32,128]{2,1,0:T(8,128)S(1)}, u32[]{:S(2)}, u32[]{:S(2)}) collective-permute-start(f32[19,32,128]{2,1,0:T(8,128)S(1)} %get-tuple-element.37), channel_id=1, source_target_pairs={{0,224},{32,64},{64,32},{96,128},{128,96},{160,192},{192,160},{224... | collective-permute-start | bytes 933896 | tf_op jit(solution)/shard_map/ppermute | solution.py:50
  5.2 0.7 %collective-permute-start.2 = (f32[37,8,128]{2,1,0:T(8,128)S(1)}, f32[37,8,128]{2,1,0:T(8,128)S(1)}, u32[]{:S(2)}, u32[]{:S(2)}) collective-permute-start(f32[37,8,128]{2,1,0:T(8,128)S(1)} %get-tuple-element.38), channel_id=1, source_target_pairs={{0,8},{8,0},{16,24},{24,16},{1,9},{9,1},{17,25},{25,17},{2,10},{10... | collective-permute-start | bytes 454664 | tf_op jit(solution)/shard_map/ppermute | solution.py:45
  6.0 1.1 %collective-permute-start.3 = (f32[37,8,128]{2,1,0:T(8,128)S(1)}, f32[37,8,128]{2,1,0:T(8,128)S(1)}, u32[]{:S(2)}, u32[]{:S(2)}) collective-permute-start(f32[37,8,128]{2,1,0:T(8,128)S(1)} %get-tuple-element.39), channel_id=1, source_target_pairs={{0,24},{8,16},{16,8},{24,0},{1,25},{9,17},{17,9},{25,1},{2,26},{10... | collective-permute-start | bytes 454664 | tf_op jit(solution)/shard_map/ppermute | solution.py:50
  7.0 0.0 collective-permute-done.rx_a
  7.0 3.0 %collective-permute-done.1.rx_b = f32[19,32,128]{2,1,0:T(8,128)S(1)} collective-permute-done((f32[19,32,128]{2,1,0:T(8,128)S(1)}, f32[19,32,128]{2,1,0:T(8,128)S(1)}, u32[]{:S(2)}, u32[]{:S(2)}) %collective-permute-start.1) | collective-permute-done | bytes 311328 | tf_op jit(solution)/shard_map/ppermute | solution.py:50
  10.1 0.8 %collective-permute-start.4 = (f32[16,8,128]{2,1,0:T(8,128)S(1)}, f32[16,8,128]{2,1,0:T(8,128)S(1)}, u32[]{:S(2)}, u32[]{:S(2)}) collective-permute-start(f32[16,8,128]{2,1,0:T(8,128)S(1)} %get-tuple-element.40), channel_id=1, source_target_pairs={{0,8},{8,0},{16,24},{24,16},{1,9},{9,1},{17,25},{25,17},{2,10},{10... | collective-permute-start | bytes 196616 | tf_op jit(solution)/shard_map/ppermute | solution.py:45
  10.9 1.3 %collective-permute-start.5 = (f32[16,8,128]{2,1,0:T(8,128)S(1)}, f32[16,8,128]{2,1,0:T(8,128)S(1)}, u32[]{:S(2)}, u32[]{:S(2)}) collective-permute-start(f32[16,8,128]{2,1,0:T(8,128)S(1)} %get-tuple-element.41), channel_id=1, source_target_pairs={{0,24},{8,16},{16,8},{24,0},{1,25},{9,17},{17,9},{25,1},{2,26},{10... | collective-permute-start | bytes 196616 | tf_op jit(solution)/shard_map/ppermute | solution.py:50
  12.2 0.0 copy-done
  12.2 0.0 copy-done.1
  12.2 1.2 %edge_own.1 = (f32[3,6,32,128]{3,2,1,0:T(8,128)S(1)}, f32[3,6,32,128]{3,2,1,0:T(8,128)S(1)}) custom-call(f32[3,16,32,128]{3,2,1,0:T(8,128)S(1)} %copy-done, f32[3,16,32,128]{3,2,1,0:T(8,128)S(1)} %copy-done.1, f32[19,32,128]{2,1,0:T(8,128)S(1)} %collective-permute-done.rx_a, f32[19,32,128]{2,1,0:T(8,128)S(1)} %collective-permute-done.1.rx_b), custom_call_target="tpu_custom_call" | custom-call | flops 25165824 | bytes 1048576 | tf_op jit(solution)/shard_map/edge_own/pallas_call | solution.py:672
  13.4 0.0 collective-permute-done.2.ryo_a
  13.4 0.0 collective-permute-done.3.ryo_b
  13.4 1.0 %collective-permute-done.4.ryc_a = f32[16,8,128]{2,1,0:T(8,128)S(1)} collective-permute-done((f32[16,8,128]{2,1,0:T(8,128)S(1)}, f32[16,8,128]{2,1,0:T(8,128)S(1)}, u32[]{:S(2)}, u32[]{:S(2)}) %collective-permute-start.4) | collective-permute-done | bytes 65568 | tf_op jit(solution)/shard_map/ppermute | solution.py:45
  14.4 2.0 %collective-permute-done.5.ryc_b = f32[16,8,128]{2,1,0:T(8,128)S(1)} collective-permute-done((f32[16,8,128]{2,1,0:T(8,128)S(1)}, f32[16,8,128]{2,1,0:T(8,128)S(1)}, u32[]{:S(2)}, u32[]{:S(2)}) %collective-permute-start.5) | collective-permute-done | bytes 65568 | tf_op jit(solution)/shard_map/ppermute | solution.py:50
  16.4 0.7 %pack_z.1 = (f32[25,8,128]{2,1,0:T(8,128)S(1)}, f32[25,8,128]{2,1,0:T(8,128)S(1)}, f32[3,6,8,128]{3,2,1,0:T(8,128)S(1)}, f32[3,6,8,128]{3,2,1,0:T(8,128)S(1)}, f32[12,8,128]{2,1,0:T(8,128)S(1)}) custom-call(f32[4,8,128]{2,1,0:T(8,128)S(1)} %get-tuple-element.35.phase_ref.phase, f32[19,32,128]{2,1,0:T(8,128)S(1)} %collective-permute-done.rx_a, ...), custom_call_target="tpu_custom_call" | custom-call | tf_op jit(solution)/shard_map/pack_z/pallas_call | solution.py:676
  17.1 2.0 %collective-permute-start.6 = (f32[25,8,128]{2,1,0:T(8,128)S(1)}, f32[25,8,128]{2,1,0:T(8,128)S(1)}, u32[]{:S(2)}, u32[]{:S(2)}) collective-permute-start(f32[25,8,128]{2,1,0:T(8,128)S(1)} %get-tuple-element.47), channel_id=1, source_target_pairs={{0,1},{1,0},{2,3},{3,2},{4,5},{5,4},{6,7},{7,6},{8,9},{9,8},{10,11... | collective-permute-start | bytes 307208 | tf_op jit(solution)/shard_map/ppermute | solution.py:45
  19.1 0.0 copy-start.4
  19.1 0.0 copy-start.5
  19.1 4.9 %collective-permute-start.7 = (f32[25,8,128]{2,1,0:T(8,128)S(1)}, f32[25,8,128]{2,1,0:T(8,128)S(1)}, u32[]{:S(2)}, u32[]{:S(2)}) collective-permute-start(f32[25,8,128]{2,1,0:T(8,128)S(1)} %get-tuple-element.48), channel_id=1, source_target_pairs={{0,7},{1,2},{2,1},{3,4},{4,3},{5,6},{6,5},{7,0},{8,15},{9,10},{10,... | collective-permute-start | bytes 307208 | tf_op jit(solution)/shard_map/ppermute | solution.py:50
  24.0 0.0 copy-done.4
  24.0 0.0 copy-done.5
  24.0 6.3 %main_work.1 = (f32[22,40,128]{2,1,0:T(8,128)}, f32[3,16,32,128]{3,2,1,0:T(8,128)}, f32[3,16,32,128]{3,2,1,0:T(8,128)S(1)}, f32[8,128]{1,0:T(8,128)S(1)}) custom-call(f32[3,16,32,128]{3,2,1,0:T(8,128)S(1)} %copy-done, f32[3,16,32,128]{3,2,1,0:T(8,128)S(1)} %copy-done.1, f32[4,8,128]{2,1,0:T(8,128)S(1)} %get-tuple-element.35.phase_ref.phase, ...), custom_call_target="tpu_custom_call" | custom-call | flops 33554432 | bytes 1048576 | tf_op jit(solution)/shard_map/main_work/pallas_call | solution.py:681
  30.3 0.0 copy-start.2
  30.3 0.0 collective-permute-done.6.rz_a
  30.3 0.0 collective-permute-done.7.rz_b
  30.3 2.6 %edge_work.1 = (f32[6,40,128]{2,1,0:T(8,128)S(1)}, f32[3,6,32,128]{3,2,1,0:T(8,128)S(1)}, f32[3,6,32,128]{3,2,1,0:T(8,128)S(1)}, f32[1,128]{1,0:T(1,128)S(1)}) custom-call(f32[25,8,128]{2,1,0:T(8,128)S(1)} %collective-permute-done.6.rz_a, f32[25,8,128]{2,1,0:T(8,128)S(1)} %collective-permute-done.7.rz_b, f32[3,6,32,128]{3,2,1,0:T(8,128)S(1)} %get-tuple-element.45.eu, ...), custom_call_target="tpu_custom_call" | custom-call | flops 8388608 | bytes 1048576 | tf_op jit(solution)/shard_map/edge_work/pallas_call | solution.py:692
  32.9 2.0 %collective-permute-start.8 = (f32[1,128]{1,0:T(1,128)S(1)}, f32[1,128]{1,0:T(1,128)S(1)}, u32[]{:S(2)}, u32[]{:S(2)}) collective-permute-start(f32[1,128]{1,0:T(1,128)S(1)} %get-tuple-element.61), channel_id=1, source_target_pairs={{0,128},{32,160},{64,192},{96,224},{128,0},{160,32},{192,64},{224,... | collective-permute-start | bytes 1544 | tf_op jit(solution)/shard_map/ppermute | solution.py:651
  34.9 3.1 %collective-permute-done.8 = f32[1,128]{1,0:T(1,128)S(1)} collective-permute-done((f32[1,128]{1,0:T(1,128)S(1)}, f32[1,128]{1,0:T(1,128)S(1)}, u32[]{:S(2)}, u32[]{:S(2)}) %collective-permute-start.8) | collective-permute-done | bytes 544 | tf_op jit(solution)/shard_map/ppermute | solution.py:651
  38.0 2.0 %collective-permute-start.9 = (f32[1,128]{1,0:T(1,128)S(1)}, f32[1,128]{1,0:T(1,128)S(1)}, u32[]{:S(2)}, u32[]{:S(2)}) collective-permute-start(f32[1,128]{1,0:T(1,128)S(1)} %add.50), channel_id=1, source_target_pairs={{0,4},{1,5},{2,6},{3,7},{4,0},{5,1},{6,2},{7,3},{8,12},{9,13},{10,... | collective-permute-start | bytes 1544 | tf_op jit(solution)/shard_map/ppermute | solution.py:651
  40.0 0.0 copy-done.2
  40.0 0.0 copy-start.3
  40.0 1.0 %copy-done.3 = f32[22,40,128]{2,1,0:T(8,128)S(1)} copy-done((f32[22,40,128]{2,1,0:T(8,128)S(1)}, f32[22,40,128]{2,1,0:T(8,128)}, u32[]{:S(2)}) %copy-start.3) | copy-done | bytes 450584
  41.0 2.9 %collect.1 = (f32[3,16,32,128]{3,2,1,0:T(8,128)}, f32[16,32,128]{2,1,0:T(8,128)}, f32[8,16,64]{2,1,0:T(8,128)}, f32[4,8,32]{2,1,0:T(8,128)}, f32[3,16,32,128]{3,2,1,0:T(8,128)}, /*index=5*/f32[4,8,128]{2,1,0:T(8,128)S(1)}) custom-call(f32[22,40,128]{2,1,0:T(8,128)S(1)} %copy-done.3, f32[3,16,32,128]{3,2,1,0:T(8,128)S(1)} %copy-done.2, ...), custom_call_target="tpu_custom_call" | custom-call | flops 8388608 | bytes 1048576 | tf_op jit(solution)/shard_map/collect/pallas_call | solution.py:705
  44.0 1.6 %collective-permute-done.9 = f32[1,128]{1,0:T(1,128)S(1)} collective-permute-done((f32[1,128]{1,0:T(1,128)S(1)}, f32[1,128]{1,0:T(1,128)S(1)}, u32[]{:S(2)}, u32[]{:S(2)}) %collective-permute-start.9) | collective-permute-done | bytes 544 | tf_op jit(solution)/shard_map/ppermute | solution.py:651
  45.5 0.1 bitcast_select_fusion.1
  45.6 0.0 collective-permute-start.10
  45.6 1.2 %collective-permute-done.10 = f32[8,128]{1,0:T(8,128)S(1)} collective-permute-done((f32[8,128]{1,0:T(8,128)S(1)}, f32[8,128]{1,0:T(8,128)S(1)}, u32[]{:S(2)}, u32[]{:S(2)}) %collective-permute-start.10) | collective-permute-done | bytes 4128 | tf_op jit(solution)/shard_map/ppermute | solution.py:45
  46.8 0.1 bitcast_select_fusion
  46.9 1.7 %collective-permute-start.11 = (f32[8,128]{1,0:T(8,128)S(1)}, f32[8,128]{1,0:T(8,128)S(1)}, u32[]{:S(2)}, u32[]{:S(2)}) collective-permute-start(f32[8,128]{1,0:T(8,128)S(1)} %bitcast_select_fusion), channel_id=1, source_target_pairs={{0,224},{32,64},{64,32},{96,128},{128,96},{160,192},{192,160},{224... | collective-permute-start | bytes 12296 | tf_op jit(solution)/shard_map/ppermute | solution.py:50
  48.5 2.6 %collective-permute-done.11 = f32[8,128]{1,0:T(8,128)S(1)} collective-permute-done((f32[8,128]{1,0:T(8,128)S(1)}, f32[8,128]{1,0:T(8,128)S(1)}, u32[]{:S(2)}, u32[]{:S(2)}) %collective-permute-start.11) | collective-permute-done | bytes 4128 | tf_op jit(solution)/shard_map/ppermute | solution.py:50
  51.1 0.1 fusion.3
  51.2 0.1 collective-permute-start.12
  51.3 3.6 %collective-permute-done.12 = f32[2,8,128]{2,1,0:T(8,128)S(1)} collective-permute-done((f32[2,8,128]{2,1,0:T(8,128)S(1)}, f32[2,8,128]{2,1,0:T(8,128)S(1)}, u32[]{:S(2)}, u32[]{:S(2)}) %collective-permute-start.12) | collective-permute-done | bytes 8224 | tf_op jit(solution)/shard_map/ppermute | solution.py:45
  54.9 0.1 fusion.2
  55.0 1.1 %collective-permute-start.13 = (f32[2,8,128]{2,1,0:T(8,128)S(1)}, f32[2,8,128]{2,1,0:T(8,128)S(1)}, u32[]{:S(2)}, u32[]{:S(2)}) collective-permute-start(f32[2,8,128]{2,1,0:T(8,128)S(1)} %fusion.2), channel_id=1, source_target_pairs={{0,24},{8,16},{16,8},{24,0},{1,25},{9,17},{17,9},{25,1},{2,26},{10... | collective-permute-start | bytes 24584 | tf_op jit(solution)/shard_map/ppermute | solution.py:50
  56.0 3.8 %collective-permute-done.13 = f32[2,8,128]{2,1,0:T(8,128)S(1)} collective-permute-done((f32[2,8,128]{2,1,0:T(8,128)S(1)}, f32[2,8,128]{2,1,0:T(8,128)S(1)}, u32[]{:S(2)}, u32[]{:S(2)}) %collective-permute-start.13) | collective-permute-done | bytes 8224 | tf_op jit(solution)/shard_map/ppermute | solution.py:50
  59.9 0.1 broadcast_select_fusion.1
  60.0 0.0 collective-permute-start.14
  60.0 3.6 %collective-permute-done.14 = f32[2,8,128]{2,1,0:T(8,128)S(1)} collective-permute-done((f32[2,8,128]{2,1,0:T(8,128)S(1)}, f32[2,8,128]{2,1,0:T(8,128)S(1)}, u32[]{:S(2)}, u32[]{:S(2)}) %collective-permute-start.14) | collective-permute-done | bytes 8224 | tf_op jit(solution)/shard_map/ppermute | solution.py:45
  63.6 0.1 broadcast_select_fusion
  63.7 1.1 %collective-permute-start.15 = (f32[2,8,128]{2,1,0:T(8,128)S(1)}, f32[2,8,128]{2,1,0:T(8,128)S(1)}, u32[]{:S(2)}, u32[]{:S(2)}) collective-permute-start(f32[2,8,128]{2,1,0:T(8,128)S(1)} %broadcast_select_fusion), channel_id=1, source_target_pairs={{0,7},{1,2},{2,1},{3,4},{4,3},{5,6},{6,5},{7,0},{8,15},{9,10},{10,... | collective-permute-start | bytes 24584 | tf_op jit(solution)/shard_map/ppermute | solution.py:50
  64.8 3.8 %collective-permute-done.15 = f32[2,8,128]{2,1,0:T(8,128)S(1)} collective-permute-done((f32[2,8,128]{2,1,0:T(8,128)S(1)}, f32[2,8,128]{2,1,0:T(8,128)S(1)}, u32[]{:S(2)}, u32[]{:S(2)}) %collective-permute-start.15) | collective-permute-done | bytes 8224 | tf_op jit(solution)/shard_map/ppermute | solution.py:50
  68.7 0.2 fusion.5
  68.9 0.7 fusion.6
  (16 shorter events, 0.1 us)
Async XLA Ops:
  0.6 11.5 %copy-start = (f32[3,16,32,128]{3,2,1,0:T(8,128)S(1)}, f32[3,16,32,128]{3,2,1,0:T(8,128)}, u32[]{:S(2)}) copy-start(f32[3,16,32,128]{3,2,1,0:T(8,128)} %vel.5) | copy-start | bytes 2359300
  0.6 11.5 %copy-start.1 = (f32[3,16,32,128]{3,2,1,0:T(8,128)S(1)}, f32[3,16,32,128]{3,2,1,0:T(8,128)}, u32[]{:S(2)}) copy-start(f32[3,16,32,128]{3,2,1,0:T(8,128)} %forc.5) | copy-start | bytes 2359300
  2.3 4.8 %collective-permute-start = (f32[19,32,128]{2,1,0:T(8,128)S(1)}, f32[19,32,128]{2,1,0:T(8,128)S(1)}, u32[]{:S(2)}, u32[]{:S(2)}) collective-permute-start(f32[19,32,128]{2,1,0:T(8,128)S(1)} %get-tuple-element.36), channel_id=1, source_target_pairs={{0,32},{32,0},{64,96},{96,64},{128,160},{160,128},{192,224},{224,1... | collective-permute-start | bytes 933896 | tf_op jit(solution)/shard_map/ppermute | solution.py:45
  2.4 7.6 %collective-permute-start.1 = (f32[19,32,128]{2,1,0:T(8,128)S(1)}, f32[19,32,128]{2,1,0:T(8,128)S(1)}, u32[]{:S(2)}, u32[]{:S(2)}) collective-permute-start(f32[19,32,128]{2,1,0:T(8,128)S(1)} %get-tuple-element.37), channel_id=1, source_target_pairs={{0,224},{32,64},{64,32},{96,128},{128,96},{160,192},{192,160},{224... | collective-permute-start | bytes 933896 | tf_op jit(solution)/shard_map/ppermute | solution.py:50
  5.2 8.1 %collective-permute-start.2 = (f32[37,8,128]{2,1,0:T(8,128)S(1)}, f32[37,8,128]{2,1,0:T(8,128)S(1)}, u32[]{:S(2)}, u32[]{:S(2)}) collective-permute-start(f32[37,8,128]{2,1,0:T(8,128)S(1)} %get-tuple-element.38), channel_id=1, source_target_pairs={{0,8},{8,0},{16,24},{24,16},{1,9},{9,1},{17,25},{25,17},{2,10},{10... | collective-permute-start | bytes 454664 | tf_op jit(solution)/shard_map/ppermute | solution.py:45
  6.0 7.4 %collective-permute-start.3 = (f32[37,8,128]{2,1,0:T(8,128)S(1)}, f32[37,8,128]{2,1,0:T(8,128)S(1)}, u32[]{:S(2)}, u32[]{:S(2)}) collective-permute-start(f32[37,8,128]{2,1,0:T(8,128)S(1)} %get-tuple-element.39), channel_id=1, source_target_pairs={{0,24},{8,16},{16,8},{24,0},{1,25},{9,17},{17,9},{25,1},{2,26},{10... | collective-permute-start | bytes 454664 | tf_op jit(solution)/shard_map/ppermute | solution.py:50
  10.1 4.4 %collective-permute-start.4 = (f32[16,8,128]{2,1,0:T(8,128)S(1)}, f32[16,8,128]{2,1,0:T(8,128)S(1)}, u32[]{:S(2)}, u32[]{:S(2)}) collective-permute-start(f32[16,8,128]{2,1,0:T(8,128)S(1)} %get-tuple-element.40), channel_id=1, source_target_pairs={{0,8},{8,0},{16,24},{24,16},{1,9},{9,1},{17,25},{25,17},{2,10},{10... | collective-permute-start | bytes 196616 | tf_op jit(solution)/shard_map/ppermute | solution.py:45
  10.9 5.5 %collective-permute-start.5 = (f32[16,8,128]{2,1,0:T(8,128)S(1)}, f32[16,8,128]{2,1,0:T(8,128)S(1)}, u32[]{:S(2)}, u32[]{:S(2)}) collective-permute-start(f32[16,8,128]{2,1,0:T(8,128)S(1)} %get-tuple-element.41), channel_id=1, source_target_pairs={{0,24},{8,16},{16,8},{24,0},{1,25},{9,17},{17,9},{25,1},{2,26},{10... | collective-permute-start | bytes 196616 | tf_op jit(solution)/shard_map/ppermute | solution.py:50
  17.1 13.3 %collective-permute-start.6 = (f32[25,8,128]{2,1,0:T(8,128)S(1)}, f32[25,8,128]{2,1,0:T(8,128)S(1)}, u32[]{:S(2)}, u32[]{:S(2)}) collective-permute-start(f32[25,8,128]{2,1,0:T(8,128)S(1)} %get-tuple-element.47), channel_id=1, source_target_pairs={{0,1},{1,0},{2,3},{3,2},{4,5},{5,4},{6,7},{7,6},{8,9},{9,8},{10,11... | collective-permute-start | bytes 307208 | tf_op jit(solution)/shard_map/ppermute | solution.py:45
  19.1 5.0 %copy-start.4 = (f32[8]{0:T(128)S(1)}, f32[8]{0:T(128)}, u32[]{:S(2)}) copy-start(f32[8]{0:T(128)} %pre.3) | copy-start | bytes 100
  19.1 5.0 %copy-start.5 = (f32[8]{0:T(128)S(1)}, f32[8]{0:T(128)}, u32[]{:S(2)}) copy-start(f32[8]{0:T(128)} %yld.3) | copy-start | bytes 100
  19.1 11.3 %collective-permute-start.7 = (f32[25,8,128]{2,1,0:T(8,128)S(1)}, f32[25,8,128]{2,1,0:T(8,128)S(1)}, u32[]{:S(2)}, u32[]{:S(2)}) collective-permute-start(f32[25,8,128]{2,1,0:T(8,128)S(1)} %get-tuple-element.48), channel_id=1, source_target_pairs={{0,7},{1,2},{2,1},{3,4},{4,3},{5,6},{6,5},{7,0},{8,15},{9,10},{10,... | collective-permute-start | bytes 307208 | tf_op jit(solution)/shard_map/ppermute | solution.py:50
  30.3 9.7 %copy-start.2 = (f32[3,16,32,128]{3,2,1,0:T(8,128)S(1)}, f32[3,16,32,128]{3,2,1,0:T(8,128)}, u32[]{:S(2)}) copy-start(f32[3,16,32,128]{3,2,1,0:T(8,128)} %get-tuple-element.43.u_own) | copy-start | bytes 2359300
  32.9 5.1 %collective-permute-start.8 = (f32[1,128]{1,0:T(1,128)S(1)}, f32[1,128]{1,0:T(1,128)S(1)}, u32[]{:S(2)}, u32[]{:S(2)}) collective-permute-start(f32[1,128]{1,0:T(1,128)S(1)} %get-tuple-element.61), channel_id=1, source_target_pairs={{0,128},{32,160},{64,192},{96,224},{128,0},{160,32},{192,64},{224,... | collective-permute-start | bytes 1544 | tf_op jit(solution)/shard_map/ppermute | solution.py:651
  38.0 7.5 %collective-permute-start.9 = (f32[1,128]{1,0:T(1,128)S(1)}, f32[1,128]{1,0:T(1,128)S(1)}, u32[]{:S(2)}, u32[]{:S(2)}) collective-permute-start(f32[1,128]{1,0:T(1,128)S(1)} %add.50), channel_id=1, source_target_pairs={{0,4},{1,5},{2,6},{3,7},{4,0},{5,1},{6,2},{7,3},{8,12},{9,13},{10,... | collective-permute-start | bytes 1544 | tf_op jit(solution)/shard_map/ppermute | solution.py:651
  40.0 1.0 %copy-start.3 = (f32[22,40,128]{2,1,0:T(8,128)S(1)}, f32[22,40,128]{2,1,0:T(8,128)}, u32[]{:S(2)}) copy-start(f32[22,40,128]{2,1,0:T(8,128)} %get-tuple-element.42.v_own) | copy-start | bytes 1351684
  45.6 1.2 %collective-permute-start.10 = (f32[8,128]{1,0:T(8,128)S(1)}, f32[8,128]{1,0:T(8,128)S(1)}, u32[]{:S(2)}, u32[]{:S(2)}) collective-permute-start(f32[8,128]{1,0:T(8,128)S(1)} %bitcast_select_fusion.1), channel_id=1, source_target_pairs={{0,32},{32,0},{64,96},{96,64},{128,160},{160,128},{192,224},{224,1... | collective-permute-start | bytes 12296 | tf_op jit(solution)/shard_map/ppermute | solution.py:45
  46.9 4.3 %collective-permute-start.11 = (f32[8,128]{1,0:T(8,128)S(1)}, f32[8,128]{1,0:T(8,128)S(1)}, u32[]{:S(2)}, u32[]{:S(2)}) collective-permute-start(f32[8,128]{1,0:T(8,128)S(1)} %bitcast_select_fusion), channel_id=1, source_target_pairs={{0,224},{32,64},{64,32},{96,128},{128,96},{160,192},{192,160},{224... | collective-permute-start | bytes 12296 | tf_op jit(solution)/shard_map/ppermute | solution.py:50
  51.2 3.7 %collective-permute-start.12 = (f32[2,8,128]{2,1,0:T(8,128)S(1)}, f32[2,8,128]{2,1,0:T(8,128)S(1)}, u32[]{:S(2)}, u32[]{:S(2)}) collective-permute-start(f32[2,8,128]{2,1,0:T(8,128)S(1)} %fusion.3), channel_id=1, source_target_pairs={{0,8},{8,0},{16,24},{24,16},{1,9},{9,1},{17,25},{25,17},{2,10},{10... | collective-permute-start | bytes 24584 | tf_op jit(solution)/shard_map/ppermute | solution.py:45
  55.0 4.9 %collective-permute-start.13 = (f32[2,8,128]{2,1,0:T(8,128)S(1)}, f32[2,8,128]{2,1,0:T(8,128)S(1)}, u32[]{:S(2)}, u32[]{:S(2)}) collective-permute-start(f32[2,8,128]{2,1,0:T(8,128)S(1)} %fusion.2), channel_id=1, source_target_pairs={{0,24},{8,16},{16,8},{24,0},{1,25},{9,17},{17,9},{25,1},{2,26},{10... | collective-permute-start | bytes 24584 | tf_op jit(solution)/shard_map/ppermute | solution.py:50
  60.0 3.7 %collective-permute-start.14 = (f32[2,8,128]{2,1,0:T(8,128)S(1)}, f32[2,8,128]{2,1,0:T(8,128)S(1)}, u32[]{:S(2)}, u32[]{:S(2)}) collective-permute-start(f32[2,8,128]{2,1,0:T(8,128)S(1)} %get-tuple-element.65), channel_id=1, source_target_pairs={{0,1},{1,0},{2,3},{3,2},{4,5},{5,4},{6,7},{7,6},{8,9},{9,8},{10,11... | collective-permute-start | bytes 24584 | tf_op jit(solution)/shard_map/ppermute | solution.py:45
  63.7 4.9 %collective-permute-start.15 = (f32[2,8,128]{2,1,0:T(8,128)S(1)}, f32[2,8,128]{2,1,0:T(8,128)S(1)}, u32[]{:S(2)}, u32[]{:S(2)}) collective-permute-start(f32[2,8,128]{2,1,0:T(8,128)S(1)} %broadcast_select_fusion), channel_id=1, source_target_pairs={{0,7},{1,2},{2,1},{3,4},{4,3},{5,6},{6,5},{7,0},{8,15},{9,10},{10,... | collective-permute-start | bytes 24584 | tf_op jit(solution)/shard_map/ppermute | solution.py:50

commit v5 on v4

--- a/solution.py
+++ b/solution.py
@@ -527,10 +527,25 @@
     return jnp.where(lane >= 124, roll(edge, 100 - 32 * g, 1), value)
 
 
-def collect(
-    v_own, u_own, residual_in, ve, ue, re,
-    smoothed, visc_out, one_out, two_out, residual, partial,
-    v_m, v_s, w_m, w_s, y1, c1, t2, t3,
+def results(v_own, u_own, residual_in, ve, ue, re, one, two, smoothed, visc_out, one_out, two_out, residual):
+    one_out[...] = one[...]
+    two_out[...] = two[...]
+    for x in range(NX):
+        g, i = (x + 4) // 6, (x + 4) % 6
+        for c in range(3):
+            for o in range(4):
+                rows = slice(8 * o, 8 * o + 8)
+                smoothed[c, x, rows] = merge(u_own[c, x, rows], ue[c, i, rows], g)
+                residual[c, x, rows] = merge(residual_in[c, x, rows], re[c, i, rows], g)
+        for o in range(4):
+            rows = slice(8 * o, 8 * o + 8)
+            visc_out[x, rows] = merge(v_own[x + 3, rows], ve[i, rows], g)
+
+
+def coarsen(
+    v_own, ve, total,
+    one_out, two_out, send,
+    v_m, v_s, w_m, w_s, y1, c1, t2, t3, parts,
 ):
     lo_x, hi_x = flags("gx")
     lo_y, hi_y = flags("gy")
@@ -544,15 +559,6 @@
             put_rows(v_m, (vx,), o, value)
             side = jnp.where(lane < 4, roll(edge, -28 - 32 * g, 1), 0.0)
             put_rows(v_s, (vx,), o, jnp.where(lane >= 124, roll(edge, 124 - 32 * g, 1), side))
-            if 3 <= vx < 19 and o < 4:
-                visc_out[vx - 3, 8 * o : 8 * o + 8] = value
-    for x in range(NX):
-        g, i = (x + 4) // 6, (x + 4) % 6
-        for c in range(3):
-            for o in range(4):
-                rows = slice(8 * o, 8 * o + 8)
-                smoothed[c, x, rows] = merge(u_own[c, x, rows], ue[c, i, rows], g)
-                residual[c, x, rows] = merge(residual_in[c, x, rows], re[c, i, rows], g)
 
     def coarse_x(k, _):
         w_m[k] = four(v_m[2 * k], v_m[2 * k + 1], v_m[2 * k + 2], v_m[2 * k + 3])
@@ -597,58 +603,44 @@
         rows.append(four(*(t3[pl.ds(1 + i, 8, stride=2)] for i in range(4))))
     band3 = band(128, lambda r: jnp.where(r < 32, r, 100000), lambda m: jnp.where(m < 18, m - 1, 1000))
     coarse = exact_dot(jnp.concatenate(rows, axis=0), band3)
+    sub = subs()
+    part = []
     for k in range(4):
-        partial[k] = coarse[8 * k : 8 * k + 8]
-
-
-def with_sum(tile, total):
-    row = lax.broadcasted_iota(jnp.int32, tile.shape, tile.ndim - 2)
-    return jnp.where(row == 7, total, tile)
-
-
-def finish(partial, total):
-    even, has_lo, has_hi = position("gx")
-    got_a = pair_a(with_sum(jnp.where(even, partial[3], partial[0]), total), "gx")
-    total = total + got_a[7:8]
-    got_b = pair_b(with_sum(jnp.where(even, partial[0], partial[3]), total), "gx")
-    total = total + got_b[7:8]
-    lo, hi = jnp.where(even, got_b, got_a), jnp.where(even, got_a, got_b)
-    inner = jnp.stack(
-        [partial[1] + jnp.where(has_lo, lo, 0.0), partial[2] + jnp.where(has_hi, hi, 0.0)]
-    )
-    even, has_lo, has_hi = position("gy")
-    got_a = pair_a(with_sum(inner, total), "gy")
-    total = total + got_a[0, 7:8]
-    got_b = pair_b(with_sum(inner, total), "gy")
-    total = total + got_b[0, 7:8]
-    lo, hi = jnp.where(even, got_b, got_a), jnp.where(even, got_a, got_b)
-    row = lax.broadcasted_iota(jnp.int32, inner.shape, 1)
-    inner = (
-        inner
-        + jnp.where((row == 1) & has_lo, jnp.roll(lo, -4, 1), 0.0)
-        + jnp.where((row == 4) & has_hi, jnp.roll(hi, 4, 1), 0.0)
-    )
-    even, has_lo, has_hi = position("gz")
-    got_a = pair_a(with_sum(inner, total), "gz")
-    total = total + got_a[0, 7:8]
-    got_b = pair_b(with_sum(inner, total), "gz")
-    total = total + got_b[0, 7:8]
-    lo, hi = jnp.where(even, got_b, got_a), jnp.where(even, got_a, got_b)
-    three = inner[:, 1:5, 1:17]
-    z = lax.broadcasted_iota(jnp.int32, three.shape, 2)
-    three = (
-        three
-        + jnp.where((z == 0) & has_lo, lo[:, 1:5, 17:18], 0.0)
-        + jnp.where((z == 15) & has_hi, hi[:, 1:5, 0:1], 0.0)
-    )
-    return total[0, 0], three
-
-
-def far(axis, total):
-    count = lax.axis_size(axis)
-    if count == 4:
-        return jnp.zeros_like(total)
-    return lax.ppermute(total, axis, [(i, (i + count // 2) % count) for i in range(count)])
+        tile = coarse[8 * k : 8 * k + 8]
+        ends = {
+            -1: jnp.where(lane == 15, roll(tile, 15, 1), 0.0),
+            0: jnp.where(lane < 16, roll(tile, -1, 1), 0.0),
+            1: jnp.where(lane == 0, roll(tile, -17, 1), 0.0),
+        }
+        part.append({})
+        for dz, value in ends.items():
+            apart = pltpu.roll(value, 0, 1, stride=16, stride_axis=0)
+            for dy, row, shift in ((-1, sub == 0, 48), (0, (sub >= 1) & (sub < 5), 112), (1, sub == 5, 48)):
+                part[k][dy, dz] = roll(jnp.sum(jnp.where(row, apart, 0.0), axis=0, keepdims=True), shift, 1)
+    offsets = [(dx, dy, dz) for dx in (-1, 0, 1) for dy in (-1, 0, 1) for dz in (-1, 0, 1)]
+    for k, (dx, dy, dz) in enumerate(offsets):
+        if dx == 0:
+            value = part[1][dy, dz] + roll(part[2][dy, dz], 64, 1)
+        else:
+            value = part[3][dy, dz] if dx == 1 else roll(part[0][dy, dz], 64, 1)
+        parts[k] = value
+    mine = [lax.axis_index(axis) for axis in AX]
+    size = [lax.axis_size(axis) for axis in AX]
+    square = total[...]
+    nothing = jnp.concatenate([square, jnp.zeros((1, 128), F32)], axis=1)
+
+    def fill(r, _):
+        send[r] = nothing
+        return 0
+
+    lax.fori_loop(0, send.shape[0], fill, 0, unroll=8)
+    for k, offset in enumerate(offsets):
+        at = [here + step for here, step in zip(mine, offset)]
+        inside = functools.reduce(lambda a, b: a & b, [(p >= 0) & (p < n) for p, n in zip(at, size)])
+
+        @pl.when(inside)
+        def _():
+            send[(at[0] * size[1] + at[1]) * size[2] + at[2], :, 128:256] = parts[k]
 
 
 def per_device(velocity, forcing, phase_block, prefactor, yield_stress):
@@ -700,26 +692,33 @@
         ],
         compiler_params=params(LIM), cost_estimate=cost(1 << 23), name="edge_work",
     )(*rz, eu, ef, eu4, ef4, tiles, square, prefactor, yield_stress)
-    total = total + far("gx", total)
-    total = total + far("gz", total)
-    smoothed, visc, one, two, residual, partial = pl.pallas_call(
-        collect,
-        out_shape=[
-            sds(3, NX, NY, NZ), sds(NX, NY, NZ), sds(8, 16, 64), sds(4, 8, 32), sds(3, NX, NY, NZ), sds(4, 8, 128),
-        ],
-        in_specs=[VMEM] * 6, out_specs=[VMEM] * 6,
+    devices = 1
+    for axis in AX:
+        devices = devices * lax.axis_size(axis)
+    one, two, send = pl.pallas_call(
+        coarsen,
+        out_shape=[sds(8, 16, 64), sds(4, 8, 32), sds(devices, 1, 256)],
+        in_specs=[VMEM] * 3, out_specs=[VMEM] * 3,
         scratch_shapes=[
             pltpu.VMEM((22, 56, 128), F32), pltpu.VMEM((22, 56, 128), F32),
             pltpu.VMEM((10, 56, 128), F32), pltpu.VMEM((10, 56, 128), F32), pltpu.VMEM((10, 24, 256), F32),
             pltpu.VMEM((10, 24, 128), F32), pltpu.VMEM((24, 128), F32), pltpu.VMEM((24, 128), F32),
+            pltpu.VMEM((27, 1, 128), F32),
         ],
-        compiler_params=params(LIM), cost_estimate=cost(1 << 23), name="collect",
-    )(v, u2, res, ve, ue, re)
-    total, three = finish(partial, total)
+        compiler_params=params(LIM), cost_estimate=cost(1 << 22), name="coarsen",
+    )(v, ve, total)
+    sums = jnp.sum(lax.all_to_all(send, AX, 0, 0, tiled=True), axis=0)[0]
+    smoothed, visc, one, two, residual = pl.pallas_call(
+        results,
+        out_shape=[sds(3, NX, NY, NZ), sds(NX, NY, NZ), sds(8, 16, 64), sds(4, 8, 32), sds(3, NX, NY, NZ)],
+        in_specs=[VMEM] * 8, out_specs=[VMEM] * 5,
+        compiler_params=params(LIM), cost_estimate=cost(1 << 22), name="results",
+    )(v, u2, res, ve, ue, re, one, two)
+    three = sums[128:].reshape(2, 4, 16)
     cells = 3.0 * NX * NY * NZ
     for axis in AX:
         cells = cells * lax.axis_size(axis)
-    return smoothed, visc, one, two, three, residual, jnp.sqrt(total / cells)
+    return smoothed, visc, one, two, three, residual, jnp.sqrt(sums[0] / cells)
 
 
 def solution(mesh):

time: 70.8 us -> 64.1 us (0.905)
  the two profiles are of different devices: /device:TPU:24 before, /device:TPU:1 now
where the time goes in v5:
time: 64.1 us; the launch traced here: 63.9 us
  starting transfers between devices  23.2 us (36%)
  waiting for transfers between devices  19 us (30%)
  Pallas kernels  17.5 us (27%)
  between operations  2.6 us (4%)
  local copies, waits for them, and re-layouts  1.25 us (2%)
    all_to_all x1, waiting for transfers between devices, per_device(): sums = jnp.sum(lax.all_to_all(send, AX, 0, 0, tiled=True), axis=0)[0]  13.4 us
    all_to_all x1, starting transfers between devices, per_device(): sums = jnp.sum(lax.all_to_all(send, AX, 0, 0, tiled=True), axis=0)[0]  9.82 us
    ppermute x4, starting transfers between devices, pair_b(): lax.ppermute(value, axis, [(i, (i + 1) % count if i % 2 else (i - 1) % co...  8.05 us
    pallas_call x1, Pallas kernels, per_device(): pl.pallas_call(main_work, out_shape=[pltpu.HBM((22, 40, 128), F32), pltpu...  6.25 us
    ppermute x4, starting transfers between devices, pair_a(): return lax.ppermute(value, axis, [(i, i ^ 1) for i in range(count)])  5.38 us
    ppermute x4, waiting for transfers between devices, pair_b(): lax.ppermute(value, axis, [(i, (i + 1) % count if i % 2 else (i - 1) % co...  5.24 us
    pallas_call x1, Pallas kernels, per_device(): pl.pallas_call(coarsen, out_shape=[sds(8, 16, 64), sds(4, 8, 32), sds(dev...  2.89 us
    pallas_call x1, Pallas kernels, per_device(): pl.pallas_call(edge_work, out_shape=[sds(6, 40, 128), sds(3, 6, 32, 128),...  2.56 us
  transfers between devices with their start and end apart: 9, of which 4 were waited for; matrix products, arithmetic and copies ran while one was open for 0% of the time, Pallas kernels for 15%

profile of v5, /device:TPU:1, one launch (start us, length us, event | category | flops | bytes accessed | tf_op | source)
XLA Modules:
  0.0 63.9 jit_solution(4809275316119630787)
XLA Ops:
  0.6 0.0 copy-start.1
  0.6 0.0 copy-start
  0.7 1.6 %pack_xy.1 = (f32[19,32,128]{2,1,0:T(8,128)S(1)}, f32[19,32,128]{2,1,0:T(8,128)S(1)}, f32[37,8,128]{2,1,0:T(8,128)S(1)}, f32[37,8,128]{2,1,0:T(8,128)S(1)}, f32[4,8,128]{2,1,0:T(8,128)S(1)}) custom-call(f32[3,16,32,128]{3,2,1,0:T(8,128)} %vel.5, f32[3,16,32,128]{3,2,1,0:T(8,128)} %forc.5, s32[4,8,32]{2,1,0:T(8,128)} %blocks_in.1), custom_call_target="tpu_custom_call" | custom-call | tf_op jit(solution)/shard_map/pack_xy/pallas_call | solution.py:647
  2.3 3.3 %collective-permute-start = (f32[19,32,128]{2,1,0:T(8,128)S(1)}, f32[19,32,128]{2,1,0:T(8,128)S(1)}, u32[]{:S(2)}, u32[]{:S(2)}) collective-permute-start(f32[19,32,128]{2,1,0:T(8,128)S(1)} %get-tuple-element.38), channel_id=1, source_target_pairs={{0,32},{32,0},{64,96},{96,64},{128,160},{160,128},{192,224},{224,1... | collective-permute-start | bytes 933896 | tf_op jit(solution)/shard_map/ppermute | solution.py:45
  5.6 0.0 collective-permute-start.1
  5.6 0.8 %collective-permute-start.2 = (f32[37,8,128]{2,1,0:T(8,128)S(1)}, f32[37,8,128]{2,1,0:T(8,128)S(1)}, u32[]{:S(2)}, u32[]{:S(2)}) collective-permute-start(f32[37,8,128]{2,1,0:T(8,128)S(1)} %get-tuple-element.40), channel_id=1, source_target_pairs={{0,8},{8,0},{16,24},{24,16},{1,9},{9,1},{17,25},{25,17},{2,10},{10... | collective-permute-start | bytes 454664 | tf_op jit(solution)/shard_map/ppermute | solution.py:45
  6.4 1.9 %collective-permute-start.3 = (f32[37,8,128]{2,1,0:T(8,128)S(1)}, f32[37,8,128]{2,1,0:T(8,128)S(1)}, u32[]{:S(2)}, u32[]{:S(2)}) collective-permute-start(f32[37,8,128]{2,1,0:T(8,128)S(1)} %get-tuple-element.41), channel_id=1, source_target_pairs={{0,24},{8,16},{16,8},{24,0},{1,25},{9,17},{17,9},{25,1},{2,26},{10... | collective-permute-start | bytes 454664 | tf_op jit(solution)/shard_map/ppermute | solution.py:50
  8.3 0.0 collective-permute-done.rx_a
  8.3 3.9 %collective-permute-done.1.rx_b = f32[19,32,128]{2,1,0:T(8,128)S(1)} collective-permute-done((f32[19,32,128]{2,1,0:T(8,128)S(1)}, f32[19,32,128]{2,1,0:T(8,128)S(1)}, u32[]{:S(2)}, u32[]{:S(2)}) %collective-permute-start.1) | collective-permute-done | bytes 311328 | tf_op jit(solution)/shard_map/ppermute | solution.py:50
  12.2 0.1 collective-permute-start.4
  12.3 1.5 %collective-permute-start.5 = (f32[16,8,128]{2,1,0:T(8,128)S(1)}, f32[16,8,128]{2,1,0:T(8,128)S(1)}, u32[]{:S(2)}, u32[]{:S(2)}) collective-permute-start(f32[16,8,128]{2,1,0:T(8,128)S(1)} %get-tuple-element.43), channel_id=1, source_target_pairs={{0,24},{8,16},{16,8},{24,0},{1,25},{9,17},{17,9},{25,1},{2,26},{10... | collective-permute-start | bytes 196616 | tf_op jit(solution)/shard_map/ppermute | solution.py:50
  13.8 0.0 copy-done.1
  13.8 0.0 copy-done
  13.8 1.2 %edge_own.1 = (f32[3,6,32,128]{3,2,1,0:T(8,128)S(1)}, f32[3,6,32,128]{3,2,1,0:T(8,128)S(1)}) custom-call(f32[3,16,32,128]{3,2,1,0:T(8,128)S(1)} %copy-done, f32[3,16,32,128]{3,2,1,0:T(8,128)S(1)} %copy-done.1, f32[19,32,128]{2,1,0:T(8,128)S(1)} %collective-permute-done.rx_a, f32[19,32,128]{2,1,0:T(8,128)S(1)} %collective-permute-done.1.rx_b), custom_call_target="tpu_custom_call" | custom-call | flops 25165824 | bytes 1048576 | tf_op jit(solution)/shard_map/edge_own/pallas_call | solution.py:664
  15.0 0.0 collective-permute-done.2.ryo_a
  15.0 0.0 collective-permute-done.3.ryo_b
  15.0 0.4 collective-permute-done.4.ryc_a
  15.4 1.3 %collective-permute-done.5.ryc_b = f32[16,8,128]{2,1,0:T(8,128)S(1)} collective-permute-done((f32[16,8,128]{2,1,0:T(8,128)S(1)}, f32[16,8,128]{2,1,0:T(8,128)S(1)}, u32[]{:S(2)}, u32[]{:S(2)}) %collective-permute-start.5) | collective-permute-done | bytes 65568 | tf_op jit(solution)/shard_map/ppermute | solution.py:50
  16.8 0.7 %pack_z.1 = (f32[25,8,128]{2,1,0:T(8,128)S(1)}, f32[25,8,128]{2,1,0:T(8,128)S(1)}, f32[3,6,8,128]{3,2,1,0:T(8,128)S(1)}, f32[3,6,8,128]{3,2,1,0:T(8,128)S(1)}, f32[12,8,128]{2,1,0:T(8,128)S(1)}) custom-call(f32[4,8,128]{2,1,0:T(8,128)S(1)} %get-tuple-element.37.phase_ref.phase, f32[19,32,128]{2,1,0:T(8,128)S(1)} %collective-permute-done.rx_a, ...), custom_call_target="tpu_custom_call" | custom-call | tf_op jit(solution)/shard_map/pack_z/pallas_call | solution.py:668
  17.5 0.0 copy-start.4
  17.5 0.0 copy-start.5
  17.5 1.2 %collective-permute-start.6 = (f32[25,8,128]{2,1,0:T(8,128)S(1)}, f32[25,8,128]{2,1,0:T(8,128)S(1)}, u32[]{:S(2)}, u32[]{:S(2)}) collective-permute-start(f32[25,8,128]{2,1,0:T(8,128)S(1)} %get-tuple-element.49), channel_id=1, source_target_pairs={{0,1},{1,0},{2,3},{3,2},{4,5},{5,4},{6,7},{7,6},{8,9},{9,8},{10,11... | collective-permute-start | bytes 307208 | tf_op jit(solution)/shard_map/ppermute | solution.py:45
  18.7 4.7 %collective-permute-start.7 = (f32[25,8,128]{2,1,0:T(8,128)S(1)}, f32[25,8,128]{2,1,0:T(8,128)S(1)}, u32[]{:S(2)}, u32[]{:S(2)}) collective-permute-start(f32[25,8,128]{2,1,0:T(8,128)S(1)} %get-tuple-element.50), channel_id=1, source_target_pairs={{0,7},{1,2},{2,1},{3,4},{4,3},{5,6},{6,5},{7,0},{8,15},{9,10},{10,... | collective-permute-start | bytes 307208 | tf_op jit(solution)/shard_map/ppermute | solution.py:50
  23.4 0.0 copy-done.4
  23.4 0.0 copy-done.5
  23.4 6.2 %main_work.1 = (f32[22,40,128]{2,1,0:T(8,128)}, f32[3,16,32,128]{3,2,1,0:T(8,128)}, f32[3,16,32,128]{3,2,1,0:T(8,128)S(1)}, f32[8,128]{1,0:T(8,128)S(1)}) custom-call(f32[3,16,32,128]{3,2,1,0:T(8,128)S(1)} %copy-done, f32[3,16,32,128]{3,2,1,0:T(8,128)S(1)} %copy-done.1, f32[4,8,128]{2,1,0:T(8,128)S(1)} %get-tuple-element.37.phase_ref.phase, ...), custom_call_target="tpu_custom_call" | custom-call | flops 33554432 | bytes 1048576 | tf_op jit(solution)/shard_map/main_work/pallas_call | solution.py:673
  29.6 0.0 collective-permute-done.6.rz_a
  29.6 0.0 collective-permute-done.7.rz_b
  29.7 0.0 copy-start.2
  29.7 2.6 %edge_work.1 = (f32[6,40,128]{2,1,0:T(8,128)S(1)}, f32[3,6,32,128]{3,2,1,0:T(8,128)S(1)}, f32[3,6,32,128]{3,2,1,0:T(8,128)S(1)}, f32[1,128]{1,0:T(1,128)S(1)}) custom-call(f32[25,8,128]{2,1,0:T(8,128)S(1)} %collective-permute-done.6.rz_a, f32[25,8,128]{2,1,0:T(8,128)S(1)} %collective-permute-done.7.rz_b, f32[3,6,32,128]{3,2,1,0:T(8,128)S(1)} %get-tuple-element.47.eu, ...), custom_call_target="tpu_custom_call" | custom-call | flops 8388608 | bytes 1048576 | tf_op jit(solution)/shard_map/edge_work/pallas_call | solution.py:684
  32.2 0.0 copy-start.3
  32.2 0.0 copy-done.2
  32.2 2.9 %coarsen.1 = (f32[8,16,64]{2,1,0:T(8,128)S(1)}, f32[4,8,32]{2,1,0:T(8,128)S(1)}, f32[256,1,256]{2,1,0:T(1,128)}) custom-call(f32[22,40,128]{2,1,0:T(8,128)S(1)} %copy-done.2, f32[6,40,128]{2,1,0:T(8,128)S(1)} %get-tuple-element.55.ve, f32[1,128]{1,0:T(1,128)S(1)} %get-tuple-element.58.total), custom_call_target="tpu_custom_call" | custom-call | flops 4194304 | bytes 1048576 | tf_op jit(solution)/shard_map/coarsen/pallas_call | solution.py:698
  35.1 9.8 %all-to-all-start = ((f32[256,1,256]{2,1,0:T(1,128)}), f32[256,1,256]{2,1,0:T(1,128)S(1)}, u32[]{:S(2)}, u32[]{:S(2)}) async-start(f32[256,1,256]{2,1,0:T(1,128)} %get-tuple-element.65), calls=%async_computation | async-start | bytes 524288 | tf_op jit(solution)/shard_map/all_to_all | solution.py:710
  45.0 0.0 copy-done.3
  45.0 2.3 %results.1 = (f32[3,16,32,128]{3,2,1,0:T(8,128)}, f32[16,32,128]{2,1,0:T(8,128)}, f32[8,16,64]{2,1,0:T(8,128)}, f32[4,8,32]{2,1,0:T(8,128)}, f32[3,16,32,128]{3,2,1,0:T(8,128)}) custom-call(f32[22,40,128]{2,1,0:T(8,128)S(1)} %copy-done.2, f32[3,16,32,128]{3,2,1,0:T(8,128)S(1)} %copy-done.3, f32[3,16,32,128]{3,2,1,0:T(8,128)S(1)} %get-tuple-element.46.residual_in, ...), custom_call_target="tpu_custom_call" | custom-call | flops 4194304 | bytes 1048576 | tf_op jit(solution)/shard_map/results/pallas_call | solution.py:711
  47.2 13.4 %all-to-all-done = f32[256,1,256]{2,1,0:T(1,128)S(1)} async-done(((f32[256,1,256]{2,1,0:T(1,128)}), f32[256,1,256]{2,1,0:T(1,128)S(1)}, u32[]{:S(2)}, u32[]{:S(2)}) %all-to-all-start) | async-done | bytes 262176 | tf_op jit(solution)/shard_map/all_to_all | solution.py:710
  60.6 0.3 reduce_sum.11
  60.9 0.5 slice.11
  62.1 0.7 %reshape.25 = f32[2,4,16]{2,1,0:T(4,128)} reshape(f32[128]{0:T(128)S(1)} %slice_reduce_fusion) | data formatting | bytes 1024 | tf_op jit(solution)/shard_map/reshape | solution.py:717
  (2 shorter events, 0.1 us)
Async XLA Ops:
  0.6 13.2 %copy-start.1 = (f32[3,16,32,128]{3,2,1,0:T(8,128)S(1)}, f32[3,16,32,128]{3,2,1,0:T(8,128)}, u32[]{:S(2)}) copy-start(f32[3,16,32,128]{3,2,1,0:T(8,128)} %forc.5) | copy-start | bytes 2359300
  0.6 13.2 %copy-start = (f32[3,16,32,128]{3,2,1,0:T(8,128)S(1)}, f32[3,16,32,128]{3,2,1,0:T(8,128)}, u32[]{:S(2)}) copy-start(f32[3,16,32,128]{3,2,1,0:T(8,128)} %vel.5) | copy-start | bytes 2359300
  2.3 6.0 %collective-permute-start = (f32[19,32,128]{2,1,0:T(8,128)S(1)}, f32[19,32,128]{2,1,0:T(8,128)S(1)}, u32[]{:S(2)}, u32[]{:S(2)}) collective-permute-start(f32[19,32,128]{2,1,0:T(8,128)S(1)} %get-tuple-element.38), channel_id=1, source_target_pairs={{0,32},{32,0},{64,96},{96,64},{128,160},{160,128},{192,224},{224,1... | collective-permute-start | bytes 933896 | tf_op jit(solution)/shard_map/ppermute | solution.py:45
  5.6 6.6 %collective-permute-start.1 = (f32[19,32,128]{2,1,0:T(8,128)S(1)}, f32[19,32,128]{2,1,0:T(8,128)S(1)}, u32[]{:S(2)}, u32[]{:S(2)}) collective-permute-start(f32[19,32,128]{2,1,0:T(8,128)S(1)} %get-tuple-element.39), channel_id=1, source_target_pairs={{0,224},{32,64},{64,32},{96,128},{128,96},{160,192},{192,160},{224... | collective-permute-start | bytes 933896 | tf_op jit(solution)/shard_map/ppermute | solution.py:50
  5.6 9.4 %collective-permute-start.2 = (f32[37,8,128]{2,1,0:T(8,128)S(1)}, f32[37,8,128]{2,1,0:T(8,128)S(1)}, u32[]{:S(2)}, u32[]{:S(2)}) collective-permute-start(f32[37,8,128]{2,1,0:T(8,128)S(1)} %get-tuple-element.40), channel_id=1, source_target_pairs={{0,8},{8,0},{16,24},{24,16},{1,9},{9,1},{17,25},{25,17},{2,10},{10... | collective-permute-start | bytes 454664 | tf_op jit(solution)/shard_map/ppermute | solution.py:45
  6.4 8.7 %collective-permute-start.3 = (f32[37,8,128]{2,1,0:T(8,128)S(1)}, f32[37,8,128]{2,1,0:T(8,128)S(1)}, u32[]{:S(2)}, u32[]{:S(2)}) collective-permute-start(f32[37,8,128]{2,1,0:T(8,128)S(1)} %get-tuple-element.41), channel_id=1, source_target_pairs={{0,24},{8,16},{16,8},{24,0},{1,25},{9,17},{17,9},{25,1},{2,26},{10... | collective-permute-start | bytes 454664 | tf_op jit(solution)/shard_map/ppermute | solution.py:50
  12.2 3.2 %collective-permute-start.4 = (f32[16,8,128]{2,1,0:T(8,128)S(1)}, f32[16,8,128]{2,1,0:T(8,128)S(1)}, u32[]{:S(2)}, u32[]{:S(2)}) collective-permute-start(f32[16,8,128]{2,1,0:T(8,128)S(1)} %get-tuple-element.42), channel_id=1, source_target_pairs={{0,8},{8,0},{16,24},{24,16},{1,9},{9,1},{17,25},{25,17},{2,10},{10... | collective-permute-start | bytes 196616 | tf_op jit(solution)/shard_map/ppermute | solution.py:45
  12.3 4.4 %collective-permute-start.5 = (f32[16,8,128]{2,1,0:T(8,128)S(1)}, f32[16,8,128]{2,1,0:T(8,128)S(1)}, u32[]{:S(2)}, u32[]{:S(2)}) collective-permute-start(f32[16,8,128]{2,1,0:T(8,128)S(1)} %get-tuple-element.43), channel_id=1, source_target_pairs={{0,24},{8,16},{16,8},{24,0},{1,25},{9,17},{17,9},{25,1},{2,26},{10... | collective-permute-start | bytes 196616 | tf_op jit(solution)/shard_map/ppermute | solution.py:50
  17.5 5.9 %copy-start.4 = (f32[8]{0:T(128)S(1)}, f32[8]{0:T(128)}, u32[]{:S(2)}) copy-start(f32[8]{0:T(128)} %pre.3) | copy-start | bytes 100
  17.5 5.9 %copy-start.5 = (f32[8]{0:T(128)S(1)}, f32[8]{0:T(128)}, u32[]{:S(2)}) copy-start(f32[8]{0:T(128)} %yld.3) | copy-start | bytes 100
  17.5 12.1 %collective-permute-start.6 = (f32[25,8,128]{2,1,0:T(8,128)S(1)}, f32[25,8,128]{2,1,0:T(8,128)S(1)}, u32[]{:S(2)}, u32[]{:S(2)}) collective-permute-start(f32[25,8,128]{2,1,0:T(8,128)S(1)} %get-tuple-element.49), channel_id=1, source_target_pairs={{0,1},{1,0},{2,3},{3,2},{4,5},{5,4},{6,7},{7,6},{8,9},{9,8},{10,11... | collective-permute-start | bytes 307208 | tf_op jit(solution)/shard_map/ppermute | solution.py:45
  18.7 10.9 %collective-permute-start.7 = (f32[25,8,128]{2,1,0:T(8,128)S(1)}, f32[25,8,128]{2,1,0:T(8,128)S(1)}, u32[]{:S(2)}, u32[]{:S(2)}) collective-permute-start(f32[25,8,128]{2,1,0:T(8,128)S(1)} %get-tuple-element.50), channel_id=1, source_target_pairs={{0,7},{1,2},{2,1},{3,4},{4,3},{5,6},{6,5},{7,0},{8,15},{9,10},{10,... | collective-permute-start | bytes 307208 | tf_op jit(solution)/shard_map/ppermute | solution.py:50
  29.7 2.6 %copy-start.2 = (f32[22,40,128]{2,1,0:T(8,128)S(1)}, f32[22,40,128]{2,1,0:T(8,128)}, u32[]{:S(2)}) copy-start(f32[22,40,128]{2,1,0:T(8,128)} %get-tuple-element.44.v_own) | copy-start | bytes 1351684
  32.2 12.7 %copy-start.3 = (f32[3,16,32,128]{3,2,1,0:T(8,128)S(1)}, f32[3,16,32,128]{3,2,1,0:T(8,128)}, u32[]{:S(2)}) copy-start(f32[3,16,32,128]{3,2,1,0:T(8,128)} %get-tuple-element.45.u_own) | copy-start | bytes 2359300
  35.1 25.5 %all-to-all-start = ((f32[256,1,256]{2,1,0:T(1,128)}), f32[256,1,256]{2,1,0:T(1,128)S(1)}, u32[]{:S(2)}, u32[]{:S(2)}) async-start(f32[256,1,256]{2,1,0:T(1,128)} %get-tuple-element.65), calls=%async_computation | async-start | bytes 524288 | tf_op jit(solution)/shard_map/all_to_all | solution.py:710

commit v6 on v5

--- a/solution.py
+++ b/solution.py
@@ -364,7 +364,7 @@
             put_rows(v_ref, (vx,), o, value)
         return 0
 
-    lax.fori_loop(0, 22, viscosity, 0, unroll=2)
+    lax.fori_loop(0, 22, viscosity, 0, unroll=22)
     copy_v = pltpu.make_async_copy(v_ref.at[:, 8:48], v_own, sems.at[0])
     copy_v.start()
 
@@ -381,8 +381,8 @@
 
         return body
 
-    lax.fori_loop(0, 20, sweep(u_ref, u1, 1, 2), 0, unroll=4)
-    lax.fori_loop(0, 18, sweep(u1, u2, 2, 1), 0, unroll=3)
+    lax.fori_loop(0, 20, sweep(u_ref, u1, 1, 2), 0, unroll=20)
+    lax.fori_loop(0, 18, sweep(u1, u2, 2, 1), 0, unroll=18)
     copy_u = pltpu.make_async_copy(u2.at[:, 1:17, 8:40], u_own, sems.at[1])
     copy_u.start()
 
@@ -396,7 +396,7 @@
                 acc = acc + value * value
         return acc
 
-    acc = lax.fori_loop(0, NX, last, jnp.zeros((8, 128), F32), unroll=4)
+    acc = lax.fori_loop(0, NX, last, jnp.zeros((8, 128), F32), unroll=16)
     lane = lanes()
     square[...] = jnp.where((lane >= 4) & (lane < 124), acc, 0.0)
     copy_v.wait()
@@ -565,7 +565,7 @@
         w_s[k] = four(v_s[2 * k], v_s[2 * k + 1], v_s[2 * k + 2], v_s[2 * k + 3])
         return 0
 
-    lax.fori_loop(0, 10, coarse_x, 0)
+    lax.fori_loop(0, 10, coarse_x, 0, unroll=10)
     y1[...] = jnp.zeros(y1.shape, F32)
     for k in range(10):
         for ref, at in ((w_m, 0), (w_s, 128)):
@@ -633,7 +633,7 @@
         send[r] = nothing
         return 0
 
-    lax.fori_loop(0, send.shape[0], fill, 0, unroll=8)
+    lax.fori_loop(0, send.shape[0], fill, 0, unroll=32)
     for k, offset in enumerate(offsets):
         at = [here + step for here, step in zip(mine, offset)]
         inside = functools.reduce(lambda a, b: a & b, [(p >= 0) & (p < n) for p, n in zip(at, size)])
@@ -641,6 +641,15 @@
         @pl.when(inside)
         def _():
             send[(at[0] * size[1] + at[1]) * size[2] + at[2], :, 128:256] = parts[k]
+
+
+def finish(cells, got, three, rms):
+    sums = jnp.sum(got[...], axis=0)
+    row = sums[:, 128:256]
+    for k in range(2):
+        for j in range(4):
+            three[k, j : j + 1] = roll(row, -16 * (4 * k + j), 1)[:, 0:16]
+    rms[...] = jnp.sqrt(sums[:, 0:128] * (1.0 / cells))
 
 
 def per_device(velocity, forcing, phase_block, prefactor, yield_stress):
@@ -707,18 +716,19 @@
         ],
         compiler_params=params(LIM), cost_estimate=cost(1 << 22), name="coarsen",
     )(v, ve, total)
-    sums = jnp.sum(lax.all_to_all(send, AX, 0, 0, tiled=True), axis=0)[0]
+    got = lax.all_to_all(send, AX, 0, 0, tiled=True)
     smoothed, visc, one, two, residual = pl.pallas_call(
         results,
         out_shape=[sds(3, NX, NY, NZ), sds(NX, NY, NZ), sds(8, 16, 64), sds(4, 8, 32), sds(3, NX, NY, NZ)],
         in_specs=[VMEM] * 8, out_specs=[VMEM] * 5,
         compiler_params=params(LIM), cost_estimate=cost(1 << 22), name="results",
     )(v, u2, res, ve, ue, re, one, two)
-    three = sums[128:].reshape(2, 4, 16)
-    cells = 3.0 * NX * NY * NZ
-    for axis in AX:
-        cells = cells * lax.axis_size(axis)
-    return smoothed, visc, one, two, three, residual, jnp.sqrt(sums[0] / cells)
+    cells = 3.0 * NX * NY * NZ * devices
+    three, rms = pl.pallas_call(
+        functools.partial(finish, cells), out_shape=[sds(2, 4, 16), sds(1, 128)],
+        in_specs=[VMEM], out_specs=[VMEM] * 2, compiler_params=params(LIM), name="finish",
+    )(got)
+    return smoothed, visc, one, two, three, residual, rms[0, 0]
 
 
 def solution(mesh):

time: 64.1 us -> 60.4 us (0.942)
  between operations: 2.6 us -> 0.78 us
  Pallas kernels: 17.5 us -> 15.9 us
  local copies, waits for them, and re-layouts: 1.25 us -> 0.03 us
  starting transfers between devices: 23.2 us -> 24.4 us
    pallas_call x1, Pallas kernels: 6.25 us -> 4.13 us  [per_device(): pl.pallas_call(main_work, out_shape=[pltpu.HBM((22, 40, 128), F32), pltpu...]
    all_to_all x1, starting transfers between devices: 9.82 us -> 10.9 us  [per_device(): got = lax.all_to_all(send, AX, 0, 0, tiled=True)]
    pallas_call x0 -> x1, Pallas kernels: none -> 0.94 us  [per_device(): pl.pallas_call(functools.partial(finish, cells), out_shape=[sds(2, 4, 16)...]
    reshape x1 -> x0, local copies, waits for them, and re-layouts: 0.68 us -> none  [per_device(): three = sums[128:].reshape(2, 4, 16)]
  transfers between devices with their start and end apart: 9 -> 9, of which waited for: 4 -> 4; matrix products, arithmetic and copies ran while one was open for 0% -> 0% of each run, Pallas kernels for 15% -> 13%
where the time goes in v6:
time: 60.4 us; the launch traced here: 60.2 us
  starting transfers between devices  24.4 us (40%)
  waiting for transfers between devices  19.1 us (32%)
  Pallas kernels  15.9 us (26%)
  between operations  0.78 us (1%)
    all_to_all x1, waiting for transfers between devices, per_device(): got = lax.all_to_all(send, AX, 0, 0, tiled=True)  13.5 us
    all_to_all x1, starting transfers between devices, per_device(): got = lax.all_to_all(send, AX, 0, 0, tiled=True)  10.9 us
    ppermute x4, starting transfers between devices, pair_b(): lax.ppermute(value, axis, [(i, (i + 1) % count if i % 2 else (i - 1) % co...  8.05 us
    ppermute x4, starting transfers between devices, pair_a(): return lax.ppermute(value, axis, [(i, i ^ 1) for i in range(count)])  5.38 us
    ppermute x4, waiting for transfers between devices, pair_b(): lax.ppermute(value, axis, [(i, (i + 1) % count if i % 2 else (i - 1) % co...  5.24 us
    pallas_call x1, Pallas kernels, per_device(): pl.pallas_call(main_work, out_shape=[pltpu.HBM((22, 40, 128), F32), pltpu...  4.13 us
    pallas_call x1, Pallas kernels, per_device(): pl.pallas_call(edge_work, out_shape=[sds(6, 40, 128), sds(3, 6, 32, 128),...  2.56 us
    pallas_call x1, Pallas kernels, per_device(): pl.pallas_call(coarsen, out_shape=[sds(8, 16, 64), sds(4, 8, 32), sds(dev...  2.49 us
  transfers between devices with their start and end apart: 9, of which 4 were waited for; matrix products, arithmetic and copies ran while one was open for 0% of the time, Pallas kernels for 13%

profile of v6, /device:TPU:1, one launch (start us, length us, event | category | flops | bytes accessed | tf_op | source)
XLA Modules:
  0.0 60.2 jit_solution(12388884052137271953)
XLA Ops:
  0.6 0.0 copy-start.1
  0.6 0.0 copy-start
  0.7 1.6 %pack_xy.1 = (f32[19,32,128]{2,1,0:T(8,128)S(1)}, f32[19,32,128]{2,1,0:T(8,128)S(1)}, f32[37,8,128]{2,1,0:T(8,128)S(1)}, f32[37,8,128]{2,1,0:T(8,128)S(1)}, f32[4,8,128]{2,1,0:T(8,128)S(1)}) custom-call(f32[3,16,32,128]{3,2,1,0:T(8,128)} %vel.5, f32[3,16,32,128]{3,2,1,0:T(8,128)} %forc.5, s32[4,8,32]{2,1,0:T(8,128)} %blocks_in.1), custom_call_target="tpu_custom_call" | custom-call | tf_op jit(solution)/shard_map/pack_xy/pallas_call | solution.py:656
  2.3 3.3 %collective-permute-start = (f32[19,32,128]{2,1,0:T(8,128)S(1)}, f32[19,32,128]{2,1,0:T(8,128)S(1)}, u32[]{:S(2)}, u32[]{:S(2)}) collective-permute-start(f32[19,32,128]{2,1,0:T(8,128)S(1)} %get-tuple-element.40), channel_id=1, source_target_pairs={{0,32},{32,0},{64,96},{96,64},{128,160},{160,128},{192,224},{224,1... | collective-permute-start | bytes 933896 | tf_op jit(solution)/shard_map/ppermute | solution.py:45
  5.6 0.0 collective-permute-start.1
  5.6 0.8 %collective-permute-start.2 = (f32[37,8,128]{2,1,0:T(8,128)S(1)}, f32[37,8,128]{2,1,0:T(8,128)S(1)}, u32[]{:S(2)}, u32[]{:S(2)}) collective-permute-start(f32[37,8,128]{2,1,0:T(8,128)S(1)} %get-tuple-element.42), channel_id=1, source_target_pairs={{0,8},{8,0},{16,24},{24,16},{1,9},{9,1},{17,25},{25,17},{2,10},{10... | collective-permute-start | bytes 454664 | tf_op jit(solution)/shard_map/ppermute | solution.py:45
  6.4 1.9 %collective-permute-start.3 = (f32[37,8,128]{2,1,0:T(8,128)S(1)}, f32[37,8,128]{2,1,0:T(8,128)S(1)}, u32[]{:S(2)}, u32[]{:S(2)}) collective-permute-start(f32[37,8,128]{2,1,0:T(8,128)S(1)} %get-tuple-element.43), channel_id=1, source_target_pairs={{0,24},{8,16},{16,8},{24,0},{1,25},{9,17},{17,9},{25,1},{2,26},{10... | collective-permute-start | bytes 454664 | tf_op jit(solution)/shard_map/ppermute | solution.py:50
  8.3 0.0 collective-permute-done.rx_a
  8.3 3.9 %collective-permute-done.1.rx_b = f32[19,32,128]{2,1,0:T(8,128)S(1)} collective-permute-done((f32[19,32,128]{2,1,0:T(8,128)S(1)}, f32[19,32,128]{2,1,0:T(8,128)S(1)}, u32[]{:S(2)}, u32[]{:S(2)}) %collective-permute-start.1) | collective-permute-done | bytes 311328 | tf_op jit(solution)/shard_map/ppermute | solution.py:50
  12.2 0.1 collective-permute-start.4
  12.3 1.5 %collective-permute-start.5 = (f32[16,8,128]{2,1,0:T(8,128)S(1)}, f32[16,8,128]{2,1,0:T(8,128)S(1)}, u32[]{:S(2)}, u32[]{:S(2)}) collective-permute-start(f32[16,8,128]{2,1,0:T(8,128)S(1)} %get-tuple-element.45), channel_id=1, source_target_pairs={{0,24},{8,16},{16,8},{24,0},{1,25},{9,17},{17,9},{25,1},{2,26},{10... | collective-permute-start | bytes 196616 | tf_op jit(solution)/shard_map/ppermute | solution.py:50
  13.8 0.0 copy-done.1
  13.8 0.0 copy-done
  13.8 1.2 %edge_own.1 = (f32[3,6,32,128]{3,2,1,0:T(8,128)S(1)}, f32[3,6,32,128]{3,2,1,0:T(8,128)S(1)}) custom-call(f32[3,16,32,128]{3,2,1,0:T(8,128)S(1)} %copy-done, f32[3,16,32,128]{3,2,1,0:T(8,128)S(1)} %copy-done.1, f32[19,32,128]{2,1,0:T(8,128)S(1)} %collective-permute-done.rx_a, f32[19,32,128]{2,1,0:T(8,128)S(1)} %collective-permute-done.1.rx_b), custom_call_target="tpu_custom_call" | custom-call | flops 25165824 | bytes 1048576 | tf_op jit(solution)/shard_map/edge_own/pallas_call | solution.py:673
  15.0 0.0 collective-permute-done.2.ryo_a
  15.0 0.0 collective-permute-done.3.ryo_b
  15.0 0.4 collective-permute-done.4.ryc_a
  15.4 1.3 %collective-permute-done.5.ryc_b = f32[16,8,128]{2,1,0:T(8,128)S(1)} collective-permute-done((f32[16,8,128]{2,1,0:T(8,128)S(1)}, f32[16,8,128]{2,1,0:T(8,128)S(1)}, u32[]{:S(2)}, u32[]{:S(2)}) %collective-permute-start.5) | collective-permute-done | bytes 65568 | tf_op jit(solution)/shard_map/ppermute | solution.py:50
  16.8 0.7 %pack_z.1 = (f32[25,8,128]{2,1,0:T(8,128)S(1)}, f32[25,8,128]{2,1,0:T(8,128)S(1)}, f32[3,6,8,128]{3,2,1,0:T(8,128)S(1)}, f32[3,6,8,128]{3,2,1,0:T(8,128)S(1)}, f32[12,8,128]{2,1,0:T(8,128)S(1)}) custom-call(f32[4,8,128]{2,1,0:T(8,128)S(1)} %get-tuple-element.39.phase_ref.phase, f32[19,32,128]{2,1,0:T(8,128)S(1)} %collective-permute-done.rx_a, ...), custom_call_target="tpu_custom_call" | custom-call | tf_op jit(solution)/shard_map/pack_z/pallas_call | solution.py:677
  17.5 0.0 copy-start.4
  17.5 0.0 copy-start.5
  17.5 1.2 %collective-permute-start.6 = (f32[25,8,128]{2,1,0:T(8,128)S(1)}, f32[25,8,128]{2,1,0:T(8,128)S(1)}, u32[]{:S(2)}, u32[]{:S(2)}) collective-permute-start(f32[25,8,128]{2,1,0:T(8,128)S(1)} %get-tuple-element.51), channel_id=1, source_target_pairs={{0,1},{1,0},{2,3},{3,2},{4,5},{5,4},{6,7},{7,6},{8,9},{9,8},{10,11... | collective-permute-start | bytes 307208 | tf_op jit(solution)/shard_map/ppermute | solution.py:45
  18.7 4.7 %collective-permute-start.7 = (f32[25,8,128]{2,1,0:T(8,128)S(1)}, f32[25,8,128]{2,1,0:T(8,128)S(1)}, u32[]{:S(2)}, u32[]{:S(2)}) collective-permute-start(f32[25,8,128]{2,1,0:T(8,128)S(1)} %get-tuple-element.52), channel_id=1, source_target_pairs={{0,7},{1,2},{2,1},{3,4},{4,3},{5,6},{6,5},{7,0},{8,15},{9,10},{10,... | collective-permute-start | bytes 307208 | tf_op jit(solution)/shard_map/ppermute | solution.py:50
  23.4 0.0 copy-done.4
  23.4 0.0 copy-done.5
  23.4 4.1 %main_work.1 = (f32[22,40,128]{2,1,0:T(8,128)}, f32[3,16,32,128]{3,2,1,0:T(8,128)}, f32[3,16,32,128]{3,2,1,0:T(8,128)S(1)}, f32[8,128]{1,0:T(8,128)S(1)}) custom-call(f32[3,16,32,128]{3,2,1,0:T(8,128)S(1)} %copy-done, f32[3,16,32,128]{3,2,1,0:T(8,128)S(1)} %copy-done.1, f32[4,8,128]{2,1,0:T(8,128)S(1)} %get-tuple-element.39.phase_ref.phase, ...), custom_call_target="tpu_custom_call" | custom-call | flops 33554432 | bytes 1048576 | tf_op jit(solution)/shard_map/main_work/pallas_call | solution.py:682
  27.5 0.0 collective-permute-done.6.rz_a
  27.5 0.0 collective-permute-done.7.rz_b
  27.5 0.0 copy-start.2
  27.5 2.6 %edge_work.1 = (f32[6,40,128]{2,1,0:T(8,128)S(1)}, f32[3,6,32,128]{3,2,1,0:T(8,128)S(1)}, f32[3,6,32,128]{3,2,1,0:T(8,128)S(1)}, f32[1,128]{1,0:T(1,128)S(1)}) custom-call(f32[25,8,128]{2,1,0:T(8,128)S(1)} %collective-permute-done.6.rz_a, f32[25,8,128]{2,1,0:T(8,128)S(1)} %collective-permute-done.7.rz_b, f32[3,6,32,128]{3,2,1,0:T(8,128)S(1)} %get-tuple-element.49.eu, ...), custom_call_target="tpu_custom_call" | custom-call | flops 8388608 | bytes 1048576 | tf_op jit(solution)/shard_map/edge_work/pallas_call | solution.py:693
  30.1 0.0 copy-start.3
  30.1 0.0 copy-done.2
  30.1 2.5 %coarsen.1 = (f32[8,16,64]{2,1,0:T(8,128)S(1)}, f32[4,8,32]{2,1,0:T(8,128)S(1)}, f32[256,1,256]{2,1,0:T(1,128)}) custom-call(f32[22,40,128]{2,1,0:T(8,128)S(1)} %copy-done.2, f32[6,40,128]{2,1,0:T(8,128)S(1)} %get-tuple-element.57.ve, f32[1,128]{1,0:T(1,128)S(1)} %get-tuple-element.60.total), custom_call_target="tpu_custom_call" | custom-call | flops 4194304 | bytes 1048576 | tf_op jit(solution)/shard_map/coarsen/pallas_call | solution.py:707
  32.6 10.9 %all-to-all-start = ((f32[256,1,256]{2,1,0:T(1,128)}), f32[256,1,256]{2,1,0:T(1,128)S(1)}, u32[]{:S(2)}, u32[]{:S(2)}) async-start(f32[256,1,256]{2,1,0:T(1,128)} %get-tuple-element.67), calls=%async_computation | async-start | bytes 524288 | tf_op jit(solution)/shard_map/all_to_all | solution.py:719
  43.6 0.0 copy-done.3
  43.6 2.3 %results.1 = (f32[3,16,32,128]{3,2,1,0:T(8,128)}, f32[16,32,128]{2,1,0:T(8,128)}, f32[8,16,64]{2,1,0:T(8,128)}, f32[4,8,32]{2,1,0:T(8,128)}, f32[3,16,32,128]{3,2,1,0:T(8,128)}) custom-call(f32[22,40,128]{2,1,0:T(8,128)S(1)} %copy-done.2, f32[3,16,32,128]{3,2,1,0:T(8,128)S(1)} %copy-done.3, f32[3,16,32,128]{3,2,1,0:T(8,128)S(1)} %get-tuple-element.48.residual_in, ...), custom_call_target="tpu_custom_call" | custom-call | flops 4194304 | bytes 1048576 | tf_op jit(solution)/shard_map/results/pallas_call | solution.py:720
  45.8 13.5 %all-to-all-done.got = f32[256,1,256]{2,1,0:T(1,128)S(1)} async-done(((f32[256,1,256]{2,1,0:T(1,128)}), f32[256,1,256]{2,1,0:T(1,128)S(1)}, u32[]{:S(2)}, u32[]{:S(2)}) %all-to-all-start) | async-done | bytes 262176 | tf_op jit(solution)/shard_map/all_to_all | solution.py:719
  59.3 0.9 %finish.1 = (f32[2,4,16]{2,1,0:T(4,128)}, f32[1,128]{1,0:T(1,128)}) custom-call(f32[256,1,256]{2,1,0:T(1,128)S(1)} %all-to-all-done.got), custom_call_target="tpu_custom_call" | custom-call | tf_op jit(solution)/shard_map/finish/pallas_call | solution.py:727
  (1 shorter events, 0.0 us)
Async XLA Ops:
  0.6 13.2 %copy-start.1 = (f32[3,16,32,128]{3,2,1,0:T(8,128)S(1)}, f32[3,16,32,128]{3,2,1,0:T(8,128)}, u32[]{:S(2)}) copy-start(f32[3,16,32,128]{3,2,1,0:T(8,128)} %forc.5) | copy-start | bytes 2359300
  0.6 13.2 %copy-start = (f32[3,16,32,128]{3,2,1,0:T(8,128)S(1)}, f32[3,16,32,128]{3,2,1,0:T(8,128)}, u32[]{:S(2)}) copy-start(f32[3,16,32,128]{3,2,1,0:T(8,128)} %vel.5) | copy-start | bytes 2359300
  2.3 6.0 %collective-permute-start = (f32[19,32,128]{2,1,0:T(8,128)S(1)}, f32[19,32,128]{2,1,0:T(8,128)S(1)}, u32[]{:S(2)}, u32[]{:S(2)}) collective-permute-start(f32[19,32,128]{2,1,0:T(8,128)S(1)} %get-tuple-element.40), channel_id=1, source_target_pairs={{0,32},{32,0},{64,96},{96,64},{128,160},{160,128},{192,224},{224,1... | collective-permute-start | bytes 933896 | tf_op jit(solution)/shard_map/ppermute | solution.py:45
  5.6 6.6 %collective-permute-start.1 = (f32[19,32,128]{2,1,0:T(8,128)S(1)}, f32[19,32,128]{2,1,0:T(8,128)S(1)}, u32[]{:S(2)}, u32[]{:S(2)}) collective-permute-start(f32[19,32,128]{2,1,0:T(8,128)S(1)} %get-tuple-element.41), channel_id=1, source_target_pairs={{0,224},{32,64},{64,32},{96,128},{128,96},{160,192},{192,160},{224... | collective-permute-start | bytes 933896 | tf_op jit(solution)/shard_map/ppermute | solution.py:50
  5.6 9.4 %collective-permute-start.2 = (f32[37,8,128]{2,1,0:T(8,128)S(1)}, f32[37,8,128]{2,1,0:T(8,128)S(1)}, u32[]{:S(2)}, u32[]{:S(2)}) collective-permute-start(f32[37,8,128]{2,1,0:T(8,128)S(1)} %get-tuple-element.42), channel_id=1, source_target_pairs={{0,8},{8,0},{16,24},{24,16},{1,9},{9,1},{17,25},{25,17},{2,10},{10... | collective-permute-start | bytes 454664 | tf_op jit(solution)/shard_map/ppermute | solution.py:45
  6.4 8.7 %collective-permute-start.3 = (f32[37,8,128]{2,1,0:T(8,128)S(1)}, f32[37,8,128]{2,1,0:T(8,128)S(1)}, u32[]{:S(2)}, u32[]{:S(2)}) collective-permute-start(f32[37,8,128]{2,1,0:T(8,128)S(1)} %get-tuple-element.43), channel_id=1, source_target_pairs={{0,24},{8,16},{16,8},{24,0},{1,25},{9,17},{17,9},{25,1},{2,26},{10... | collective-permute-start | bytes 454664 | tf_op jit(solution)/shard_map/ppermute | solution.py:50
  12.2 3.2 %collective-permute-start.4 = (f32[16,8,128]{2,1,0:T(8,128)S(1)}, f32[16,8,128]{2,1,0:T(8,128)S(1)}, u32[]{:S(2)}, u32[]{:S(2)}) collective-permute-start(f32[16,8,128]{2,1,0:T(8,128)S(1)} %get-tuple-element.44), channel_id=1, source_target_pairs={{0,8},{8,0},{16,24},{24,16},{1,9},{9,1},{17,25},{25,17},{2,10},{10... | collective-permute-start | bytes 196616 | tf_op jit(solution)/shard_map/ppermute | solution.py:45
  12.3 4.4 %collective-permute-start.5 = (f32[16,8,128]{2,1,0:T(8,128)S(1)}, f32[16,8,128]{2,1,0:T(8,128)S(1)}, u32[]{:S(2)}, u32[]{:S(2)}) collective-permute-start(f32[16,8,128]{2,1,0:T(8,128)S(1)} %get-tuple-element.45), channel_id=1, source_target_pairs={{0,24},{8,16},{16,8},{24,0},{1,25},{9,17},{17,9},{25,1},{2,26},{10... | collective-permute-start | bytes 196616 | tf_op jit(solution)/shard_map/ppermute | solution.py:50
  17.5 5.9 %copy-start.4 = (f32[8]{0:T(128)S(1)}, f32[8]{0:T(128)}, u32[]{:S(2)}) copy-start(f32[8]{0:T(128)} %pre.3) | copy-start | bytes 100
  17.5 5.9 %copy-start.5 = (f32[8]{0:T(128)S(1)}, f32[8]{0:T(128)}, u32[]{:S(2)}) copy-start(f32[8]{0:T(128)} %yld.3) | copy-start | bytes 100
  17.5 10.0 %collective-permute-start.6 = (f32[25,8,128]{2,1,0:T(8,128)S(1)}, f32[25,8,128]{2,1,0:T(8,128)S(1)}, u32[]{:S(2)}, u32[]{:S(2)}) collective-permute-start(f32[25,8,128]{2,1,0:T(8,128)S(1)} %get-tuple-element.51), channel_id=1, source_target_pairs={{0,1},{1,0},{2,3},{3,2},{4,5},{5,4},{6,7},{7,6},{8,9},{9,8},{10,11... | collective-permute-start | bytes 307208 | tf_op jit(solution)/shard_map/ppermute | solution.py:45
  18.7 8.8 %collective-permute-start.7 = (f32[25,8,128]{2,1,0:T(8,128)S(1)}, f32[25,8,128]{2,1,0:T(8,128)S(1)}, u32[]{:S(2)}, u32[]{:S(2)}) collective-permute-start(f32[25,8,128]{2,1,0:T(8,128)S(1)} %get-tuple-element.52), channel_id=1, source_target_pairs={{0,7},{1,2},{2,1},{3,4},{4,3},{5,6},{6,5},{7,0},{8,15},{9,10},{10,... | collective-permute-start | bytes 307208 | tf_op jit(solution)/shard_map/ppermute | solution.py:50
  27.5 2.6 %copy-start.2 = (f32[22,40,128]{2,1,0:T(8,128)S(1)}, f32[22,40,128]{2,1,0:T(8,128)}, u32[]{:S(2)}) copy-start(f32[22,40,128]{2,1,0:T(8,128)} %get-tuple-element.46.v_own) | copy-start | bytes 1351684
  30.1 13.4 %copy-start.3 = (f32[3,16,32,128]{3,2,1,0:T(8,128)S(1)}, f32[3,16,32,128]{3,2,1,0:T(8,128)}, u32[]{:S(2)}) copy-start(f32[3,16,32,128]{3,2,1,0:T(8,128)} %get-tuple-element.47.u_own) | copy-start | bytes 2359300
  32.6 26.7 %all-to-all-start = ((f32[256,1,256]{2,1,0:T(1,128)}), f32[256,1,256]{2,1,0:T(1,128)S(1)}, u32[]{:S(2)}, u32[]{:S(2)}) async-start(f32[256,1,256]{2,1,0:T(1,128)} %get-tuple-element.67), calls=%async_computation | async-start | bytes 524288 | tf_op jit(solution)/shard_map/all_to_all | solution.py:719
